TPU v7x, 256 devices: a 4x2x16 block of a 4x16x16 slice. The times are simulated.
256 devices in a mesh: groups: 2 (over y), ctx: 32 (over z, core), head: 4 (over x).
Axes of the slice: x: 4, y: 2, z: 16, core: 2. Of those that a mesh axis runs over, the one named last changes fastest.
The devices are a block of a 4x16x16 slice.
Arguments:
- query: bfloat16 [8, 64, 32, 128], P('groups', 'head'), parts along dimension 0
- key_cache: bfloat16 [8, 65536, 8, 128], P('groups', 'ctx', 'head'), parts along dimension 0
- value_cache: bfloat16 [8, 65536, 8, 128], P('groups', 'ctx', 'head'), parts along dimension 0, may hold values from -6 to 6
- new_key: bfloat16 [8, 8, 32, 128], P('groups', 'head'), parts along dimension 0, may hold values from -9 to 9
- new_value: bfloat16 [8, 8, 32, 128], P('groups', 'head'), parts along dimension 0, may hold values from -6 to 6
- lengths: int32 [8], P('groups'), parts along dimension 0, may hold values from 256 to 65536, as said below
- out_weight: bfloat16 [8192, 8192], P('head', 'ctx'), may hold values from -0.0625 to 0.0625
Outputs:
- projected: float32 [8, 32, 8192], P('groups', None, 'ctx'), parts along dimension 0
There are 2 independent parts, one for each index of `groups`. A program takes and returns all parts, laid end to end along the dimension named above; an argument that names none is the same for every part. Nothing has to cross between parts.
Inputs may be any that keep to these rules, and one draw needn't show every extreme that they name: `lengths`: multiples of 256; in every draw exactly one sequence has length 65536, the others less.
All inputs are finite; a program needn't handle non-finite values.
Results may differ from a plain program's by a relative error of at most 0.003.
Values sent between devices are 32-bit elements; how exact they have to be, the bound alone decides.
No kernel may reach another device: no remote copies, remote signals or barrier semaphores. Data moves between devices by JAX's collectives and lax.ppermute only.
A program may use at most 128 MiB of HBM per device.

v0:
```python
import functools
import math

import jax
import jax.numpy as jnp
from jax import lax
from jax.experimental import pallas as pl
from jax.experimental.pallas import tpu as pltpu
from jax.sharding import PartitionSpec as P


very_low = -1e30
page = 256
radix = 4
stat_rows = 8

VMEM = pltpu.VMEM
f32 = jnp.float32
bf16 = jnp.bfloat16


def stats(top, total):
    row = lax.broadcasted_iota(jnp.int32, (stat_rows, top.shape[-1]), 0)
    return jnp.where(row == 0, top, jnp.where(row == 1, total, 0.0))


def contract(a, b, da, db, precision=None):
    return lax.dot_general(
        a, b, (((da,), (db,)), ((), ())), preferred_element_type=f32, precision=precision
    )


def attend_kernel(scaling, order, lens, info, q_ref, k_ref, v_ref, mine_ref, theirs_ref, s_ref, acc_ref):
    seq = jnp.bitwise_xor(info[1], order(pl.program_id(0)))
    core = info[3]
    rows, head_dim = k_ref.shape
    queries = q_ref.shape[1]
    per_page = 2 * page
    usable = jnp.clip(lens[seq] - info[0], 0, rows // 2)
    pages = usable // page
    factor = scaling * math.log2(math.e)
    d2 = 2 * head_dim

    even_row = lax.broadcasted_iota(jnp.int32, (16, head_dim), 0) % 2 == 0
    pick_even = jnp.where(even_row, 1.0, 0.0).astype(bf16)
    pick_odd = jnp.where(even_row, 0.0, 1.0).astype(bf16)
    qc = jnp.concatenate([q_ref[0], q_ref[1]], axis=1)

    def scores(p, tile):
        k = k_ref[pl.ds(p * per_page, tile), :].reshape(tile // 16, 16, head_dim)
        wide = jnp.concatenate(
            [
                (k * pick_even[None]).reshape(tile, head_dim),
                (k * pick_odd[None]).reshape(tile, head_dim),
            ],
            axis=1,
        )
        s = contract(wide, qc, 1, 1)
        s_ref[pl.ds(p * per_page, tile), :] = s
        return jnp.max(s.reshape(tile // 8, 8, queries), axis=0)

    def tops(most):
        even = lax.broadcasted_iota(jnp.int32, (8, queries), 0) % 2 == 0
        low = jnp.full_like(most, -jnp.inf)
        top0 = jnp.max(jnp.where(even, most, low), axis=0, keepdims=True)
        top1 = jnp.max(jnp.where(even, low, most), axis=0, keepdims=True)
        return top0, top1, jnp.where(even, top0, top1)

    def weighted(p, tile, both):
        s = s_ref[pl.ds(p * per_page, tile), :].reshape(tile // 8, 8, queries)
        w = jnp.exp2((s - both[None]) * factor).reshape(tile, queries).astype(bf16)
        v = v_ref[pl.ds(p * per_page, tile), :].T
        even = lax.broadcasted_iota(jnp.int32, (16, tile), 1) % 2 == 0
        even_lane = jnp.where(even, 1.0, 0.0).astype(bf16)
        odd_lane = jnp.where(even, 0.0, 1.0).astype(bf16)
        first = lax.broadcasted_iota(jnp.int32, (16, tile), 0)
        ones = jnp.where(
            first == 0, even_lane.astype(f32), jnp.where(first == 1, odd_lane.astype(f32), 0.0)
        ).astype(bf16)
        v3 = v.reshape(head_dim // 16, 16, tile)
        wide = jnp.concatenate(
            [
                (v3 * even_lane[None]).reshape(head_dim, tile),
                (v3 * odd_lane[None]).reshape(head_dim, tile),
                ones,
            ],
            axis=0,
        )
        return contract(wide, w, 1, 0)

    def put(acc, top0, top1):
        a0, a1 = acc[:head_dim], acc[head_dim:d2]
        s0 = stats(top0 * scaling, acc[d2 : d2 + 1])
        s1 = stats(top1 * scaling, acc[d2 + 1 : d2 + 2])
        first = core == 0
        mine_ref[:head_dim, :] = jnp.where(first, a0, a1)
        theirs_ref[:head_dim, :] = jnp.where(first, a1, a0)
        mine_ref[head_dim:, :] = jnp.where(first, s0, s1)
        theirs_ref[head_dim:, :] = jnp.where(first, s1, s0)

    whole = rows // per_page

    @pl.when(pages == whole)
    def _():
        most = scores(0, per_page)
        for p in range(1, whole):
            most = jnp.maximum(most, scores(p, per_page))
        top0, top1, both = tops(most)
        acc = weighted(0, per_page, both)
        for p in range(1, whole):
            acc = acc + weighted(p, per_page, both)
        put(acc, top0, top1)

    @pl.when(jnp.logical_and(pages < whole, pages > 0))
    def _():
        most = lax.fori_loop(
            0,
            pages,
            lambda p, m: jnp.maximum(m, scores(p, per_page)),
            jnp.full((8, queries), -jnp.inf, f32),
        )
        top0, top1, both = tops(most)
        acc_ref[...] = jnp.zeros_like(acc_ref)

        def add(p, _):
            acc_ref[...] += weighted(p, per_page, both)
            return _

        lax.fori_loop(0, pages, add, 0)
        put(acc_ref[...], top0, top1)

    @pl.when(pages == 0)
    def _():
        nothing = stats(jnp.full((1, queries), very_low, f32), jnp.zeros((1, queries), f32))
        for ref in (mine_ref, theirs_ref):
            ref[:head_dim, :] = jnp.zeros((head_dim, queries), f32)
            ref[head_dim:, :] = nothing


def attend(query, key_cache, value_cache, lengths, info, scaling, order, steps):
    _, heads, queries, head_dim = query.shape
    rows = key_cache.shape[1]
    block = (None, head_dim + stat_rows, queries)
    out = jax.ShapeDtypeStruct((steps, *block[1:]), f32)
    of_seq = lambda k, lens, info: (jnp.bitwise_xor(info[1], order(k)), 0, 0)
    spec = pltpu.PrefetchScalarGridSpec(
        num_scalar_prefetch=2,
        grid=(steps,),
        in_specs=[
            pl.BlockSpec(
                (None, heads, queries, head_dim),
                lambda k, lens, info: (jnp.bitwise_xor(info[1], order(k)), 0, 0, 0),
            ),
            pl.BlockSpec((None, rows, head_dim), of_seq),
            pl.BlockSpec((None, rows, head_dim), of_seq),
        ],
        out_specs=[pl.BlockSpec(block, lambda k, lens, info: (k, 0, 0))] * 2,
        scratch_shapes=[VMEM((rows, queries), f32), VMEM((2 * head_dim + 16, queries), f32)],
    )
    cost = pl.CostEstimate(
        flops=8 * steps * rows * queries * head_dim,
        transcendentals=steps * rows * queries,
        bytes_accessed=4 * steps * rows * head_dim,
    )
    in_hbm = [pltpu.with_memory_space_constraint(x, pltpu.HBM) for x in (query, key_cache, value_cache)]
    return pl.pallas_call(
        functools.partial(attend_kernel, scaling, order),
        grid_spec=spec,
        out_shape=[out, out],
        name="attend",
        compiler_params=limit(24),
        cost_estimate=cost,
    )(lengths, info, *in_hbm)


def merged(parts, depth):
    tops = [p[depth : depth + 1] for p in parts]
    top = functools.reduce(jnp.maximum, tops)
    shares = [jnp.exp(t - top) for t in tops]
    numer = sum(p[:depth] * e for p, e in zip(parts, shares))
    total = sum(p[depth + 1 : depth + 2] * e for p, e in zip(parts, shares))
    return numer, top, total


def merge_core_kernel(mine_ref, got_ref, *outs):
    depth = mine_ref.shape[1] - stat_rows
    for k, out in enumerate(outs):
        numer, top, total = merged([mine_ref[k], got_ref[k]], depth)
        out[:depth, :] = numer
        out[depth:, :] = stats(top, total)


def merge_near_kernel(info, *refs):
    parts, outs, pieces = refs[:radix], refs[radix:-1], refs[-1]
    depth = parts[0].shape[0] - stat_rows
    numer, top, total = merged([p[...] for p in parts], depth)
    half, lanes = depth // 2, numer.shape[1] // 2
    for a in range(2):
        at = slice(a * lanes, (a + 1) * lanes)
        s = stats(top[:, at], total[:, at])
        for d in range(2):
            pieces[2 * a + d, :half, :] = numer[d * half : (d + 1) * half, at]
            pieces[2 * a + d, half:, :] = s
    for k, out in enumerate(outs):
        out[...] = pieces[jnp.bitwise_xor(info[2], k)]


def finish_kernel(scaling, draft, info, *refs):
    parts, (q_ref, key_ref, value_ref), out = refs[:radix], refs[radix:-1], refs[-1]
    depth = parts[0].shape[0] - stat_rows
    numer, top, total = merged([p[...] for p in parts], depth)
    own = contract(key_ref[...], q_ref[...], 1, 1) * scaling
    at = lax.broadcasted_iota(jnp.int32, own.shape, 0)
    row = lax.broadcasted_iota(jnp.int32, own.shape, 1) % draft
    causal = at <= row
    own = jnp.where(causal, own, very_low)
    overall = jnp.maximum(top, jnp.max(own, axis=0, keepdims=True))
    carried = jnp.exp(top - overall)
    fresh = jnp.where(causal, jnp.exp(own - overall), 0.0)
    denominator = total * carried + jnp.sum(fresh, axis=0, keepdims=True)
    added = contract(value_ref[...].astype(f32), fresh, 0, 0, lax.Precision.HIGHEST)
    added = jnp.where(info[2] % 2 == 0, added[:depth], added[depth:])
    out[...] = ((numer * carried + added) / denominator).astype(bf16).astype(f32)


def collect_kernel(info, *refs):
    parts, out = refs[:-1], refs[-1]
    for k, part in enumerate(parts):
        out[jnp.bitwise_xor(info[2], k)] = part[...]


def project_kernel(draft, info, *refs):
    pieces, (w_ref, out_ref, x_ref) = refs[:-3], refs[-3:]
    width = x_ref.shape[2]
    for i, piece in enumerate(pieces):
        k, other = i // 2, i % 2
        g = jnp.bitwise_xor(info[3], other)
        for a in range(2):
            att = jnp.concatenate([piece[2 * a + d] for d in range(2)], axis=0)
            lanes, rows = att.shape
            att = att.T.astype(bf16)
            for h in range(rows // draft):
                col = (a * (rows // draft) + h) * lanes
                x_ref[g, k * draft : (k + 1) * draft, col : col + lanes] = att[h * draft : (h + 1) * draft]
    out_ref[...] = sum(contract(x_ref[g], w_ref[g * width : (g + 1) * width, :], 1, 0) for g in range(2))


def total_kernel(draft, n, info, *refs):
    parts, out = refs[:-1], refs[-1]
    for half in range(len(parts) // n):
        whole = sum(p[...] for p in parts[half * n : (half + 1) * n])
        count = whole.shape[0] // draft
        for i in range(count):
            seq = jnp.bitwise_xor(info[1], half * count + i)
            out[seq] = whole[i * draft : (i + 1) * draft]


def whole_vmem(n):
    return [pl.BlockSpec(memory_space=VMEM)] * n


def limit(mib):
    return pltpu.CompilerParams(vmem_limit_bytes=mib * 2**20)


smem = pl.BlockSpec(memory_space=pltpu.SMEM)


def step(query, key_cache, value_cache, new_key, new_value, lengths, out_weight):
    seqs, q_count, draft, head_dim = query.shape
    ctx_len, heads = key_cache.shape[1], key_cache.shape[2]
    queries = q_count // heads * draft
    scaling = 1.0 / math.sqrt(head_dim)
    n_ctx = lax.axis_size("ctx")
    chips = n_ctx // 2
    far = chips // radix

    def place(z, c):
        return (z - c * (radix // 2)) % chips // radix, z % radix

    def chip(b, j, c):
        shift = c * (radix // 2)
        return (b * radix + shift + (j - shift) % radix) % chips

    def pairs(move):
        out = []
        for i in range(n_ctx):
            z, c = i // 2, i % 2
            b, j = place(z, c)
            b2, j2 = move(b, j)
            out.append((i, 2 * chip(b2, j2, c) + c))
        return out

    near_pairs = [pairs(lambda b, j: (b, j ^ k)) for k in range(radix)]
    far_pairs = [pairs(lambda b, j: (b ^ k, j)) for k in range(far)]
    core_pairs = [(i, i ^ 1) for i in range(n_ctx)]

    swap = lambda x: lax.ppermute(x, "ctx", core_pairs)
    to_near = lambda x, k: lax.ppermute(x, "ctx", near_pairs[k])
    to_far = lambda x, k: lax.ppermute(x, "ctx", far_pairs[k])

    index = lax.axis_index("ctx")
    core = index % 2
    block, spot = place(index // 2, core)
    info = jnp.stack([index * ctx_len, spot, block, core]).astype(jnp.int32)

    grouped = query.reshape(seqs, heads, queries, head_dim)
    keys = key_cache.reshape(seqs, ctx_len * heads, head_dim)
    values = value_cache.reshape(seqs, ctx_len * heads, head_dim)
    chunk = jax.ShapeDtypeStruct((head_dim + stat_rows, queries), f32)
    half_seqs = seqs // 2
    gate = info
    chunks = {}
    for half in range(2):
        order = lambda k, half=half: seqs - 1 - half * half_seqs - k
        mine, theirs = attend(grouped, keys, values, lengths, gate, scaling, order, half_seqs)
        got = swap(theirs)
        found = pl.pallas_call(
            merge_core_kernel,
            in_specs=whole_vmem(2),
            out_specs=whole_vmem(half_seqs),
            out_shape=[chunk] * half_seqs,
            name="merge_core",
            compiler_params=limit(8),
        )(mine, got)
        gate, *found = lax.optimization_barrier((info, *found))
        for k, x in enumerate(found):
            chunks[order(k)] = to_near(x, order(k)) if order(k) else x
    chunks = [chunks[k] for k in range(radix)]
    piece_shape = (head_dim // 2 + stat_rows, queries // 2)
    piece = jax.ShapeDtypeStruct(piece_shape, f32)
    pieces = pl.pallas_call(
        merge_near_kernel,
        in_specs=[smem] + whole_vmem(radix),
        out_specs=whole_vmem(far),
        out_shape=[piece] * far,
        scratch_shapes=[VMEM((4, *piece_shape), f32)],
        name="merge_near",
        compiler_params=limit(4),
    )(info, *chunks)
    order = (2, 1, 3)
    moved = {k: to_far(pieces[k], k) for k in order}
    pieces = [pieces[0]] + [moved[k] for k in range(1, far)]
    att_shape = (head_dim // 2, queries // 2)
    picked = pltpu.PrefetchScalarGridSpec(
        num_scalar_prefetch=1,
        grid=(1,),
        in_specs=[pl.BlockSpec(piece_shape, lambda i, info: (0, 0))] * far
        + [
            pl.BlockSpec(
                (None, None, queries // 2, head_dim),
                lambda i, info: (info[1], info[3], info[2] // 2, 0),
            )
        ]
        + [
            pl.BlockSpec(
                (None, None, draft, head_dim), lambda i, info: (info[1], info[3], 0, 0)
            )
        ]
        * 2,
        out_specs=pl.BlockSpec(att_shape, lambda i, info: (0, 0)),
    )
    att = pl.pallas_call(
        functools.partial(finish_kernel, scaling, draft),
        grid_spec=picked,
        out_shape=jax.ShapeDtypeStruct(att_shape, f32),
        name="finish",
        compiler_params=limit(4),
    )(info, *pieces, grouped, new_key, new_value)
    moved = {k: to_far(att, k) for k in order}
    block_att = pl.pallas_call(
        collect_kernel,
        in_specs=[smem] + whole_vmem(far),
        out_specs=pl.BlockSpec(memory_space=VMEM),
        out_shape=jax.ShapeDtypeStruct((far, *att_shape), f32),
        name="collect",
        compiler_params=limit(4),
    )(info, att, *[moved[k] for k in range(1, far)])
    near = [block_att] + [to_near(block_att, k) for k in range(1, radix)]
    width = out_weight.shape[1]
    n_head = lax.axis_size("head")
    parts = []
    for half in range(2):
        pieces = []
        for k in range(half * half_seqs, (half + 1) * half_seqs):
            pieces += [near[k], swap(near[k])]
        partial_out = pl.pallas_call(
            functools.partial(project_kernel, draft),
            in_specs=[smem] + whole_vmem(len(pieces) + 1),
            out_specs=pl.BlockSpec(memory_space=VMEM),
            out_shape=jax.ShapeDtypeStruct((half_seqs * draft, width), f32),
            scratch_shapes=[VMEM((heads, half_seqs * draft, out_weight.shape[0] // heads), bf16)],
            name="project",
            compiler_params=limit(8),
        )(info, *pieces, out_weight)
        parts.append(partial_out)
        for k in range(1, n_head):
            moves = [(i, (i + k) % n_head) for i in range(n_head)]
            parts.append(lax.ppermute(partial_out, "head", moves))
    return pl.pallas_call(
        functools.partial(total_kernel, draft, n_head),
        in_specs=[smem] + whole_vmem(len(parts)),
        out_specs=pl.BlockSpec(memory_space=VMEM),
        out_shape=jax.ShapeDtypeStruct((seqs, draft, width), f32),
        name="total",
        compiler_params=limit(4),
    )(info, *parts)


def solution(mesh):
    placed = (
        P("groups", "head", None, None),
        P("groups", "ctx", "head", None),
        P("groups", "ctx", "head", None),
        P("groups", "head", None, None),
        P("groups", "head", None, None),
        P("groups"),
        P("head", "ctx"),
    )
    return jax.shard_map(
        step, mesh=mesh, in_specs=placed, out_specs=P("groups", None, "ctx"), check_vma=False
    )
```

profile of v0, /device:TPU:33, one launch (start us, length us, event | category | flops | bytes accessed | tf_op | source)
XLA Modules:
  0.0 108.7 jit_solution(15263273107442920335)
XLA Ops:
  0.0 0.1 pad_add_fusion.info
  0.1 0.7 copy-done.4
  0.7 7.4 %attend.2 = (f32[2,136,256]{2,1,0:T(8,128)S(1)}, f32[2,136,256]{2,1,0:T(8,128)S(1)}) custom-call(s32[4]{0:T(128)S(1)} %copy-done.4, s32[4]{0:T(128)S(1)} %pad_add_fusion.info, bf16[4,2,256,128]{3,2,1,0:T(8,128)(2,1)} %bitcast.7, bf16[4,4096,128]{2,1,0:T(8,128)(2,1)} %bitcast.10, bf16[4,4096,128]{2,1,0:T(8,128)(2,1)} %bitcast.12), custom_call_target="tpu_custom_call" | custom-call | flops 2147483648 | bytes 4194304 | tf_op jit(solution)/shard_map/attend/pallas_call | solution.py:166
  8.1 20.5 %collective-permute-start = (f32[2,136,256]{2,1,0:T(8,128)S(1)}, f32[2,136,256]{2,1,0:T(8,128)S(1)}, u32[]{:S(2)}, u32[]{:S(2)}) collective-permute-start(f32[2,136,256]{2,1,0:T(8,128)S(1)} %get-tuple-element.23), channel_id=1, source_target_pairs={{0,4},{4,0},{8,12},{12,8},{16,20},{20,16},{24,28},{28,24},{32,36},... | collective-permute-start | bytes 835592 | tf_op jit(solution)/shard_map/ppermute | solution.py:298
  28.7 1.2 %collective-permute-done.got_ref = f32[2,136,256]{2,1,0:T(8,128)S(1)} collective-permute-done((f32[2,136,256]{2,1,0:T(8,128)S(1)}, f32[2,136,256]{2,1,0:T(8,128)S(1)}, u32[]{:S(2)}, u32[]{:S(2)}) %collective-permute-start) | collective-permute-done | bytes 278560 | tf_op jit(solution)/shard_map/ppermute | solution.py:298
  29.9 0.1 merge_core.2
  29.9 0.0 copy-start
  29.9 0.0 copy-start.2
  30.0 0.0 copy-start.3
  30.0 0.0 copy-start.1
  30.0 7.4 %attend.3 = (f32[2,136,256]{2,1,0:T(8,128)S(1)}, f32[2,136,256]{2,1,0:T(8,128)S(1)}) custom-call(s32[4]{0:T(128)S(1)} %copy-done.4, s32[4]{0:T(128)S(1)} %pad_add_fusion.info, bf16[4,2,256,128]{3,2,1,0:T(8,128)(2,1)} %bitcast.8, bf16[4,4096,128]{2,1,0:T(8,128)(2,1)} %bitcast.11, bf16[4,4096,128]{2,1,0:T(8,128)(2,1)} %bitcast.13), custom_call_target="tpu_custom_call" | custom-call | flops 2147483648 | bytes 4194304 | tf_op jit(solution)/shard_map/attend/pallas_call | solution.py:166
  37.4 0.5 collective-permute-start.1
  37.9 0.0 collective-permute-start.3
  37.9 0.0 collective-permute-start.4
  37.9 1.2 %collective-permute-done.1.got_ref = f32[2,136,256]{2,1,0:T(8,128)S(1)} collective-permute-done((f32[2,136,256]{2,1,0:T(8,128)S(1)}, f32[2,136,256]{2,1,0:T(8,128)S(1)}, u32[]{:S(2)}, u32[]{:S(2)}) %collective-permute-start.1) | collective-permute-done | bytes 278560 | tf_op jit(solution)/shard_map/ppermute | solution.py:298
  39.1 0.1 merge_core.3
  39.2 3.7 %collective-permute-start.2 = (f32[136,256]{1,0:T(8,128)S(1)}, f32[136,256]{1,0:T(8,128)S(1)}, u32[]{:S(2)}, u32[]{:S(2)}) collective-permute-start(f32[136,256]{1,0:T(8,128)S(1)} %get-tuple-element.32), channel_id=1, source_target_pairs={{0,8},{4,12},{8,0},{12,4},{16,24},{20,28},{24,16},{28,20},{32,40},... | collective-permute-start | bytes 417800 | tf_op jit(solution)/shard_map/ppermute | solution.py:299
  42.9 2.1 %collective-permute-done.3.refs_2_ = f32[136,256]{1,0:T(8,128)S(1)} collective-permute-done((f32[136,256]{1,0:T(8,128)S(1)}, f32[136,256]{1,0:T(8,128)S(1)}, u32[]{:S(2)}, u32[]{:S(2)}) %collective-permute-start.3) | collective-permute-done | bytes 139296 | tf_op jit(solution)/shard_map/ppermute | solution.py:299
  45.0 0.0 collective-permute-done.4.refs_3_
  45.0 4.3 %collective-permute-done.2.refs_1_ = f32[136,256]{1,0:T(8,128)S(1)} collective-permute-done((f32[136,256]{1,0:T(8,128)S(1)}, f32[136,256]{1,0:T(8,128)S(1)}, u32[]{:S(2)}, u32[]{:S(2)}) %collective-permute-start.2) | collective-permute-done | bytes 139296 | tf_op jit(solution)/shard_map/ppermute | solution.py:299
  49.3 0.6 merge_near.1
  49.9 0.1 collective-permute-start.5
  50.1 0.1 collective-permute-start.6
  50.2 10.3 %collective-permute-start.7 = (f32[72,128]{1,0:T(8,128)S(1)}, f32[72,128]{1,0:T(8,128)S(1)}, u32[]{:S(2)}, u32[]{:S(2)}) collective-permute-start(f32[72,128]{1,0:T(8,128)S(1)} %get-tuple-element.38), channel_id=1, source_target_pairs={{0,96},{4,36},{8,104},{12,44},{16,112},{20,116},{24,120},{28,124},... | collective-permute-start | bytes 110600 | tf_op jit(solution)/shard_map/ppermute | solution.py:300
  60.5 0.0 collective-permute-done.5.refs_1_
  60.5 1.5 %collective-permute-done.6.refs_2_ = f32[72,128]{1,0:T(8,128)S(1)} collective-permute-done((f32[72,128]{1,0:T(8,128)S(1)}, f32[72,128]{1,0:T(8,128)S(1)}, u32[]{:S(2)}, u32[]{:S(2)}) %collective-permute-start.6) | collective-permute-done | bytes 36896 | tf_op jit(solution)/shard_map/ppermute | solution.py:300
  62.0 1.0 collective-permute-done.7.refs_3_
  63.0 0.9 finish.1.refs_0_
  63.9 4.8 %collective-permute-start.10 = (f32[64,128]{1,0:T(8,128)S(1)}, f32[64,128]{1,0:T(8,128)S(1)}, u32[]{:S(2)}, u32[]{:S(2)}) collective-permute-start(f32[64,128]{1,0:T(8,128)S(1)} %finish.1.refs_0_), channel_id=1, source_target_pairs={{0,96},{4,36},{8,104},{12,44},{16,112},{20,116},{24,120},{28,124},... | collective-permute-start | bytes 98312 | tf_op jit(solution)/shard_map/ppermute | solution.py:300
  68.8 4.7 %collective-permute-start.9 = (f32[64,128]{1,0:T(8,128)S(1)}, f32[64,128]{1,0:T(8,128)S(1)}, u32[]{:S(2)}, u32[]{:S(2)}) collective-permute-start(f32[64,128]{1,0:T(8,128)S(1)} %finish.1.refs_0_), channel_id=1, source_target_pairs={{0,64},{4,68},{8,72},{12,76},{16,80},{20,84},{24,88},{28,92},{32,9... | collective-permute-start | bytes 98312 | tf_op jit(solution)/shard_map/ppermute | solution.py:300
  73.5 1.0 collective-permute-start.8
  74.5 0.0 collective-permute-done.10.refs_3_
  74.5 6.0 %collective-permute-done.9.refs_2_ = f32[64,128]{1,0:T(8,128)S(1)} collective-permute-done((f32[64,128]{1,0:T(8,128)S(1)}, f32[64,128]{1,0:T(8,128)S(1)}, u32[]{:S(2)}, u32[]{:S(2)}) %collective-permute-start.9) | collective-permute-done | bytes 32800 | tf_op jit(solution)/shard_map/ppermute | solution.py:300
  80.5 0.0 collective-permute-done.8.refs_1_
  80.5 0.6 collect.1.refs_0_
  81.1 0.5 collective-permute-start.19
  81.6 3.6 %collective-permute-start.17 = (f32[4,64,128]{2,1,0:T(8,128)S(1)}, f32[4,64,128]{2,1,0:T(8,128)S(1)}, u32[]{:S(2)}, u32[]{:S(2)}) collective-permute-start(f32[4,64,128]{2,1,0:T(8,128)S(1)} %collect.1.refs_0_), channel_id=1, source_target_pairs={{0,16},{4,116},{8,24},{12,124},{16,0},{20,36},{24,8},{28,44},{32,4... | collective-permute-start | bytes 393224 | tf_op jit(solution)/shard_map/ppermute | solution.py:299
  85.2 0.0 collective-permute-start.12
  85.2 1.1 collective-permute-done.19.refs_2_
  86.2 7.4 %collective-permute-start.20 = (f32[4,64,128]{2,1,0:T(8,128)S(1)}, f32[4,64,128]{2,1,0:T(8,128)S(1)}, u32[]{:S(2)}, u32[]{:S(2)}) collective-permute-start(f32[4,64,128]{2,1,0:T(8,128)S(1)} %collective-permute-done.19.refs_2_), channel_id=1, source_target_pairs={{0,4},{4,0},{8,12},{12,8},{16,20},{20,16},{24,28},{28,24},{32,36},... | collective-permute-start | bytes 393224 | tf_op jit(solution)/shard_map/ppermute | solution.py:298
  93.6 0.0 collective-permute-done.17.refs_0_
  93.7 0.0 collective-permute-start.18
  93.7 0.5 collective-permute-start.11
  94.2 0.0 collective-permute-done.12.refs_2_
  94.2 0.0 collective-permute-start.13
  94.2 0.4 collective-permute-done.20.refs_3_
  94.6 0.4 collective-permute-done.18.refs_1_
  95.0 1.0 project.3.refs_4_
  96.0 0.1 collective-permute-start.23
  96.1 0.1 collective-permute-start.22
  96.3 1.3 %collective-permute-start.21 = (f32[64,256]{1,0:T(8,128)S(1)}, f32[64,256]{1,0:T(8,128)S(1)}, u32[]{:S(2)}, u32[]{:S(2)}) collective-permute-start(f32[64,256]{1,0:T(8,128)S(1)} %project.3.refs_4_), channel_id=1, source_target_pairs={{0,1},{1,2},{2,3},{3,0},{4,5},{5,6},{6,7},{7,4},{8,9},{9,10},{10,1... | collective-permute-start | bytes 196616 | tf_op jit(solution)/shard_map/ppermute | solution.py:399
  97.6 0.0 collective-permute-done.11.refs_1_
  97.6 0.0 collective-permute-done.13.refs_3_
  97.6 1.0 project.2.refs_0_
  98.5 2.5 %collective-permute-start.16 = (f32[64,256]{1,0:T(8,128)S(1)}, f32[64,256]{1,0:T(8,128)S(1)}, u32[]{:S(2)}, u32[]{:S(2)}) collective-permute-start(f32[64,256]{1,0:T(8,128)S(1)} %project.2.refs_0_), channel_id=1, source_target_pairs={{0,3},{1,0},{2,1},{3,2},{4,7},{5,4},{6,5},{7,6},{8,11},{9,8},{10,9... | collective-permute-start | bytes 196616 | tf_op jit(solution)/shard_map/ppermute | solution.py:399
  101.1 1.3 %collective-permute-start.15 = (f32[64,256]{1,0:T(8,128)S(1)}, f32[64,256]{1,0:T(8,128)S(1)}, u32[]{:S(2)}, u32[]{:S(2)}) collective-permute-start(f32[64,256]{1,0:T(8,128)S(1)} %project.2.refs_0_), channel_id=1, source_target_pairs={{0,2},{1,3},{2,0},{3,1},{4,6},{5,7},{6,4},{7,5},{8,10},{9,11},{10,... | collective-permute-start | bytes 196616 | tf_op jit(solution)/shard_map/ppermute | solution.py:399
  102.4 0.0 collective-permute-done.23.refs_7_
  102.4 0.7 collective-permute-start.14
  103.1 0.0 collective-permute-done.22.refs_6_
  103.1 0.0 collective-permute-done.21.refs_5_
  103.1 0.0 collective-permute-done.16.refs_3_
  103.1 2.6 %collective-permute-done.15.refs_2_ = f32[64,256]{1,0:T(8,128)S(1)} collective-permute-done((f32[64,256]{1,0:T(8,128)S(1)}, f32[64,256]{1,0:T(8,128)S(1)}, u32[]{:S(2)}, u32[]{:S(2)}) %collective-permute-start.15) | collective-permute-done | bytes 65568 | tf_op jit(solution)/shard_map/ppermute | solution.py:399
  105.7 1.8 %collective-permute-done.14.refs_1_ = f32[64,256]{1,0:T(8,128)S(1)} collective-permute-done((f32[64,256]{1,0:T(8,128)S(1)}, f32[64,256]{1,0:T(8,128)S(1)}, u32[]{:S(2)}, u32[]{:S(2)}) %collective-permute-start.14) | collective-permute-done | bytes 65568 | tf_op jit(solution)/shard_map/ppermute | solution.py:399
  107.5 1.2 %total.1 = f32[4,32,256]{2,1,0:T(8,128)} custom-call(s32[4]{0:T(128)S(1)} %pad_add_fusion.info, f32[64,256]{1,0:T(8,128)S(1)} %project.2.refs_0_, f32[64,256]{1,0:T(8,128)S(1)} %collective-permute-done.14.refs_1_, f32[64,256]{1,0:T(8,128)S(1)} %collective-permute-done.15.refs_2_, f32[64,256]{1,0:T(8,128)S(1)} %collective-permute-done.16.refs_3_, ...), custom_call_target="tpu_custom_call" | custom-call | tf_op jit(solution)/shard_map/total/pallas_call | solution.py:400
  (5 shorter events, 0.0 us)
Async XLA Ops:
  0.1 0.7 copy-start.4
  8.1 21.7 %collective-permute-start = (f32[2,136,256]{2,1,0:T(8,128)S(1)}, f32[2,136,256]{2,1,0:T(8,128)S(1)}, u32[]{:S(2)}, u32[]{:S(2)}) collective-permute-start(f32[2,136,256]{2,1,0:T(8,128)S(1)} %get-tuple-element.23), channel_id=1, source_target_pairs={{0,4},{4,0},{8,12},{12,8},{16,20},{20,16},{24,28},{28,24},{32,36},... | collective-permute-start | bytes 835592 | tf_op jit(solution)/shard_map/ppermute | solution.py:298
  29.9 33.0 %copy-start = (bf16[4,16,32,128]{3,2,1,0:T(8,128)(2,1)S(1)}, bf16[4,16,32,128]{3,2,1,0:T(8,128)(2,1)}, u32[]{:S(2)}) copy-start(bf16[4,16,32,128]{3,2,1,0:T(8,128)(2,1)} %param.7) | copy-start | bytes 1572868
  29.9 33.0 %copy-start.2 = (bf16[4,2,32,128]{3,2,1,0:T(8,128)(2,1)S(1)}, bf16[4,2,32,128]{3,2,1,0:T(8,128)(2,1)}, u32[]{:S(2)}) copy-start(bf16[4,2,32,128]{3,2,1,0:T(8,128)(2,1)} %refs_5_.1) | copy-start | bytes 196612
  30.0 33.0 %copy-start.3 = (bf16[4,2,32,128]{3,2,1,0:T(8,128)(2,1)S(1)}, bf16[4,2,32,128]{3,2,1,0:T(8,128)(2,1)}, u32[]{:S(2)}) copy-start(bf16[4,2,32,128]{3,2,1,0:T(8,128)(2,1)} %refs_6_.1) | copy-start | bytes 196612
  30.0 65.0 %copy-start.1 = (bf16[2048,256]{1,0:T(8,128)(2,1)S(1)}, bf16[2048,256]{1,0:T(8,128)(2,1)}, u32[]{:S(2)}) copy-start(bf16[2048,256]{1,0:T(8,128)(2,1)} %refs_4_.3) | copy-start | bytes 3145732
  37.4 1.7 %collective-permute-start.1 = (f32[2,136,256]{2,1,0:T(8,128)S(1)}, f32[2,136,256]{2,1,0:T(8,128)S(1)}, u32[]{:S(2)}, u32[]{:S(2)}) collective-permute-start(f32[2,136,256]{2,1,0:T(8,128)S(1)} %get-tuple-element.28), channel_id=1, source_target_pairs={{0,4},{4,0},{8,12},{12,8},{16,20},{20,16},{24,28},{28,24},{32,36},... | collective-permute-start | bytes 835592 | tf_op jit(solution)/shard_map/ppermute | solution.py:298
  37.9 7.1 %collective-permute-start.3 = (f32[136,256]{1,0:T(8,128)S(1)}, f32[136,256]{1,0:T(8,128)S(1)}, u32[]{:S(2)}, u32[]{:S(2)}) collective-permute-start(f32[136,256]{1,0:T(8,128)S(1)} %get-tuple-element.33), channel_id=1, source_target_pairs={{0,16},{4,116},{8,24},{12,124},{16,0},{20,36},{24,8},{28,44},{32,4... | collective-permute-start | bytes 417800 | tf_op jit(solution)/shard_map/ppermute | solution.py:299
  37.9 7.1 %collective-permute-start.4 = (f32[136,256]{1,0:T(8,128)S(1)}, f32[136,256]{1,0:T(8,128)S(1)}, u32[]{:S(2)}, u32[]{:S(2)}) collective-permute-start(f32[136,256]{1,0:T(8,128)S(1)} %get-tuple-element.34), channel_id=1, source_target_pairs={{0,24},{4,124},{8,16},{12,116},{16,8},{20,44},{24,0},{28,36},{32,5... | collective-permute-start | bytes 417800 | tf_op jit(solution)/shard_map/ppermute | solution.py:299
  39.2 10.1 %collective-permute-start.2 = (f32[136,256]{1,0:T(8,128)S(1)}, f32[136,256]{1,0:T(8,128)S(1)}, u32[]{:S(2)}, u32[]{:S(2)}) collective-permute-start(f32[136,256]{1,0:T(8,128)S(1)} %get-tuple-element.32), channel_id=1, source_target_pairs={{0,8},{4,12},{8,0},{12,4},{16,24},{20,28},{24,16},{28,20},{32,40},... | collective-permute-start | bytes 417800 | tf_op jit(solution)/shard_map/ppermute | solution.py:299
  49.9 10.6 %collective-permute-start.5 = (f32[72,128]{1,0:T(8,128)S(1)}, f32[72,128]{1,0:T(8,128)S(1)}, u32[]{:S(2)}, u32[]{:S(2)}) collective-permute-start(f32[72,128]{1,0:T(8,128)S(1)} %get-tuple-element.36), channel_id=1, source_target_pairs={{0,32},{4,100},{8,40},{12,108},{16,48},{20,52},{24,56},{28,60},{32... | collective-permute-start | bytes 110600 | tf_op jit(solution)/shard_map/ppermute | solution.py:300
  50.1 11.9 %collective-permute-start.6 = (f32[72,128]{1,0:T(8,128)S(1)}, f32[72,128]{1,0:T(8,128)S(1)}, u32[]{:S(2)}, u32[]{:S(2)}) collective-permute-start(f32[72,128]{1,0:T(8,128)S(1)} %get-tuple-element.37), channel_id=1, source_target_pairs={{0,64},{4,68},{8,72},{12,76},{16,80},{20,84},{24,88},{28,92},{32,9... | collective-permute-start | bytes 110600 | tf_op jit(solution)/shard_map/ppermute | solution.py:300
  50.2 12.8 %collective-permute-start.7 = (f32[72,128]{1,0:T(8,128)S(1)}, f32[72,128]{1,0:T(8,128)S(1)}, u32[]{:S(2)}, u32[]{:S(2)}) collective-permute-start(f32[72,128]{1,0:T(8,128)S(1)} %get-tuple-element.38), channel_id=1, source_target_pairs={{0,96},{4,36},{8,104},{12,44},{16,112},{20,116},{24,120},{28,124},... | collective-permute-start | bytes 110600 | tf_op jit(solution)/shard_map/ppermute | solution.py:300
  63.9 10.6 %collective-permute-start.10 = (f32[64,128]{1,0:T(8,128)S(1)}, f32[64,128]{1,0:T(8,128)S(1)}, u32[]{:S(2)}, u32[]{:S(2)}) collective-permute-start(f32[64,128]{1,0:T(8,128)S(1)} %finish.1.refs_0_), channel_id=1, source_target_pairs={{0,96},{4,36},{8,104},{12,44},{16,112},{20,116},{24,120},{28,124},... | collective-permute-start | bytes 98312 | tf_op jit(solution)/shard_map/ppermute | solution.py:300
  68.8 11.8 %collective-permute-start.9 = (f32[64,128]{1,0:T(8,128)S(1)}, f32[64,128]{1,0:T(8,128)S(1)}, u32[]{:S(2)}, u32[]{:S(2)}) collective-permute-start(f32[64,128]{1,0:T(8,128)S(1)} %finish.1.refs_0_), channel_id=1, source_target_pairs={{0,64},{4,68},{8,72},{12,76},{16,80},{20,84},{24,88},{28,92},{32,9... | collective-permute-start | bytes 98312 | tf_op jit(solution)/shard_map/ppermute | solution.py:300
  73.5 7.0 %collective-permute-start.8 = (f32[64,128]{1,0:T(8,128)S(1)}, f32[64,128]{1,0:T(8,128)S(1)}, u32[]{:S(2)}, u32[]{:S(2)}) collective-permute-start(f32[64,128]{1,0:T(8,128)S(1)} %finish.1.refs_0_), channel_id=1, source_target_pairs={{0,32},{4,100},{8,40},{12,108},{16,48},{20,52},{24,56},{28,60},{32... | collective-permute-start | bytes 98312 | tf_op jit(solution)/shard_map/ppermute | solution.py:300
  81.1 5.2 %collective-permute-start.19 = (f32[4,64,128]{2,1,0:T(8,128)S(1)}, f32[4,64,128]{2,1,0:T(8,128)S(1)}, u32[]{:S(2)}, u32[]{:S(2)}) collective-permute-start(f32[4,64,128]{2,1,0:T(8,128)S(1)} %collect.1.refs_0_), channel_id=1, source_target_pairs={{0,24},{4,124},{8,16},{12,116},{16,8},{20,44},{24,0},{28,36},{32,5... | collective-permute-start | bytes 393224 | tf_op jit(solution)/shard_map/ppermute | solution.py:299
  81.6 12.1 %collective-permute-start.17 = (f32[4,64,128]{2,1,0:T(8,128)S(1)}, f32[4,64,128]{2,1,0:T(8,128)S(1)}, u32[]{:S(2)}, u32[]{:S(2)}) collective-permute-start(f32[4,64,128]{2,1,0:T(8,128)S(1)} %collect.1.refs_0_), channel_id=1, source_target_pairs={{0,16},{4,116},{8,24},{12,124},{16,0},{20,36},{24,8},{28,44},{32,4... | collective-permute-start | bytes 393224 | tf_op jit(solution)/shard_map/ppermute | solution.py:299
  85.2 9.0 %collective-permute-start.12 = (f32[4,64,128]{2,1,0:T(8,128)S(1)}, f32[4,64,128]{2,1,0:T(8,128)S(1)}, u32[]{:S(2)}, u32[]{:S(2)}) collective-permute-start(f32[4,64,128]{2,1,0:T(8,128)S(1)} %collect.1.refs_0_), channel_id=1, source_target_pairs={{0,8},{4,12},{8,0},{12,4},{16,24},{20,28},{24,16},{28,20},{32,40},... | collective-permute-start | bytes 393224 | tf_op jit(solution)/shard_map/ppermute | solution.py:299
  86.2 8.4 %collective-permute-start.20 = (f32[4,64,128]{2,1,0:T(8,128)S(1)}, f32[4,64,128]{2,1,0:T(8,128)S(1)}, u32[]{:S(2)}, u32[]{:S(2)}) collective-permute-start(f32[4,64,128]{2,1,0:T(8,128)S(1)} %collective-permute-done.19.refs_2_), channel_id=1, source_target_pairs={{0,4},{4,0},{8,12},{12,8},{16,20},{20,16},{24,28},{28,24},{32,36},... | collective-permute-start | bytes 393224 | tf_op jit(solution)/shard_map/ppermute | solution.py:298
  93.7 1.3 %collective-permute-start.18 = (f32[4,64,128]{2,1,0:T(8,128)S(1)}, f32[4,64,128]{2,1,0:T(8,128)S(1)}, u32[]{:S(2)}, u32[]{:S(2)}) collective-permute-start(f32[4,64,128]{2,1,0:T(8,128)S(1)} %collective-permute-done.17.refs_0_), channel_id=1, source_target_pairs={{0,4},{4,0},{8,12},{12,8},{16,20},{20,16},{24,28},{28,24},{32,36},... | collective-permute-start | bytes 393224 | tf_op jit(solution)/shard_map/ppermute | solution.py:298
  93.7 3.9 %collective-permute-start.11 = (f32[4,64,128]{2,1,0:T(8,128)S(1)}, f32[4,64,128]{2,1,0:T(8,128)S(1)}, u32[]{:S(2)}, u32[]{:S(2)}) collective-permute-start(f32[4,64,128]{2,1,0:T(8,128)S(1)} %collect.1.refs_0_), channel_id=1, source_target_pairs={{0,4},{4,0},{8,12},{12,8},{16,20},{20,16},{24,28},{28,24},{32,36},... | collective-permute-start | bytes 393224 | tf_op jit(solution)/shard_map/ppermute | solution.py:298
  94.2 3.4 %collective-permute-start.13 = (f32[4,64,128]{2,1,0:T(8,128)S(1)}, f32[4,64,128]{2,1,0:T(8,128)S(1)}, u32[]{:S(2)}, u32[]{:S(2)}) collective-permute-start(f32[4,64,128]{2,1,0:T(8,128)S(1)} %collective-permute-done.12.refs_2_), channel_id=1, source_target_pairs={{0,4},{4,0},{8,12},{12,8},{16,20},{20,16},{24,28},{28,24},{32,36},... | collective-permute-start | bytes 393224 | tf_op jit(solution)/shard_map/ppermute | solution.py:298
  96.0 6.4 %collective-permute-start.23 = (f32[64,256]{1,0:T(8,128)S(1)}, f32[64,256]{1,0:T(8,128)S(1)}, u32[]{:S(2)}, u32[]{:S(2)}) collective-permute-start(f32[64,256]{1,0:T(8,128)S(1)} %project.3.refs_4_), channel_id=1, source_target_pairs={{0,3},{1,0},{2,1},{3,2},{4,7},{5,4},{6,5},{7,6},{8,11},{9,8},{10,9... | collective-permute-start | bytes 196616 | tf_op jit(solution)/shard_map/ppermute | solution.py:399
  96.1 7.0 %collective-permute-start.22 = (f32[64,256]{1,0:T(8,128)S(1)}, f32[64,256]{1,0:T(8,128)S(1)}, u32[]{:S(2)}, u32[]{:S(2)}) collective-permute-start(f32[64,256]{1,0:T(8,128)S(1)} %project.3.refs_4_), channel_id=1, source_target_pairs={{0,2},{1,3},{2,0},{3,1},{4,6},{5,7},{6,4},{7,5},{8,10},{9,11},{10,... | collective-permute-start | bytes 196616 | tf_op jit(solution)/shard_map/ppermute | solution.py:399
  96.3 6.8 %collective-permute-start.21 = (f32[64,256]{1,0:T(8,128)S(1)}, f32[64,256]{1,0:T(8,128)S(1)}, u32[]{:S(2)}, u32[]{:S(2)}) collective-permute-start(f32[64,256]{1,0:T(8,128)S(1)} %project.3.refs_4_), channel_id=1, source_target_pairs={{0,1},{1,2},{2,3},{3,0},{4,5},{5,6},{6,7},{7,4},{8,9},{9,10},{10,1... | collective-permute-start | bytes 196616 | tf_op jit(solution)/shard_map/ppermute | solution.py:399
  98.5 4.6 %collective-permute-start.16 = (f32[64,256]{1,0:T(8,128)S(1)}, f32[64,256]{1,0:T(8,128)S(1)}, u32[]{:S(2)}, u32[]{:S(2)}) collective-permute-start(f32[64,256]{1,0:T(8,128)S(1)} %project.2.refs_0_), channel_id=1, source_target_pairs={{0,3},{1,0},{2,1},{3,2},{4,7},{5,4},{6,5},{7,6},{8,11},{9,8},{10,9... | collective-permute-start | bytes 196616 | tf_op jit(solution)/shard_map/ppermute | solution.py:399
  101.1 4.6 %collective-permute-start.15 = (f32[64,256]{1,0:T(8,128)S(1)}, f32[64,256]{1,0:T(8,128)S(1)}, u32[]{:S(2)}, u32[]{:S(2)}) collective-permute-start(f32[64,256]{1,0:T(8,128)S(1)} %project.2.refs_0_), channel_id=1, source_target_pairs={{0,2},{1,3},{2,0},{3,1},{4,6},{5,7},{6,4},{7,5},{8,10},{9,11},{10,... | collective-permute-start | bytes 196616 | tf_op jit(solution)/shard_map/ppermute | solution.py:399
  102.4 5.1 %collective-permute-start.14 = (f32[64,256]{1,0:T(8,128)S(1)}, f32[64,256]{1,0:T(8,128)S(1)}, u32[]{:S(2)}, u32[]{:S(2)}) collective-permute-start(f32[64,256]{1,0:T(8,128)S(1)} %project.2.refs_0_), channel_id=1, source_target_pairs={{0,1},{1,2},{2,3},{3,0},{4,5},{5,6},{6,7},{7,4},{8,9},{9,10},{10,1... | collective-permute-start | bytes 196616 | tf_op jit(solution)/shard_map/ppermute | solution.py:399
where the time goes:
time: 109 us
  starting transfers between devices  64 us (59%)
  waiting for transfers between devices  23.5 us (22%)
  Pallas kernels  20.2 us (19%)
    ppermute x6, starting transfers between devices, step(): swap = lambda x: lax.ppermute(x, 'ctx', core_pairs)  29 us
    ppermute x6, starting transfers between devices, step(): to_far = lambda x, k: lax.ppermute(x, 'ctx', far_pairs[k])  21.2 us
    pallas_call x2, Pallas kernels, attend(): pl.pallas_call(functools.partial(attend_kernel, scaling, order), grid_spe...  14.8 us
    ppermute x6, waiting for transfers between devices, step(): to_far = lambda x, k: lax.ppermute(x, 'ctx', far_pairs[k])  8.47 us
    ppermute x6, starting transfers between devices, step(): to_near = lambda x, k: lax.ppermute(x, 'ctx', near_pairs[k])  7.79 us
    ppermute x6, waiting for transfers between devices, step(): to_near = lambda x, k: lax.ppermute(x, 'ctx', near_pairs[k])  7.51 us
    ppermute x6, starting transfers between devices, step(): parts.append(lax.ppermute(partial_out, 'head', moves))  6.11 us
    ppermute x6, waiting for transfers between devices, step(): parts.append(lax.ppermute(partial_out, 'head', moves))  4.35 us
  transfers between devices with their start and end apart: 24, of which 12 were waited for; matrix products, arithmetic and copies ran while one was open for 0% of the time, Pallas kernels for 2%

commit v1 on v0

--- a/solution.py
+++ b/solution.py
@@ -32,7 +32,7 @@
 
 def attend_kernel(scaling, order, lens, info, q_ref, k_ref, v_ref, mine_ref, theirs_ref, s_ref, acc_ref):
     seq = jnp.bitwise_xor(info[1], order(pl.program_id(0)))
-    core = info[3]
+    core = info[2]
     rows, head_dim = k_ref.shape
     queries = q_ref.shape[1]
     per_page = 2 * page
@@ -190,23 +190,16 @@
         out[depth:, :] = stats(top, total)
 
 
-def merge_near_kernel(info, *refs):
-    parts, outs, pieces = refs[:radix], refs[radix:-1], refs[-1]
-    depth = parts[0].shape[0] - stat_rows
+def merge_kernel(*refs):
+    parts, out = refs[:-1], refs[-1]
+    depth = out.shape[0] - stat_rows
     numer, top, total = merged([p[...] for p in parts], depth)
-    half, lanes = depth // 2, numer.shape[1] // 2
-    for a in range(2):
-        at = slice(a * lanes, (a + 1) * lanes)
-        s = stats(top[:, at], total[:, at])
-        for d in range(2):
-            pieces[2 * a + d, :half, :] = numer[d * half : (d + 1) * half, at]
-            pieces[2 * a + d, half:, :] = s
-    for k, out in enumerate(outs):
-        out[...] = pieces[jnp.bitwise_xor(info[2], k)]
+    out[:depth, :] = numer
+    out[depth:, :] = stats(top, total)
 
 
 def finish_kernel(scaling, draft, info, *refs):
-    parts, (q_ref, key_ref, value_ref), out = refs[:radix], refs[radix:-1], refs[-1]
+    parts, (q_ref, key_ref, value_ref), out = refs[:-4], refs[-4:-1], refs[-1]
     depth = parts[0].shape[0] - stat_rows
     numer, top, total = merged([p[...] for p in parts], depth)
     own = contract(key_ref[...], q_ref[...], 1, 1) * scaling
@@ -219,14 +212,7 @@
     fresh = jnp.where(causal, jnp.exp(own - overall), 0.0)
     denominator = total * carried + jnp.sum(fresh, axis=0, keepdims=True)
     added = contract(value_ref[...].astype(f32), fresh, 0, 0, lax.Precision.HIGHEST)
-    added = jnp.where(info[2] % 2 == 0, added[:depth], added[depth:])
     out[...] = ((numer * carried + added) / denominator).astype(bf16).astype(f32)
-
-
-def collect_kernel(info, *refs):
-    parts, out = refs[:-1], refs[-1]
-    for k, part in enumerate(parts):
-        out[jnp.bitwise_xor(info[2], k)] = part[...]
 
 
 def project_kernel(draft, info, *refs):
@@ -234,25 +220,16 @@
     width = x_ref.shape[2]
     for i, piece in enumerate(pieces):
         k, other = i // 2, i % 2
-        g = jnp.bitwise_xor(info[3], other)
-        for a in range(2):
-            att = jnp.concatenate([piece[2 * a + d] for d in range(2)], axis=0)
-            lanes, rows = att.shape
-            att = att.T.astype(bf16)
-            for h in range(rows // draft):
-                col = (a * (rows // draft) + h) * lanes
-                x_ref[g, k * draft : (k + 1) * draft, col : col + lanes] = att[h * draft : (h + 1) * draft]
+        g = jnp.bitwise_xor(info[2], other)
+        seq = jnp.bitwise_xor(info[1], k)
+        at = pl.ds(pl.multiple_of(seq * draft, draft), draft)
+        depth, queries = piece.shape
+        for a in range(queries // depth):
+            att = piece[:, a * depth : (a + 1) * depth].T.astype(bf16)
+            for h in range(depth // draft):
+                col = (a * (depth // draft) + h) * depth
+                x_ref[g, at, col : col + depth] = att[h * draft : (h + 1) * draft]
     out_ref[...] = sum(contract(x_ref[g], w_ref[g * width : (g + 1) * width, :], 1, 0) for g in range(2))
-
-
-def total_kernel(draft, n, info, *refs):
-    parts, out = refs[:-1], refs[-1]
-    for half in range(len(parts) // n):
-        whole = sum(p[...] for p in parts[half * n : (half + 1) * n])
-        count = whole.shape[0] // draft
-        for i in range(count):
-            seq = jnp.bitwise_xor(info[1], half * count + i)
-            out[seq] = whole[i * draft : (i + 1) * draft]
 
 
 def whole_vmem(n):
@@ -287,22 +264,35 @@
         for i in range(n_ctx):
             z, c = i // 2, i % 2
             b, j = place(z, c)
-            b2, j2 = move(b, j)
+            b2, j2 = move(b, j, c)
             out.append((i, 2 * chip(b2, j2, c) + c))
         return out
 
-    near_pairs = [pairs(lambda b, j: (b, j ^ k)) for k in range(radix)]
-    far_pairs = [pairs(lambda b, j: (b ^ k, j)) for k in range(far)]
+    def partner(i, n, turn):
+        return i ^ 1 if turn == 0 else (((i + 1) % n) ^ 1) - 1 if ((i + 1) % n) ^ 1 else n - 1
+
+    near_pairs = [pairs(lambda b, j, c: (b, j ^ k)) for k in range(radix)]
+    far_pairs = [pairs(lambda b, j, c: (partner(b, far, t ^ c), j)) for t in range(2)]
+    n_head = lax.axis_size("head")
+    head_pairs = [
+        [
+            (i * n_head + h, i * n_head + partner(h, n_head, t ^ (i % 2)))
+            for i in range(n_ctx)
+            for h in range(n_head)
+        ]
+        for t in range(2)
+    ]
     core_pairs = [(i, i ^ 1) for i in range(n_ctx)]
 
     swap = lambda x: lax.ppermute(x, "ctx", core_pairs)
     to_near = lambda x, k: lax.ppermute(x, "ctx", near_pairs[k])
-    to_far = lambda x, k: lax.ppermute(x, "ctx", far_pairs[k])
+    to_far = lambda x, t: lax.ppermute(x, "ctx", far_pairs[t])
+    to_head = lambda x, t: lax.ppermute(x, ("ctx", "head"), head_pairs[t])
 
     index = lax.axis_index("ctx")
     core = index % 2
-    block, spot = place(index // 2, core)
-    info = jnp.stack([index * ctx_len, spot, block, core]).astype(jnp.int32)
+    spot = place(index // 2, core)[1]
+    info = jnp.stack([index * ctx_len, spot, core]).astype(jnp.int32)
 
     grouped = query.reshape(seqs, heads, queries, head_dim)
     keys = key_cache.reshape(seqs, ctx_len * heads, head_dim)
@@ -327,37 +317,28 @@
         for k, x in enumerate(found):
             chunks[order(k)] = to_near(x, order(k)) if order(k) else x
     chunks = [chunks[k] for k in range(radix)]
-    piece_shape = (head_dim // 2 + stat_rows, queries // 2)
-    piece = jax.ShapeDtypeStruct(piece_shape, f32)
-    pieces = pl.pallas_call(
-        merge_near_kernel,
-        in_specs=[smem] + whole_vmem(radix),
-        out_specs=whole_vmem(far),
-        out_shape=[piece] * far,
-        scratch_shapes=[VMEM((4, *piece_shape), f32)],
-        name="merge_near",
-        compiler_params=limit(4),
-    )(info, *chunks)
-    order = (2, 1, 3)
-    moved = {k: to_far(pieces[k], k) for k in order}
-    pieces = [pieces[0]] + [moved[k] for k in range(1, far)]
-    att_shape = (head_dim // 2, queries // 2)
+
+    def merge(parts):
+        return pl.pallas_call(
+            merge_kernel,
+            in_specs=whole_vmem(len(parts)),
+            out_specs=pl.BlockSpec(memory_space=VMEM),
+            out_shape=chunk,
+            name="merge",
+            compiler_params=limit(4),
+        )(*parts)
+
+    found = merge(chunks)
+    found = merge([found, to_far(found, 0)])
+    parts = [found, to_far(found, 1)]
+    att_shape = (head_dim, queries)
+    of_spot = lambda i, info: (info[1], info[2], 0, 0)
     picked = pltpu.PrefetchScalarGridSpec(
         num_scalar_prefetch=1,
         grid=(1,),
-        in_specs=[pl.BlockSpec(piece_shape, lambda i, info: (0, 0))] * far
-        + [
-            pl.BlockSpec(
-                (None, None, queries // 2, head_dim),
-                lambda i, info: (info[1], info[3], info[2] // 2, 0),
-            )
-        ]
-        + [
-            pl.BlockSpec(
-                (None, None, draft, head_dim), lambda i, info: (info[1], info[3], 0, 0)
-            )
-        ]
-        * 2,
+        in_specs=[pl.BlockSpec(chunk.shape, lambda i, info: (0, 0))] * 2
+        + [pl.BlockSpec((None, None, queries, head_dim), of_spot)]
+        + [pl.BlockSpec((None, None, draft, head_dim), of_spot)] * 2,
         out_specs=pl.BlockSpec(att_shape, lambda i, info: (0, 0)),
     )
     att = pl.pallas_call(
@@ -366,45 +347,24 @@
         out_shape=jax.ShapeDtypeStruct(att_shape, f32),
         name="finish",
         compiler_params=limit(4),
-    )(info, *pieces, grouped, new_key, new_value)
-    moved = {k: to_far(att, k) for k in order}
-    block_att = pl.pallas_call(
-        collect_kernel,
-        in_specs=[smem] + whole_vmem(far),
+    )(info, *parts, grouped, new_key, new_value)
+    near = [att] + [to_near(att, k) for k in range(1, radix)]
+    pieces = []
+    for part in near:
+        pieces += [part, swap(part)]
+    width = out_weight.shape[1]
+    out = pl.pallas_call(
+        functools.partial(project_kernel, draft),
+        in_specs=[smem] + whole_vmem(len(pieces) + 1),
         out_specs=pl.BlockSpec(memory_space=VMEM),
-        out_shape=jax.ShapeDtypeStruct((far, *att_shape), f32),
-        name="collect",
-        compiler_params=limit(4),
-    )(info, att, *[moved[k] for k in range(1, far)])
-    near = [block_att] + [to_near(block_att, k) for k in range(1, radix)]
-    width = out_weight.shape[1]
-    n_head = lax.axis_size("head")
-    parts = []
-    for half in range(2):
-        pieces = []
-        for k in range(half * half_seqs, (half + 1) * half_seqs):
-            pieces += [near[k], swap(near[k])]
-        partial_out = pl.pallas_call(
-            functools.partial(project_kernel, draft),
-            in_specs=[smem] + whole_vmem(len(pieces) + 1),
-            out_specs=pl.BlockSpec(memory_space=VMEM),
-            out_shape=jax.ShapeDtypeStruct((half_seqs * draft, width), f32),
-            scratch_shapes=[VMEM((heads, half_seqs * draft, out_weight.shape[0] // heads), bf16)],
-            name="project",
-            compiler_params=limit(8),
-        )(info, *pieces, out_weight)
-        parts.append(partial_out)
-        for k in range(1, n_head):
-            moves = [(i, (i + k) % n_head) for i in range(n_head)]
-            parts.append(lax.ppermute(partial_out, "head", moves))
-    return pl.pallas_call(
-        functools.partial(total_kernel, draft, n_head),
-        in_specs=[smem] + whole_vmem(len(parts)),
-        out_specs=pl.BlockSpec(memory_space=VMEM),
-        out_shape=jax.ShapeDtypeStruct((seqs, draft, width), f32),
-        name="total",
-        compiler_params=limit(4),
-    )(info, *parts)
+        out_shape=jax.ShapeDtypeStruct((seqs * draft, width), f32),
+        scratch_shapes=[VMEM((heads, seqs * draft, out_weight.shape[0] // heads), bf16)],
+        name="project",
+        compiler_params=limit(8),
+    )(info, *pieces, out_weight)
+    for t in range(2):
+        out = out + to_head(out, t)
+    return out.reshape(seqs, draft, width)
 
 
 def solution(mesh):

time: 109 us -> 99.8 us (0.916)
  starting transfers between devices: 64 us -> 34.6 us
  waiting for transfers between devices: 23.5 us -> 46.5 us
  Pallas kernels: 20.2 us -> 17.1 us
    ppermute x12 -> x4, starting transfers between devices: 27.3 us -> 0.57 us  [the longest x2 0.28 us: step(): to_far = lambda x, t: lax.ppermute(x, 'ctx', far_pairs[t])]
    ppermute x12 -> x4, waiting for transfers between devices: 12.8 us -> 33.7 us  [the longest x2 24.9 us: step(): to_far = lambda x, t: lax.ppermute(x, 'ctx', far_pairs[t])]
    ppermute x6, starting transfers between devices: 29 us -> 26.3 us  [step(): swap = lambda x: lax.ppermute(x, 'ctx', core_pairs)]
    pallas_call x3 -> x2, Pallas kernels: 2.39 us -> 0.09 us  [merge(): pl.pallas_call(merge_kernel, in_specs=whole_vmem(len(parts)), out_specs=p...]
    ppermute x6, waiting for transfers between devices: 7.51 us -> 9.09 us  [step(): to_near = lambda x, k: lax.ppermute(x, 'ctx', near_pairs[k])]
  transfers between devices with their start and end apart: 24 -> 16, of which waited for: 12 -> 11; matrix products, arithmetic and copies ran while one was open for 0% -> 0% of each run, Pallas kernels for 2% -> 0%
where the time goes in v1:
time: 99.8 us; the launch traced here: 99.7 us
  waiting for transfers between devices  46.5 us (47%)
  starting transfers between devices  34.6 us (35%)
  Pallas kernels  17.1 us (17%)
    ppermute x6, starting transfers between devices, step(): swap = lambda x: lax.ppermute(x, 'ctx', core_pairs)  26.3 us
    ppermute x2, waiting for transfers between devices, step(): to_far = lambda x, t: lax.ppermute(x, 'ctx', far_pairs[t])  24.9 us
    pallas_call x2, Pallas kernels, attend(): pl.pallas_call(functools.partial(attend_kernel, scaling, order), grid_spe...  14.8 us
    ppermute x6, waiting for transfers between devices, step(): to_near = lambda x, k: lax.ppermute(x, 'ctx', near_pairs[k])  9.09 us
    ppermute x2, waiting for transfers between devices, step(): to_head = lambda x, t: lax.ppermute(x, ('ctx', 'head'), head_pairs[t])  8.79 us
    ppermute x6, starting transfers between devices, step(): to_near = lambda x, k: lax.ppermute(x, 'ctx', near_pairs[k])  7.67 us
    ppermute x6, waiting for transfers between devices, step(): swap = lambda x: lax.ppermute(x, 'ctx', core_pairs)  3.7 us
  transfers between devices with their start and end apart: 16, of which 11 were waited for; matrix products, arithmetic and copies ran while one was open for 0% of the time, Pallas kernels for 0%

profile of v1, /device:TPU:33, one launch (start us, length us, event | category | flops | bytes accessed | tf_op | source)
XLA Modules:
  0.0 99.7 jit_solution(8175410849115788525)
XLA Ops:
  0.0 0.1 pad_add_fusion.info
  0.1 0.0 copy-start.4
  0.1 0.7 copy-done.4
  0.7 7.4 %attend.2 = (f32[2,136,256]{2,1,0:T(8,128)S(1)}, f32[2,136,256]{2,1,0:T(8,128)S(1)}) custom-call(s32[4]{0:T(128)S(1)} %copy-done.4, s32[3]{0:T(128)S(1)} %pad_add_fusion.info, bf16[4,2,256,128]{3,2,1,0:T(8,128)(2,1)} %bitcast.7, bf16[4,4096,128]{2,1,0:T(8,128)(2,1)} %bitcast.10, bf16[4,4096,128]{2,1,0:T(8,128)(2,1)} %bitcast.12), custom_call_target="tpu_custom_call" | custom-call | flops 2147483648 | bytes 4194304 | tf_op jit(solution)/shard_map/attend/pallas_call | solution.py:166
  8.1 20.5 %collective-permute-start = (f32[2,136,256]{2,1,0:T(8,128)S(1)}, f32[2,136,256]{2,1,0:T(8,128)S(1)}, u32[]{:S(2)}, u32[]{:S(2)}) collective-permute-start(f32[2,136,256]{2,1,0:T(8,128)S(1)} %get-tuple-element.19), channel_id=1, source_target_pairs={{0,4},{4,0},{8,12},{12,8},{16,20},{20,16},{24,28},{28,24},{32,36},... | collective-permute-start | bytes 835592 | tf_op jit(solution)/shard_map/ppermute | solution.py:287
  28.7 1.2 %collective-permute-done.got_ref = f32[2,136,256]{2,1,0:T(8,128)S(1)} collective-permute-done((f32[2,136,256]{2,1,0:T(8,128)S(1)}, f32[2,136,256]{2,1,0:T(8,128)S(1)}, u32[]{:S(2)}, u32[]{:S(2)}) %collective-permute-start) | collective-permute-done | bytes 278560 | tf_op jit(solution)/shard_map/ppermute | solution.py:287
  29.9 0.1 merge_core.2
  29.9 0.0 copy-start
  29.9 0.0 copy-start.2
  30.0 0.0 copy-start.3
  30.0 0.0 copy-start.1
  30.0 7.4 %attend.3 = (f32[2,136,256]{2,1,0:T(8,128)S(1)}, f32[2,136,256]{2,1,0:T(8,128)S(1)}) custom-call(s32[4]{0:T(128)S(1)} %copy-done.4, s32[3]{0:T(128)S(1)} %pad_add_fusion.info, bf16[4,2,256,128]{3,2,1,0:T(8,128)(2,1)} %bitcast.8, bf16[4,4096,128]{2,1,0:T(8,128)(2,1)} %bitcast.11, bf16[4,4096,128]{2,1,0:T(8,128)(2,1)} %bitcast.13), custom_call_target="tpu_custom_call" | custom-call | flops 2147483648 | bytes 4194304 | tf_op jit(solution)/shard_map/attend/pallas_call | solution.py:166
  37.4 0.5 collective-permute-start.1
  37.9 0.0 collective-permute-start.3
  37.9 0.0 collective-permute-start.4
  37.9 1.2 %collective-permute-done.1.got_ref = f32[2,136,256]{2,1,0:T(8,128)S(1)} collective-permute-done((f32[2,136,256]{2,1,0:T(8,128)S(1)}, f32[2,136,256]{2,1,0:T(8,128)S(1)}, u32[]{:S(2)}, u32[]{:S(2)}) %collective-permute-start.1) | collective-permute-done | bytes 278560 | tf_op jit(solution)/shard_map/ppermute | solution.py:287
  39.1 0.1 merge_core.3
  39.2 3.7 %collective-permute-start.2 = (f32[136,256]{1,0:T(8,128)S(1)}, f32[136,256]{1,0:T(8,128)S(1)}, u32[]{:S(2)}, u32[]{:S(2)}) collective-permute-start(f32[136,256]{1,0:T(8,128)S(1)} %get-tuple-element.28), channel_id=1, source_target_pairs={{0,8},{4,12},{8,0},{12,4},{16,24},{20,28},{24,16},{28,20},{32,40},... | collective-permute-start | bytes 417800 | tf_op jit(solution)/shard_map/ppermute | solution.py:288
  42.9 2.1 %collective-permute-done.3.refs_2_ = f32[136,256]{1,0:T(8,128)S(1)} collective-permute-done((f32[136,256]{1,0:T(8,128)S(1)}, f32[136,256]{1,0:T(8,128)S(1)}, u32[]{:S(2)}, u32[]{:S(2)}) %collective-permute-start.3) | collective-permute-done | bytes 139296 | tf_op jit(solution)/shard_map/ppermute | solution.py:288
  45.0 0.0 collective-permute-done.4.refs_3_
  45.0 4.3 %collective-permute-done.2.refs_1_ = f32[136,256]{1,0:T(8,128)S(1)} collective-permute-done((f32[136,256]{1,0:T(8,128)S(1)}, f32[136,256]{1,0:T(8,128)S(1)}, u32[]{:S(2)}, u32[]{:S(2)}) %collective-permute-start.2) | collective-permute-done | bytes 139296 | tf_op jit(solution)/shard_map/ppermute | solution.py:288
  49.3 0.1 merge.2.refs_0_
  49.3 0.1 collective-permute-start.5
  49.5 16.3 %collective-permute-done.5.refs_1_ = f32[136,256]{1,0:T(8,128)S(1)} collective-permute-done((f32[136,256]{1,0:T(8,128)S(1)}, f32[136,256]{1,0:T(8,128)S(1)}, u32[]{:S(2)}, u32[]{:S(2)}) %collective-permute-start.5) | collective-permute-done | bytes 139296 | tf_op jit(solution)/shard_map/ppermute | solution.py:289
  65.8 0.1 collective-permute-start.6
  65.9 8.6 %collective-permute-done.6.refs_1_ = f32[136,256]{1,0:T(8,128)S(1)} collective-permute-done((f32[136,256]{1,0:T(8,128)S(1)}, f32[136,256]{1,0:T(8,128)S(1)}, u32[]{:S(2)}, u32[]{:S(2)}) %collective-permute-start.6) | collective-permute-done | bytes 139296 | tf_op jit(solution)/shard_map/ppermute | solution.py:289
  74.6 0.0 copy-done
  74.6 0.0 copy-done.2
  74.6 0.0 copy-done.3
  74.6 1.0 finish.1.refs_0_
  75.6 0.1 collective-permute-start.12
  75.7 0.1 collective-permute-start.10
  75.9 3.7 %collective-permute-start.8 = (f32[128,256]{1,0:T(8,128)S(1)}, f32[128,256]{1,0:T(8,128)S(1)}, u32[]{:S(2)}, u32[]{:S(2)}) collective-permute-start(f32[128,256]{1,0:T(8,128)S(1)} %finish.1.refs_0_), channel_id=1, source_target_pairs={{0,8},{4,12},{8,0},{12,4},{16,24},{20,28},{24,16},{28,20},{32,40},... | collective-permute-start | bytes 393224 | tf_op jit(solution)/shard_map/ppermute | solution.py:288
  79.5 1.9 %collective-permute-start.7 = (f32[128,256]{1,0:T(8,128)S(1)}, f32[128,256]{1,0:T(8,128)S(1)}, u32[]{:S(2)}, u32[]{:S(2)}) collective-permute-start(f32[128,256]{1,0:T(8,128)S(1)} %finish.1.refs_0_), channel_id=1, source_target_pairs={{0,4},{4,0},{8,12},{12,8},{16,20},{20,16},{24,28},{28,24},{32,36},... | collective-permute-start | bytes 393224 | tf_op jit(solution)/shard_map/ppermute | solution.py:287
  81.4 0.0 collective-permute-done.12.refs_6_
  81.4 2.8 %collective-permute-start.13 = (f32[128,256]{1,0:T(8,128)S(1)}, f32[128,256]{1,0:T(8,128)S(1)}, u32[]{:S(2)}, u32[]{:S(2)}) collective-permute-start(f32[128,256]{1,0:T(8,128)S(1)} %collective-permute-done.12.refs_6_), channel_id=1, source_target_pairs={{0,4},{4,0},{8,12},{12,8},{16,20},{20,16},{24,28},{28,24},{32,36},... | collective-permute-start | bytes 393224 | tf_op jit(solution)/shard_map/ppermute | solution.py:287
  84.2 1.1 %collective-permute-done.10.refs_4_ = f32[128,256]{1,0:T(8,128)S(1)} collective-permute-done((f32[128,256]{1,0:T(8,128)S(1)}, f32[128,256]{1,0:T(8,128)S(1)}, u32[]{:S(2)}, u32[]{:S(2)}) %collective-permute-start.10) | collective-permute-done | bytes 131104 | tf_op jit(solution)/shard_map/ppermute | solution.py:288
  85.4 0.6 collective-permute-start.11
  86.0 1.5 %collective-permute-done.8.refs_2_ = f32[128,256]{1,0:T(8,128)S(1)} collective-permute-done((f32[128,256]{1,0:T(8,128)S(1)}, f32[128,256]{1,0:T(8,128)S(1)}, u32[]{:S(2)}, u32[]{:S(2)}) %collective-permute-start.8) | collective-permute-done | bytes 131104 | tf_op jit(solution)/shard_map/ppermute | solution.py:288
  87.5 0.0 collective-permute-start.9
  87.5 0.0 collective-permute-done.7.refs_1_
  87.5 0.0 collective-permute-done.13.refs_7_
  87.5 0.0 collective-permute-done.11.refs_5_
  87.5 1.3 %collective-permute-done.9.refs_3_ = f32[128,256]{1,0:T(8,128)S(1)} collective-permute-done((f32[128,256]{1,0:T(8,128)S(1)}, f32[128,256]{1,0:T(8,128)S(1)}, u32[]{:S(2)}, u32[]{:S(2)}) %collective-permute-start.9) | collective-permute-done | bytes 131104 | tf_op jit(solution)/shard_map/ppermute | solution.py:287
  88.9 0.0 copy-done.1
  88.9 1.1 %project.1 = f32[128,256]{1,0:T(8,128)S(1)} custom-call(s32[3]{0:T(128)S(1)} %pad_add_fusion.info, f32[128,256]{1,0:T(8,128)S(1)} %finish.1.refs_0_, f32[128,256]{1,0:T(8,128)S(1)} %collective-permute-done.7.refs_1_, f32[128,256]{1,0:T(8,128)S(1)} %collective-permute-done.8.refs_2_, f32[128,256]{1,0:T(8,128)S(1)} %collective-permute-done.9.refs_3_, ...), custom_call_target="tpu_custom_call" | custom-call | tf_op jit(solution)/shard_map/project/pallas_call | solution.py:356
  89.9 0.1 collective-permute-start.14
  90.1 5.0 %collective-permute-done.14 = f32[128,256]{1,0:T(8,128)S(1)} collective-permute-done((f32[128,256]{1,0:T(8,128)S(1)}, f32[128,256]{1,0:T(8,128)S(1)}, u32[]{:S(2)}, u32[]{:S(2)}) %collective-permute-start.14) | collective-permute-done | bytes 131104 | tf_op jit(solution)/shard_map/ppermute | solution.py:290
  95.1 0.1 collective-permute-start.15
  95.3 3.8 %collective-permute-done.15 = f32[128,256]{1,0:T(8,128)S(1)} collective-permute-done((f32[128,256]{1,0:T(8,128)S(1)}, f32[128,256]{1,0:T(8,128)S(1)}, u32[]{:S(2)}, u32[]{:S(2)}) %collective-permute-start.15) | collective-permute-done | bytes 131104 | tf_op jit(solution)/shard_map/ppermute | solution.py:290
  99.1 0.7 add.17
  (2 shorter events, 0.0 us)
Async XLA Ops:
  0.1 0.7 copy-start.4
  8.1 21.7 %collective-permute-start = (f32[2,136,256]{2,1,0:T(8,128)S(1)}, f32[2,136,256]{2,1,0:T(8,128)S(1)}, u32[]{:S(2)}, u32[]{:S(2)}) collective-permute-start(f32[2,136,256]{2,1,0:T(8,128)S(1)} %get-tuple-element.19), channel_id=1, source_target_pairs={{0,4},{4,0},{8,12},{12,8},{16,20},{20,16},{24,28},{28,24},{32,36},... | collective-permute-start | bytes 835592 | tf_op jit(solution)/shard_map/ppermute | solution.py:287
  29.9 44.6 %copy-start = (bf16[4,16,32,128]{3,2,1,0:T(8,128)(2,1)S(1)}, bf16[4,16,32,128]{3,2,1,0:T(8,128)(2,1)}, u32[]{:S(2)}) copy-start(bf16[4,16,32,128]{3,2,1,0:T(8,128)(2,1)} %param.7) | copy-start | bytes 1572868
  29.9 44.6 %copy-start.2 = (bf16[4,2,32,128]{3,2,1,0:T(8,128)(2,1)S(1)}, bf16[4,2,32,128]{3,2,1,0:T(8,128)(2,1)}, u32[]{:S(2)}) copy-start(bf16[4,2,32,128]{3,2,1,0:T(8,128)(2,1)} %refs_3_.1) | copy-start | bytes 196612
  30.0 44.6 %copy-start.3 = (bf16[4,2,32,128]{3,2,1,0:T(8,128)(2,1)S(1)}, bf16[4,2,32,128]{3,2,1,0:T(8,128)(2,1)}, u32[]{:S(2)}) copy-start(bf16[4,2,32,128]{3,2,1,0:T(8,128)(2,1)} %refs_4_.1) | copy-start | bytes 196612
  30.0 58.9 %copy-start.1 = (bf16[2048,256]{1,0:T(8,128)(2,1)S(1)}, bf16[2048,256]{1,0:T(8,128)(2,1)}, u32[]{:S(2)}) copy-start(bf16[2048,256]{1,0:T(8,128)(2,1)} %refs_8_.1) | copy-start | bytes 3145732
  37.4 1.7 %collective-permute-start.1 = (f32[2,136,256]{2,1,0:T(8,128)S(1)}, f32[2,136,256]{2,1,0:T(8,128)S(1)}, u32[]{:S(2)}, u32[]{:S(2)}) collective-permute-start(f32[2,136,256]{2,1,0:T(8,128)S(1)} %get-tuple-element.24), channel_id=1, source_target_pairs={{0,4},{4,0},{8,12},{12,8},{16,20},{20,16},{24,28},{28,24},{32,36},... | collective-permute-start | bytes 835592 | tf_op jit(solution)/shard_map/ppermute | solution.py:287
  37.9 7.1 %collective-permute-start.3 = (f32[136,256]{1,0:T(8,128)S(1)}, f32[136,256]{1,0:T(8,128)S(1)}, u32[]{:S(2)}, u32[]{:S(2)}) collective-permute-start(f32[136,256]{1,0:T(8,128)S(1)} %get-tuple-element.29), channel_id=1, source_target_pairs={{0,16},{4,116},{8,24},{12,124},{16,0},{20,36},{24,8},{28,44},{32,4... | collective-permute-start | bytes 417800 | tf_op jit(solution)/shard_map/ppermute | solution.py:288
  37.9 7.1 %collective-permute-start.4 = (f32[136,256]{1,0:T(8,128)S(1)}, f32[136,256]{1,0:T(8,128)S(1)}, u32[]{:S(2)}, u32[]{:S(2)}) collective-permute-start(f32[136,256]{1,0:T(8,128)S(1)} %get-tuple-element.30), channel_id=1, source_target_pairs={{0,24},{4,124},{8,16},{12,116},{16,8},{20,44},{24,0},{28,36},{32,5... | collective-permute-start | bytes 417800 | tf_op jit(solution)/shard_map/ppermute | solution.py:288
  39.2 10.1 %collective-permute-start.2 = (f32[136,256]{1,0:T(8,128)S(1)}, f32[136,256]{1,0:T(8,128)S(1)}, u32[]{:S(2)}, u32[]{:S(2)}) collective-permute-start(f32[136,256]{1,0:T(8,128)S(1)} %get-tuple-element.28), channel_id=1, source_target_pairs={{0,8},{4,12},{8,0},{12,4},{16,24},{20,28},{24,16},{28,20},{32,40},... | collective-permute-start | bytes 417800 | tf_op jit(solution)/shard_map/ppermute | solution.py:288
  49.3 16.4 %collective-permute-start.5 = (f32[136,256]{1,0:T(8,128)S(1)}, f32[136,256]{1,0:T(8,128)S(1)}, u32[]{:S(2)}, u32[]{:S(2)}) collective-permute-start(f32[136,256]{1,0:T(8,128)S(1)} %merge.2.refs_0_), channel_id=1, source_target_pairs={{0,32},{4,36},{8,40},{12,44},{16,48},{20,116},{24,56},{28,124},{32... | collective-permute-start | bytes 417800 | tf_op jit(solution)/shard_map/ppermute | solution.py:289
  65.8 8.8 %collective-permute-start.6 = (f32[136,256]{1,0:T(8,128)S(1)}, f32[136,256]{1,0:T(8,128)S(1)}, u32[]{:S(2)}, u32[]{:S(2)}) collective-permute-start(f32[136,256]{1,0:T(8,128)S(1)} %merge.3.refs_0_), channel_id=1, source_target_pairs={{0,96},{4,100},{8,104},{12,108},{16,112},{20,52},{24,120},{28,60},... | collective-permute-start | bytes 417800 | tf_op jit(solution)/shard_map/ppermute | solution.py:289
  75.6 5.9 %collective-permute-start.12 = (f32[128,256]{1,0:T(8,128)S(1)}, f32[128,256]{1,0:T(8,128)S(1)}, u32[]{:S(2)}, u32[]{:S(2)}) collective-permute-start(f32[128,256]{1,0:T(8,128)S(1)} %finish.1.refs_0_), channel_id=1, source_target_pairs={{0,24},{4,124},{8,16},{12,116},{16,8},{20,44},{24,0},{28,36},{32,5... | collective-permute-start | bytes 393224 | tf_op jit(solution)/shard_map/ppermute | solution.py:288
  75.7 9.7 %collective-permute-start.10 = (f32[128,256]{1,0:T(8,128)S(1)}, f32[128,256]{1,0:T(8,128)S(1)}, u32[]{:S(2)}, u32[]{:S(2)}) collective-permute-start(f32[128,256]{1,0:T(8,128)S(1)} %finish.1.refs_0_), channel_id=1, source_target_pairs={{0,16},{4,116},{8,24},{12,124},{16,0},{20,36},{24,8},{28,44},{32,4... | collective-permute-start | bytes 393224 | tf_op jit(solution)/shard_map/ppermute | solution.py:288
  75.9 11.7 %collective-permute-start.8 = (f32[128,256]{1,0:T(8,128)S(1)}, f32[128,256]{1,0:T(8,128)S(1)}, u32[]{:S(2)}, u32[]{:S(2)}) collective-permute-start(f32[128,256]{1,0:T(8,128)S(1)} %finish.1.refs_0_), channel_id=1, source_target_pairs={{0,8},{4,12},{8,0},{12,4},{16,24},{20,28},{24,16},{28,20},{32,40},... | collective-permute-start | bytes 393224 | tf_op jit(solution)/shard_map/ppermute | solution.py:288
  79.5 8.0 %collective-permute-start.7 = (f32[128,256]{1,0:T(8,128)S(1)}, f32[128,256]{1,0:T(8,128)S(1)}, u32[]{:S(2)}, u32[]{:S(2)}) collective-permute-start(f32[128,256]{1,0:T(8,128)S(1)} %finish.1.refs_0_), channel_id=1, source_target_pairs={{0,4},{4,0},{8,12},{12,8},{16,20},{20,16},{24,28},{28,24},{32,36},... | collective-permute-start | bytes 393224 | tf_op jit(solution)/shard_map/ppermute | solution.py:287
  81.4 6.1 %collective-permute-start.13 = (f32[128,256]{1,0:T(8,128)S(1)}, f32[128,256]{1,0:T(8,128)S(1)}, u32[]{:S(2)}, u32[]{:S(2)}) collective-permute-start(f32[128,256]{1,0:T(8,128)S(1)} %collective-permute-done.12.refs_6_), channel_id=1, source_target_pairs={{0,4},{4,0},{8,12},{12,8},{16,20},{20,16},{24,28},{28,24},{32,36},... | collective-permute-start | bytes 393224 | tf_op jit(solution)/shard_map/ppermute | solution.py:287
  85.4 2.2 %collective-permute-start.11 = (f32[128,256]{1,0:T(8,128)S(1)}, f32[128,256]{1,0:T(8,128)S(1)}, u32[]{:S(2)}, u32[]{:S(2)}) collective-permute-start(f32[128,256]{1,0:T(8,128)S(1)} %collective-permute-done.10.refs_4_), channel_id=1, source_target_pairs={{0,4},{4,0},{8,12},{12,8},{16,20},{20,16},{24,28},{28,24},{32,36},... | collective-permute-start | bytes 393224 | tf_op jit(solution)/shard_map/ppermute | solution.py:287
  87.5 1.3 %collective-permute-start.9 = (f32[128,256]{1,0:T(8,128)S(1)}, f32[128,256]{1,0:T(8,128)S(1)}, u32[]{:S(2)}, u32[]{:S(2)}) collective-permute-start(f32[128,256]{1,0:T(8,128)S(1)} %collective-permute-done.8.refs_2_), channel_id=1, source_target_pairs={{0,4},{4,0},{8,12},{12,8},{16,20},{20,16},{24,28},{28,24},{32,36},... | collective-permute-start | bytes 393224 | tf_op jit(solution)/shard_map/ppermute | solution.py:287
  89.9 5.2 %collective-permute-start.14 = (f32[128,256]{1,0:T(8,128)S(1)}, f32[128,256]{1,0:T(8,128)S(1)}, u32[]{:S(2)}, u32[]{:S(2)}) collective-permute-start(f32[128,256]{1,0:T(8,128)S(1)} %project.1), channel_id=1, source_target_pairs={{0,1},{1,0},{2,3},{3,2},{4,7},{5,6},{6,5},{7,4},{8,9},{9,8},{10,11... | collective-permute-start | bytes 393224 | tf_op jit(solution)/shard_map/ppermute | solution.py:290
  95.1 3.9 %collective-permute-start.15 = (f32[128,256]{1,0:T(8,128)S(1)}, f32[128,256]{1,0:T(8,128)S(1)}, u32[]{:S(2)}, u32[]{:S(2)}) collective-permute-start(f32[128,256]{1,0:T(8,128)S(1)} %add.16), channel_id=1, source_target_pairs={{0,3},{1,2},{2,1},{3,0},{4,5},{5,4},{6,7},{7,6},{8,11},{9,10},{10,... | collective-permute-start | bytes 393224 | tf_op jit(solution)/shard_map/ppermute | solution.py:290

commit v2 on v1

--- a/solution.py
+++ b/solution.py
@@ -30,13 +30,13 @@
     )
 
 
-def attend_kernel(scaling, order, lens, info, q_ref, k_ref, v_ref, mine_ref, theirs_ref, s_ref, acc_ref):
+def attend_kernel(scaling, order, info, q_ref, k_ref, v_ref, mine_ref, theirs_ref, s_ref, acc_ref):
     seq = jnp.bitwise_xor(info[1], order(pl.program_id(0)))
     core = info[2]
     rows, head_dim = k_ref.shape
     queries = q_ref.shape[1]
     per_page = 2 * page
-    usable = jnp.clip(lens[seq] - info[0], 0, rows // 2)
+    usable = jnp.clip(info[3 + seq] - info[0], 0, rows // 2)
     pages = usable // page
     factor = scaling * math.log2(math.e)
     d2 = 2 * head_dim
@@ -137,24 +137,36 @@
             ref[head_dim:, :] = nothing
 
 
-def attend(query, key_cache, value_cache, lengths, info, scaling, order, steps):
+def attend(query, key_cache, value_cache, info, scaling, order, steps):
     _, heads, queries, head_dim = query.shape
     rows = key_cache.shape[1]
     block = (None, head_dim + stat_rows, queries)
     out = jax.ShapeDtypeStruct((steps, *block[1:]), f32)
-    of_seq = lambda k, lens, info: (jnp.bitwise_xor(info[1], order(k)), 0, 0)
+
+    def used(k, info):
+        return info[3 + jnp.bitwise_xor(info[1], order(k))] > info[0]
+
+    def of_seq(k, info):
+        first = jnp.int32(0)
+        for step in reversed(range(1, steps)):
+            first = jnp.where(used(step, info), step, first)
+        at = jnp.where(used(0, info), 0, first)
+        for step in range(1, steps):
+            at = jnp.where(jnp.logical_and(k >= step, used(step, info)), step, at)
+        return jnp.bitwise_xor(info[1], order(at)), 0, 0
+
     spec = pltpu.PrefetchScalarGridSpec(
-        num_scalar_prefetch=2,
+        num_scalar_prefetch=1,
         grid=(steps,),
         in_specs=[
             pl.BlockSpec(
                 (None, heads, queries, head_dim),
-                lambda k, lens, info: (jnp.bitwise_xor(info[1], order(k)), 0, 0, 0),
+                lambda k, info: (jnp.bitwise_xor(info[1], order(k)), 0, 0, 0),
             ),
             pl.BlockSpec((None, rows, head_dim), of_seq),
             pl.BlockSpec((None, rows, head_dim), of_seq),
         ],
-        out_specs=[pl.BlockSpec(block, lambda k, lens, info: (k, 0, 0))] * 2,
+        out_specs=[pl.BlockSpec(block, lambda k, info: (k, 0, 0))] * 2,
         scratch_shapes=[VMEM((rows, queries), f32), VMEM((2 * head_dim + 16, queries), f32)],
     )
     cost = pl.CostEstimate(
@@ -170,7 +182,7 @@
         name="attend",
         compiler_params=limit(24),
         cost_estimate=cost,
-    )(lengths, info, *in_hbm)
+    )(info, *in_hbm)
 
 
 def merged(parts, depth):
@@ -202,7 +214,7 @@
     parts, (q_ref, key_ref, value_ref), out = refs[:-4], refs[-4:-1], refs[-1]
     depth = parts[0].shape[0] - stat_rows
     numer, top, total = merged([p[...] for p in parts], depth)
-    own = contract(key_ref[...], q_ref[...], 1, 1) * scaling
+    own = contract(key_ref[info[1], info[2]], q_ref[info[1], info[2]], 1, 1) * scaling
     at = lax.broadcasted_iota(jnp.int32, own.shape, 0)
     row = lax.broadcasted_iota(jnp.int32, own.shape, 1) % draft
     causal = at <= row
@@ -211,7 +223,7 @@
     carried = jnp.exp(top - overall)
     fresh = jnp.where(causal, jnp.exp(own - overall), 0.0)
     denominator = total * carried + jnp.sum(fresh, axis=0, keepdims=True)
-    added = contract(value_ref[...].astype(f32), fresh, 0, 0, lax.Precision.HIGHEST)
+    added = contract(value_ref[info[1], info[2]].astype(f32), fresh, 0, 0, lax.Precision.HIGHEST)
     out[...] = ((numer * carried + added) / denominator).astype(bf16).astype(f32)
 
 
@@ -259,20 +271,26 @@
         shift = c * (radix // 2)
         return (b * radix + shift + (j - shift) % radix) % chips
 
-    def pairs(move):
+    def pairs(k):
         out = []
         for i in range(n_ctx):
-            z, c = i // 2, i % 2
+            z, c = divmod(i, 2)
             b, j = place(z, c)
-            b2, j2 = move(b, j, c)
-            out.append((i, 2 * chip(b2, j2, c) + c))
+            out.append((i, 2 * chip(b, j ^ k, c) + c))
         return out
 
     def partner(i, n, turn):
         return i ^ 1 if turn == 0 else (((i + 1) % n) ^ 1) - 1 if ((i + 1) % n) ^ 1 else n - 1
 
-    near_pairs = [pairs(lambda b, j, c: (b, j ^ k)) for k in range(radix)]
-    far_pairs = [pairs(lambda b, j, c: (partner(b, far, t ^ c), j)) for t in range(2)]
+    near_pairs = [pairs(k) for k in range(radix)]
+    far_pairs = [
+        [
+            (i, 2 * (partner(z // radix, far, t ^ c) * radix + z % radix) + c)
+            for i in range(n_ctx)
+            for z, c in [divmod(i, 2)]
+        ]
+        for t in range(2)
+    ]
     n_head = lax.axis_size("head")
     head_pairs = [
         [
@@ -292,7 +310,7 @@
     index = lax.axis_index("ctx")
     core = index % 2
     spot = place(index // 2, core)[1]
-    info = jnp.stack([index * ctx_len, spot, core]).astype(jnp.int32)
+    info = jnp.concatenate([jnp.stack([index * ctx_len, spot, core]).astype(jnp.int32), lengths])
 
     grouped = query.reshape(seqs, heads, queries, head_dim)
     keys = key_cache.reshape(seqs, ctx_len * heads, head_dim)
@@ -303,7 +321,7 @@
     chunks = {}
     for half in range(2):
         order = lambda k, half=half: seqs - 1 - half * half_seqs - k
-        mine, theirs = attend(grouped, keys, values, lengths, gate, scaling, order, half_seqs)
+        mine, theirs = attend(grouped, keys, values, gate, scaling, order, half_seqs)
         got = swap(theirs)
         found = pl.pallas_call(
             merge_core_kernel,
@@ -331,20 +349,11 @@
     found = merge(chunks)
     found = merge([found, to_far(found, 0)])
     parts = [found, to_far(found, 1)]
-    att_shape = (head_dim, queries)
-    of_spot = lambda i, info: (info[1], info[2], 0, 0)
-    picked = pltpu.PrefetchScalarGridSpec(
-        num_scalar_prefetch=1,
-        grid=(1,),
-        in_specs=[pl.BlockSpec(chunk.shape, lambda i, info: (0, 0))] * 2
-        + [pl.BlockSpec((None, None, queries, head_dim), of_spot)]
-        + [pl.BlockSpec((None, None, draft, head_dim), of_spot)] * 2,
-        out_specs=pl.BlockSpec(att_shape, lambda i, info: (0, 0)),
-    )
     att = pl.pallas_call(
         functools.partial(finish_kernel, scaling, draft),
-        grid_spec=picked,
-        out_shape=jax.ShapeDtypeStruct(att_shape, f32),
+        in_specs=[smem] + whole_vmem(5),
+        out_specs=pl.BlockSpec(memory_space=VMEM),
+        out_shape=jax.ShapeDtypeStruct((head_dim, queries), f32),
         name="finish",
         compiler_params=limit(4),
     )(info, *parts, grouped, new_key, new_value)

time: 99.8 us -> 94 us (0.942)
  waiting for transfers between devices: 46.5 us -> 38 us
  starting transfers between devices: 34.6 us -> 37.1 us
    ppermute x2, waiting for transfers between devices: 24.9 us -> 18.6 us  [step(): to_far = lambda x, t: lax.ppermute(x, 'ctx', far_pairs[t])]
    ppermute x6, starting transfers between devices: 26.3 us -> 28.9 us  [step(): swap = lambda x: lax.ppermute(x, 'ctx', core_pairs)]
    ppermute x6, waiting for transfers between devices: 9.09 us -> 7.24 us  [step(): to_near = lambda x, k: lax.ppermute(x, 'ctx', near_pairs[k])]
  transfers between devices with their start and end apart: 16 -> 16, of which waited for: 11 -> 12; matrix products, arithmetic and copies ran while one was open for 0% -> 0% of each run, Pallas kernels for 0% -> 0%
where the time goes in v2:
time: 94 us; the launch traced here: 93.9 us
  waiting for transfers between devices  38 us (40%)
  starting transfers between devices  37.1 us (39%)
  Pallas kernels  17.2 us (18%)
  other arithmetic  1.42 us (2%)
    ppermute x6, starting transfers between devices, step(): swap = lambda x: lax.ppermute(x, 'ctx', core_pairs)  28.9 us
    ppermute x2, waiting for transfers between devices, step(): to_far = lambda x, t: lax.ppermute(x, 'ctx', far_pairs[t])  18.6 us
    pallas_call x2, Pallas kernels, attend(): pl.pallas_call(functools.partial(attend_kernel, scaling, order), grid_spe...  15 us
    ppermute x2, waiting for transfers between devices, step(): to_head = lambda x, t: lax.ppermute(x, ('ctx', 'head'), head_pairs[t])  8.79 us
    ppermute x6, starting transfers between devices, step(): to_near = lambda x, k: lax.ppermute(x, 'ctx', near_pairs[k])  7.68 us
    ppermute x6, waiting for transfers between devices, step(): to_near = lambda x, k: lax.ppermute(x, 'ctx', near_pairs[k])  7.24 us
    ppermute x6, waiting for transfers between devices, step(): swap = lambda x: lax.ppermute(x, 'ctx', core_pairs)  3.35 us
  transfers between devices with their start and end apart: 16, of which 12 were waited for; matrix products, arithmetic and copies ran while one was open for 0% of the time, Pallas kernels for 0%

profile of v2, /device:TPU:33, one launch (start us, length us, event | category | flops | bytes accessed | tf_op | source)
XLA Modules:
  0.0 93.9 jit_solution(16871113817438605595)
XLA Ops:
  0.0 0.7 pad_add_fusion.info
  0.7 7.5 %attend.2 = (f32[2,136,256]{2,1,0:T(8,128)S(1)}, f32[2,136,256]{2,1,0:T(8,128)S(1)}) custom-call(s32[7]{0:T(128)S(1)} %pad_add_fusion.info, bf16[4,2,256,128]{3,2,1,0:T(8,128)(2,1)} %bitcast.7, bf16[4,4096,128]{2,1,0:T(8,128)(2,1)} %bitcast.10, bf16[4,4096,128]{2,1,0:T(8,128)(2,1)} %bitcast.12), custom_call_target="tpu_custom_call" | custom-call | flops 2147483648 | bytes 4194304 | tf_op jit(solution)/shard_map/attend/pallas_call | solution.py:178
  8.2 20.5 %collective-permute-start = (f32[2,136,256]{2,1,0:T(8,128)S(1)}, f32[2,136,256]{2,1,0:T(8,128)S(1)}, u32[]{:S(2)}, u32[]{:S(2)}) collective-permute-start(f32[2,136,256]{2,1,0:T(8,128)S(1)} %get-tuple-element.19), channel_id=1, source_target_pairs={{0,4},{4,0},{8,12},{12,8},{16,20},{20,16},{24,28},{28,24},{32,36},... | collective-permute-start | bytes 835592 | tf_op jit(solution)/shard_map/ppermute | solution.py:305
  28.8 1.2 %collective-permute-done.got_ref = f32[2,136,256]{2,1,0:T(8,128)S(1)} collective-permute-done((f32[2,136,256]{2,1,0:T(8,128)S(1)}, f32[2,136,256]{2,1,0:T(8,128)S(1)}, u32[]{:S(2)}, u32[]{:S(2)}) %collective-permute-start) | collective-permute-done | bytes 278560 | tf_op jit(solution)/shard_map/ppermute | solution.py:305
  29.9 0.1 merge_core.2
  30.0 0.0 copy-start
  30.0 0.0 copy-start.2
  30.0 0.0 copy-start.3
  30.0 0.0 copy-start.1
  30.1 7.5 %attend.3 = (f32[2,136,256]{2,1,0:T(8,128)S(1)}, f32[2,136,256]{2,1,0:T(8,128)S(1)}) custom-call(s32[7]{0:T(128)S(1)} %pad_add_fusion.info, bf16[4,2,256,128]{3,2,1,0:T(8,128)(2,1)} %bitcast.8, bf16[4,4096,128]{2,1,0:T(8,128)(2,1)} %bitcast.11, bf16[4,4096,128]{2,1,0:T(8,128)(2,1)} %bitcast.13), custom_call_target="tpu_custom_call" | custom-call | flops 2147483648 | bytes 4194304 | tf_op jit(solution)/shard_map/attend/pallas_call | solution.py:178
  37.6 0.5 collective-permute-start.1
  38.0 0.0 collective-permute-start.3
  38.1 0.0 collective-permute-start.4
  38.1 1.2 %collective-permute-done.1.got_ref = f32[2,136,256]{2,1,0:T(8,128)S(1)} collective-permute-done((f32[2,136,256]{2,1,0:T(8,128)S(1)}, f32[2,136,256]{2,1,0:T(8,128)S(1)}, u32[]{:S(2)}, u32[]{:S(2)}) %collective-permute-start.1) | collective-permute-done | bytes 278560 | tf_op jit(solution)/shard_map/ppermute | solution.py:305
  39.2 0.1 merge_core.3
  39.3 3.7 %collective-permute-start.2 = (f32[136,256]{1,0:T(8,128)S(1)}, f32[136,256]{1,0:T(8,128)S(1)}, u32[]{:S(2)}, u32[]{:S(2)}) collective-permute-start(f32[136,256]{1,0:T(8,128)S(1)} %get-tuple-element.28), channel_id=1, source_target_pairs={{0,8},{4,12},{8,0},{12,4},{16,24},{20,28},{24,16},{28,20},{32,40},... | collective-permute-start | bytes 417800 | tf_op jit(solution)/shard_map/ppermute | solution.py:306
  43.0 1.7 %collective-permute-done.3.refs_2_ = f32[136,256]{1,0:T(8,128)S(1)} collective-permute-done((f32[136,256]{1,0:T(8,128)S(1)}, f32[136,256]{1,0:T(8,128)S(1)}, u32[]{:S(2)}, u32[]{:S(2)}) %collective-permute-start.3) | collective-permute-done | bytes 139296 | tf_op jit(solution)/shard_map/ppermute | solution.py:306
  44.7 1.5 %collective-permute-done.4.refs_3_ = f32[136,256]{1,0:T(8,128)S(1)} collective-permute-done((f32[136,256]{1,0:T(8,128)S(1)}, f32[136,256]{1,0:T(8,128)S(1)}, u32[]{:S(2)}, u32[]{:S(2)}) %collective-permute-start.4) | collective-permute-done | bytes 139296 | tf_op jit(solution)/shard_map/ppermute | solution.py:306
  46.2 3.3 %collective-permute-done.2.refs_1_ = f32[136,256]{1,0:T(8,128)S(1)} collective-permute-done((f32[136,256]{1,0:T(8,128)S(1)}, f32[136,256]{1,0:T(8,128)S(1)}, u32[]{:S(2)}, u32[]{:S(2)}) %collective-permute-start.2) | collective-permute-done | bytes 139296 | tf_op jit(solution)/shard_map/ppermute | solution.py:306
  49.4 0.1 merge.2.refs_0_
  49.5 0.1 collective-permute-start.5
  49.6 9.4 %collective-permute-done.5.refs_1_ = f32[136,256]{1,0:T(8,128)S(1)} collective-permute-done((f32[136,256]{1,0:T(8,128)S(1)}, f32[136,256]{1,0:T(8,128)S(1)}, u32[]{:S(2)}, u32[]{:S(2)}) %collective-permute-start.5) | collective-permute-done | bytes 139296 | tf_op jit(solution)/shard_map/ppermute | solution.py:307
  59.1 0.1 collective-permute-start.6
  59.3 9.1 %collective-permute-done.6.refs_1_ = f32[136,256]{1,0:T(8,128)S(1)} collective-permute-done((f32[136,256]{1,0:T(8,128)S(1)}, f32[136,256]{1,0:T(8,128)S(1)}, u32[]{:S(2)}, u32[]{:S(2)}) %collective-permute-start.6) | collective-permute-done | bytes 139296 | tf_op jit(solution)/shard_map/ppermute | solution.py:307
  68.4 0.0 copy-done
  68.4 0.0 copy-done.2
  68.4 0.0 copy-done.3
  68.4 1.0 %finish.1.refs_0_ = f32[128,256]{1,0:T(8,128)S(1)} custom-call(s32[7]{0:T(128)S(1)} %pad_add_fusion.info, f32[136,256]{1,0:T(8,128)S(1)} %merge.3.refs_0_, f32[136,256]{1,0:T(8,128)S(1)} %collective-permute-done.6.refs_1_, bf16[4,2,256,128]{3,2,1,0:T(8,128)(2,1)S(1)} %bitcast.9, bf16[4,2,32,128]{3,2,1,0:T(8,128)(2,1)S(1)} %copy-done.2, ...), custom_call_target="tpu_custom_call" | custom-call | tf_op jit(solution)/shard_map/finish/pallas_call | solution.py:352
  69.4 0.1 collective-permute-start.12
  69.6 2.4 %collective-permute-start.10 = (f32[128,256]{1,0:T(8,128)S(1)}, f32[128,256]{1,0:T(8,128)S(1)}, u32[]{:S(2)}, u32[]{:S(2)}) collective-permute-start(f32[128,256]{1,0:T(8,128)S(1)} %finish.1.refs_0_), channel_id=1, source_target_pairs={{0,16},{4,116},{8,24},{12,124},{16,0},{20,36},{24,8},{28,44},{32,4... | collective-permute-start | bytes 393224 | tf_op jit(solution)/shard_map/ppermute | solution.py:306
  72.0 1.4 %collective-permute-start.8 = (f32[128,256]{1,0:T(8,128)S(1)}, f32[128,256]{1,0:T(8,128)S(1)}, u32[]{:S(2)}, u32[]{:S(2)}) collective-permute-start(f32[128,256]{1,0:T(8,128)S(1)} %finish.1.refs_0_), channel_id=1, source_target_pairs={{0,8},{4,12},{8,0},{12,4},{16,24},{20,28},{24,16},{28,20},{32,40},... | collective-permute-start | bytes 393224 | tf_op jit(solution)/shard_map/ppermute | solution.py:306
  73.4 3.3 %collective-permute-start.7 = (f32[128,256]{1,0:T(8,128)S(1)}, f32[128,256]{1,0:T(8,128)S(1)}, u32[]{:S(2)}, u32[]{:S(2)}) collective-permute-start(f32[128,256]{1,0:T(8,128)S(1)} %finish.1.refs_0_), channel_id=1, source_target_pairs={{0,4},{4,0},{8,12},{12,8},{16,20},{20,16},{24,28},{28,24},{32,36},... | collective-permute-start | bytes 393224 | tf_op jit(solution)/shard_map/ppermute | solution.py:305
  76.7 0.3 collective-permute-done.12.refs_6_
  76.9 3.6 %collective-permute-start.13 = (f32[128,256]{1,0:T(8,128)S(1)}, f32[128,256]{1,0:T(8,128)S(1)}, u32[]{:S(2)}, u32[]{:S(2)}) collective-permute-start(f32[128,256]{1,0:T(8,128)S(1)} %collective-permute-done.12.refs_6_), channel_id=1, source_target_pairs={{0,4},{4,0},{8,12},{12,8},{16,20},{20,16},{24,28},{28,24},{32,36},... | collective-permute-start | bytes 393224 | tf_op jit(solution)/shard_map/ppermute | solution.py:305
  80.6 0.0 collective-permute-done.10.refs_4_
  80.6 0.0 collective-permute-start.11
  80.6 0.5 collective-permute-done.8.refs_2_
  81.1 1.0 %collective-permute-start.9 = (f32[128,256]{1,0:T(8,128)S(1)}, f32[128,256]{1,0:T(8,128)S(1)}, u32[]{:S(2)}, u32[]{:S(2)}) collective-permute-start(f32[128,256]{1,0:T(8,128)S(1)} %collective-permute-done.8.refs_2_), channel_id=1, source_target_pairs={{0,4},{4,0},{8,12},{12,8},{16,20},{20,16},{24,28},{28,24},{32,36},... | collective-permute-start | bytes 393224 | tf_op jit(solution)/shard_map/ppermute | solution.py:305
  82.1 0.0 collective-permute-done.7.refs_1_
  82.1 0.0 collective-permute-done.13.refs_7_
  82.1 0.0 collective-permute-done.11.refs_5_
  82.1 1.0 %collective-permute-done.9.refs_3_ = f32[128,256]{1,0:T(8,128)S(1)} collective-permute-done((f32[128,256]{1,0:T(8,128)S(1)}, f32[128,256]{1,0:T(8,128)S(1)}, u32[]{:S(2)}, u32[]{:S(2)}) %collective-permute-start.9) | collective-permute-done | bytes 131104 | tf_op jit(solution)/shard_map/ppermute | solution.py:305
  83.0 0.0 copy-done.1
  83.0 1.1 %project.1 = f32[128,256]{1,0:T(8,128)S(1)} custom-call(s32[7]{0:T(128)S(1)} %pad_add_fusion.info, f32[128,256]{1,0:T(8,128)S(1)} %finish.1.refs_0_, f32[128,256]{1,0:T(8,128)S(1)} %collective-permute-done.7.refs_1_, f32[128,256]{1,0:T(8,128)S(1)} %collective-permute-done.8.refs_2_, f32[128,256]{1,0:T(8,128)S(1)} %collective-permute-done.9.refs_3_, ...), custom_call_target="tpu_custom_call" | custom-call | tf_op jit(solution)/shard_map/project/pallas_call | solution.py:365
  84.1 0.1 collective-permute-start.14
  84.3 5.0 %collective-permute-done.14 = f32[128,256]{1,0:T(8,128)S(1)} collective-permute-done((f32[128,256]{1,0:T(8,128)S(1)}, f32[128,256]{1,0:T(8,128)S(1)}, u32[]{:S(2)}, u32[]{:S(2)}) %collective-permute-start.14) | collective-permute-done | bytes 131104 | tf_op jit(solution)/shard_map/ppermute | solution.py:308
  89.3 0.1 collective-permute-start.15
  89.4 3.8 %collective-permute-done.15 = f32[128,256]{1,0:T(8,128)S(1)} collective-permute-done((f32[128,256]{1,0:T(8,128)S(1)}, f32[128,256]{1,0:T(8,128)S(1)}, u32[]{:S(2)}, u32[]{:S(2)}) %collective-permute-start.15) | collective-permute-done | bytes 131104 | tf_op jit(solution)/shard_map/ppermute | solution.py:308
  93.2 0.7 add.17
  (2 shorter events, 0.0 us)
Async XLA Ops:
  8.2 21.7 %collective-permute-start = (f32[2,136,256]{2,1,0:T(8,128)S(1)}, f32[2,136,256]{2,1,0:T(8,128)S(1)}, u32[]{:S(2)}, u32[]{:S(2)}) collective-permute-start(f32[2,136,256]{2,1,0:T(8,128)S(1)} %get-tuple-element.19), channel_id=1, source_target_pairs={{0,4},{4,0},{8,12},{12,8},{16,20},{20,16},{24,28},{28,24},{32,36},... | collective-permute-start | bytes 835592 | tf_op jit(solution)/shard_map/ppermute | solution.py:305
  30.0 38.4 %copy-start = (bf16[4,16,32,128]{3,2,1,0:T(8,128)(2,1)S(1)}, bf16[4,16,32,128]{3,2,1,0:T(8,128)(2,1)}, u32[]{:S(2)}) copy-start(bf16[4,16,32,128]{3,2,1,0:T(8,128)(2,1)} %param.7) | copy-start | bytes 1572868
  30.0 38.4 %copy-start.2 = (bf16[4,2,32,128]{3,2,1,0:T(8,128)(2,1)S(1)}, bf16[4,2,32,128]{3,2,1,0:T(8,128)(2,1)}, u32[]{:S(2)}) copy-start(bf16[4,2,32,128]{3,2,1,0:T(8,128)(2,1)} %refs_3_.1) | copy-start | bytes 196612
  30.0 38.4 %copy-start.3 = (bf16[4,2,32,128]{3,2,1,0:T(8,128)(2,1)S(1)}, bf16[4,2,32,128]{3,2,1,0:T(8,128)(2,1)}, u32[]{:S(2)}) copy-start(bf16[4,2,32,128]{3,2,1,0:T(8,128)(2,1)} %refs_4_.1) | copy-start | bytes 196612
  30.0 53.0 %copy-start.1 = (bf16[2048,256]{1,0:T(8,128)(2,1)S(1)}, bf16[2048,256]{1,0:T(8,128)(2,1)}, u32[]{:S(2)}) copy-start(bf16[2048,256]{1,0:T(8,128)(2,1)} %refs_8_.1) | copy-start | bytes 3145732
  37.6 1.7 %collective-permute-start.1 = (f32[2,136,256]{2,1,0:T(8,128)S(1)}, f32[2,136,256]{2,1,0:T(8,128)S(1)}, u32[]{:S(2)}, u32[]{:S(2)}) collective-permute-start(f32[2,136,256]{2,1,0:T(8,128)S(1)} %get-tuple-element.24), channel_id=1, source_target_pairs={{0,4},{4,0},{8,12},{12,8},{16,20},{20,16},{24,28},{28,24},{32,36},... | collective-permute-start | bytes 835592 | tf_op jit(solution)/shard_map/ppermute | solution.py:305
  38.0 6.6 %collective-permute-start.3 = (f32[136,256]{1,0:T(8,128)S(1)}, f32[136,256]{1,0:T(8,128)S(1)}, u32[]{:S(2)}, u32[]{:S(2)}) collective-permute-start(f32[136,256]{1,0:T(8,128)S(1)} %get-tuple-element.29), channel_id=1, source_target_pairs={{0,16},{4,116},{8,24},{12,124},{16,0},{20,36},{24,8},{28,44},{32,4... | collective-permute-start | bytes 417800 | tf_op jit(solution)/shard_map/ppermute | solution.py:306
  38.1 8.1 %collective-permute-start.4 = (f32[136,256]{1,0:T(8,128)S(1)}, f32[136,256]{1,0:T(8,128)S(1)}, u32[]{:S(2)}, u32[]{:S(2)}) collective-permute-start(f32[136,256]{1,0:T(8,128)S(1)} %get-tuple-element.30), channel_id=1, source_target_pairs={{0,24},{4,124},{8,16},{12,116},{16,8},{20,44},{24,0},{28,36},{32,5... | collective-permute-start | bytes 417800 | tf_op jit(solution)/shard_map/ppermute | solution.py:306
  39.3 10.1 %collective-permute-start.2 = (f32[136,256]{1,0:T(8,128)S(1)}, f32[136,256]{1,0:T(8,128)S(1)}, u32[]{:S(2)}, u32[]{:S(2)}) collective-permute-start(f32[136,256]{1,0:T(8,128)S(1)} %get-tuple-element.28), channel_id=1, source_target_pairs={{0,8},{4,12},{8,0},{12,4},{16,24},{20,28},{24,16},{28,20},{32,40},... | collective-permute-start | bytes 417800 | tf_op jit(solution)/shard_map/ppermute | solution.py:306
  49.5 9.6 %collective-permute-start.5 = (f32[136,256]{1,0:T(8,128)S(1)}, f32[136,256]{1,0:T(8,128)S(1)}, u32[]{:S(2)}, u32[]{:S(2)}) collective-permute-start(f32[136,256]{1,0:T(8,128)S(1)} %merge.2.refs_0_), channel_id=1, source_target_pairs={{0,32},{4,100},{8,40},{12,108},{16,48},{20,116},{24,56},{28,124},{... | collective-permute-start | bytes 417800 | tf_op jit(solution)/shard_map/ppermute | solution.py:307
  59.1 9.3 %collective-permute-start.6 = (f32[136,256]{1,0:T(8,128)S(1)}, f32[136,256]{1,0:T(8,128)S(1)}, u32[]{:S(2)}, u32[]{:S(2)}) collective-permute-start(f32[136,256]{1,0:T(8,128)S(1)} %merge.3.refs_0_), channel_id=1, source_target_pairs={{0,96},{4,36},{8,104},{12,44},{16,112},{20,52},{24,120},{28,60},{3... | collective-permute-start | bytes 417800 | tf_op jit(solution)/shard_map/ppermute | solution.py:307
  69.4 7.5 %collective-permute-start.12 = (f32[128,256]{1,0:T(8,128)S(1)}, f32[128,256]{1,0:T(8,128)S(1)}, u32[]{:S(2)}, u32[]{:S(2)}) collective-permute-start(f32[128,256]{1,0:T(8,128)S(1)} %finish.1.refs_0_), channel_id=1, source_target_pairs={{0,24},{4,124},{8,16},{12,116},{16,8},{20,44},{24,0},{28,36},{32,5... | collective-permute-start | bytes 393224 | tf_op jit(solution)/shard_map/ppermute | solution.py:306
  69.6 11.0 %collective-permute-start.10 = (f32[128,256]{1,0:T(8,128)S(1)}, f32[128,256]{1,0:T(8,128)S(1)}, u32[]{:S(2)}, u32[]{:S(2)}) collective-permute-start(f32[128,256]{1,0:T(8,128)S(1)} %finish.1.refs_0_), channel_id=1, source_target_pairs={{0,16},{4,116},{8,24},{12,124},{16,0},{20,36},{24,8},{28,44},{32,4... | collective-permute-start | bytes 393224 | tf_op jit(solution)/shard_map/ppermute | solution.py:306
  72.0 9.1 %collective-permute-start.8 = (f32[128,256]{1,0:T(8,128)S(1)}, f32[128,256]{1,0:T(8,128)S(1)}, u32[]{:S(2)}, u32[]{:S(2)}) collective-permute-start(f32[128,256]{1,0:T(8,128)S(1)} %finish.1.refs_0_), channel_id=1, source_target_pairs={{0,8},{4,12},{8,0},{12,4},{16,24},{20,28},{24,16},{28,20},{32,40},... | collective-permute-start | bytes 393224 | tf_op jit(solution)/shard_map/ppermute | solution.py:306
  73.4 8.7 %collective-permute-start.7 = (f32[128,256]{1,0:T(8,128)S(1)}, f32[128,256]{1,0:T(8,128)S(1)}, u32[]{:S(2)}, u32[]{:S(2)}) collective-permute-start(f32[128,256]{1,0:T(8,128)S(1)} %finish.1.refs_0_), channel_id=1, source_target_pairs={{0,4},{4,0},{8,12},{12,8},{16,20},{20,16},{24,28},{28,24},{32,36},... | collective-permute-start | bytes 393224 | tf_op jit(solution)/shard_map/ppermute | solution.py:305
  76.9 5.1 %collective-permute-start.13 = (f32[128,256]{1,0:T(8,128)S(1)}, f32[128,256]{1,0:T(8,128)S(1)}, u32[]{:S(2)}, u32[]{:S(2)}) collective-permute-start(f32[128,256]{1,0:T(8,128)S(1)} %collective-permute-done.12.refs_6_), channel_id=1, source_target_pairs={{0,4},{4,0},{8,12},{12,8},{16,20},{20,16},{24,28},{28,24},{32,36},... | collective-permute-start | bytes 393224 | tf_op jit(solution)/shard_map/ppermute | solution.py:305
  80.6 1.5 %collective-permute-start.11 = (f32[128,256]{1,0:T(8,128)S(1)}, f32[128,256]{1,0:T(8,128)S(1)}, u32[]{:S(2)}, u32[]{:S(2)}) collective-permute-start(f32[128,256]{1,0:T(8,128)S(1)} %collective-permute-done.10.refs_4_), channel_id=1, source_target_pairs={{0,4},{4,0},{8,12},{12,8},{16,20},{20,16},{24,28},{28,24},{32,36},... | collective-permute-start | bytes 393224 | tf_op jit(solution)/shard_map/ppermute | solution.py:305
  81.1 1.9 %collective-permute-start.9 = (f32[128,256]{1,0:T(8,128)S(1)}, f32[128,256]{1,0:T(8,128)S(1)}, u32[]{:S(2)}, u32[]{:S(2)}) collective-permute-start(f32[128,256]{1,0:T(8,128)S(1)} %collective-permute-done.8.refs_2_), channel_id=1, source_target_pairs={{0,4},{4,0},{8,12},{12,8},{16,20},{20,16},{24,28},{28,24},{32,36},... | collective-permute-start | bytes 393224 | tf_op jit(solution)/shard_map/ppermute | solution.py:305
  84.1 5.2 %collective-permute-start.14 = (f32[128,256]{1,0:T(8,128)S(1)}, f32[128,256]{1,0:T(8,128)S(1)}, u32[]{:S(2)}, u32[]{:S(2)}) collective-permute-start(f32[128,256]{1,0:T(8,128)S(1)} %project.1), channel_id=1, source_target_pairs={{0,1},{1,0},{2,3},{3,2},{4,7},{5,6},{6,5},{7,4},{8,9},{9,8},{10,11... | collective-permute-start | bytes 393224 | tf_op jit(solution)/shard_map/ppermute | solution.py:308
  89.3 3.9 %collective-permute-start.15 = (f32[128,256]{1,0:T(8,128)S(1)}, f32[128,256]{1,0:T(8,128)S(1)}, u32[]{:S(2)}, u32[]{:S(2)}) collective-permute-start(f32[128,256]{1,0:T(8,128)S(1)} %add.16), channel_id=1, source_target_pairs={{0,3},{1,2},{2,1},{3,0},{4,5},{5,4},{6,7},{7,6},{8,11},{9,10},{10,... | collective-permute-start | bytes 393224 | tf_op jit(solution)/shard_map/ppermute | solution.py:308

commit v3 on v2

--- a/solution.py
+++ b/solution.py
@@ -30,21 +30,66 @@
     )
 
 
-def attend_kernel(scaling, order, info, q_ref, k_ref, v_ref, mine_ref, theirs_ref, s_ref, acc_ref):
-    seq = jnp.bitwise_xor(info[1], order(pl.program_id(0)))
-    core = info[2]
+def attend_kernel(scaling, order, info, q_hbm, k_hbm, v_hbm, mine_ref, theirs_ref, *scratch):
+    q_buf, k_buf, v_buf, s_ref, acc_ref, sems = scratch
+    steps = q_buf.shape[0]
+
+    def copies(i):
+        seq = jnp.bitwise_xor(info[1], order(i))
+        return [
+            pltpu.make_async_copy(hbm.at[seq], buf.at[i], sems.at[i, n])
+            for n, (hbm, buf) in enumerate(((q_hbm, q_buf), (k_hbm, k_buf), (v_hbm, v_buf)))
+        ]
+
+    def usable(i):
+        seq = jnp.bitwise_xor(info[1], order(i))
+        return jnp.clip(info[3 + seq] - info[0], 0, k_buf.shape[1] // 2)
+
+    for i in range(steps):
+
+        @pl.when(usable(i) > 0)
+        def _():
+            for copy in copies(i):
+                copy.start()
+
+    def one(i, _):
+        attend_one(
+            scaling,
+            info[2],
+            usable(i),
+            copies(i),
+            q_buf.at[i],
+            k_buf.at[i],
+            v_buf.at[i],
+            mine_ref.at[i],
+            theirs_ref.at[i],
+            s_ref,
+            acc_ref,
+        )
+        return _
+
+    lax.fori_loop(0, steps, one, 0)
+
+
+def attend_one(scaling, core, usable, copies, q_ref, k_ref, v_ref, mine_ref, theirs_ref, s_ref, acc_ref):
     rows, head_dim = k_ref.shape
     queries = q_ref.shape[1]
     per_page = 2 * page
-    usable = jnp.clip(info[3 + seq] - info[0], 0, rows // 2)
     pages = usable // page
+    some = pages > 0
     factor = scaling * math.log2(math.e)
     d2 = 2 * head_dim
 
     even_row = lax.broadcasted_iota(jnp.int32, (16, head_dim), 0) % 2 == 0
     pick_even = jnp.where(even_row, 1.0, 0.0).astype(bf16)
     pick_odd = jnp.where(even_row, 0.0, 1.0).astype(bf16)
-    qc = jnp.concatenate([q_ref[0], q_ref[1]], axis=1)
+
+    @pl.when(some)
+    def _():
+        copies[0].wait()
+        copies[1].wait()
+
+    qc = jnp.concatenate([q_ref[0].T, q_ref[1].T], axis=0)
 
     def scores(p, tile):
         k = k_ref[pl.ds(p * per_page, tile), :].reshape(tile // 16, 16, head_dim)
@@ -55,7 +100,7 @@
             ],
             axis=1,
         )
-        s = contract(wide, qc, 1, 1)
+        s = contract(wide, qc, 1, 0)
         s_ref[pl.ds(p * per_page, tile), :] = s
         return jnp.max(s.reshape(tile // 8, 8, queries), axis=0)
 
@@ -88,87 +133,51 @@
         )
         return contract(wide, w, 1, 0)
 
-    def put(acc, top0, top1):
-        a0, a1 = acc[:head_dim], acc[head_dim:d2]
-        s0 = stats(top0 * scaling, acc[d2 : d2 + 1])
-        s1 = stats(top1 * scaling, acc[d2 + 1 : d2 + 2])
-        first = core == 0
-        mine_ref[:head_dim, :] = jnp.where(first, a0, a1)
-        theirs_ref[:head_dim, :] = jnp.where(first, a1, a0)
-        mine_ref[head_dim:, :] = jnp.where(first, s0, s1)
-        theirs_ref[head_dim:, :] = jnp.where(first, s1, s0)
-
     whole = rows // per_page
-
-    @pl.when(pages == whole)
+    spans, start = [], jnp.int32(0)
+    for run in (whole, whole // 2, 1):
+        count = (pages - start) // run
+        spans.append((run, start, count))
+        start = start + count * run
+
+    def look(p, count, most):
+        for i in range(count):
+            most = jnp.maximum(most, scores(p + i, per_page))
+        return most
+
+    most = jnp.full((8, queries), -jnp.inf, f32)
+    for run, start, count in spans:
+        most = lax.fori_loop(
+            0, count, lambda i, m, run=run, start=start: look(start + i * run, run, m), most
+        )
+    top0, top1, both = tops(most)
+    acc_ref[...] = jnp.zeros_like(acc_ref)
+
+    @pl.when(some)
     def _():
-        most = scores(0, per_page)
-        for p in range(1, whole):
-            most = jnp.maximum(most, scores(p, per_page))
-        top0, top1, both = tops(most)
-        acc = weighted(0, per_page, both)
-        for p in range(1, whole):
-            acc = acc + weighted(p, per_page, both)
-        put(acc, top0, top1)
-
-    @pl.when(jnp.logical_and(pages < whole, pages > 0))
-    def _():
-        most = lax.fori_loop(
-            0,
-            pages,
-            lambda p, m: jnp.maximum(m, scores(p, per_page)),
-            jnp.full((8, queries), -jnp.inf, f32),
+        copies[2].wait()
+
+    def add(p, count):
+        acc_ref[...] += sum(weighted(p + i, per_page, both) for i in range(count))
+
+    for run, start, count in spans:
+        lax.fori_loop(
+            0, count, lambda i, _, run=run, start=start: add(start + i * run, run), None
         )
-        top0, top1, both = tops(most)
-        acc_ref[...] = jnp.zeros_like(acc_ref)
-
-        def add(p, _):
-            acc_ref[...] += weighted(p, per_page, both)
-            return _
-
-        lax.fori_loop(0, pages, add, 0)
-        put(acc_ref[...], top0, top1)
-
-    @pl.when(pages == 0)
-    def _():
-        nothing = stats(jnp.full((1, queries), very_low, f32), jnp.zeros((1, queries), f32))
-        for ref in (mine_ref, theirs_ref):
-            ref[:head_dim, :] = jnp.zeros((head_dim, queries), f32)
-            ref[head_dim:, :] = nothing
+    a0, a1 = acc_ref[:head_dim], acc_ref[head_dim:d2]
+    s0 = stats(jnp.where(some, top0 * scaling, very_low), acc_ref[d2 : d2 + 1])
+    s1 = stats(jnp.where(some, top1 * scaling, very_low), acc_ref[d2 + 1 : d2 + 2])
+    first = core == 0
+    mine_ref[:head_dim, :] = jnp.where(first, a0, a1)
+    theirs_ref[:head_dim, :] = jnp.where(first, a1, a0)
+    mine_ref[head_dim:, :] = jnp.where(first, s0, s1)
+    theirs_ref[head_dim:, :] = jnp.where(first, s1, s0)
 
 
 def attend(query, key_cache, value_cache, info, scaling, order, steps):
     _, heads, queries, head_dim = query.shape
     rows = key_cache.shape[1]
-    block = (None, head_dim + stat_rows, queries)
-    out = jax.ShapeDtypeStruct((steps, *block[1:]), f32)
-
-    def used(k, info):
-        return info[3 + jnp.bitwise_xor(info[1], order(k))] > info[0]
-
-    def of_seq(k, info):
-        first = jnp.int32(0)
-        for step in reversed(range(1, steps)):
-            first = jnp.where(used(step, info), step, first)
-        at = jnp.where(used(0, info), 0, first)
-        for step in range(1, steps):
-            at = jnp.where(jnp.logical_and(k >= step, used(step, info)), step, at)
-        return jnp.bitwise_xor(info[1], order(at)), 0, 0
-
-    spec = pltpu.PrefetchScalarGridSpec(
-        num_scalar_prefetch=1,
-        grid=(steps,),
-        in_specs=[
-            pl.BlockSpec(
-                (None, heads, queries, head_dim),
-                lambda k, info: (jnp.bitwise_xor(info[1], order(k)), 0, 0, 0),
-            ),
-            pl.BlockSpec((None, rows, head_dim), of_seq),
-            pl.BlockSpec((None, rows, head_dim), of_seq),
-        ],
-        out_specs=[pl.BlockSpec(block, lambda k, info: (k, 0, 0))] * 2,
-        scratch_shapes=[VMEM((rows, queries), f32), VMEM((2 * head_dim + 16, queries), f32)],
-    )
+    out = jax.ShapeDtypeStruct((steps, head_dim + stat_rows, queries), f32)
     cost = pl.CostEstimate(
         flops=8 * steps * rows * queries * head_dim,
         transcendentals=steps * rows * queries,
@@ -177,8 +186,17 @@
     in_hbm = [pltpu.with_memory_space_constraint(x, pltpu.HBM) for x in (query, key_cache, value_cache)]
     return pl.pallas_call(
         functools.partial(attend_kernel, scaling, order),
-        grid_spec=spec,
+        in_specs=[smem] + [pl.BlockSpec(memory_space=pltpu.HBM)] * 3,
+        out_specs=[pl.BlockSpec(memory_space=VMEM)] * 2,
         out_shape=[out, out],
+        scratch_shapes=[
+            VMEM((steps, heads, queries, head_dim), bf16),
+            VMEM((steps, rows, head_dim), bf16),
+            VMEM((steps, rows, head_dim), bf16),
+            VMEM((rows, queries), f32),
+            VMEM((2 * head_dim + 16, queries), f32),
+            pltpu.SemaphoreType.DMA((steps, 3)),
+        ],
         name="attend",
         compiler_params=limit(24),
         cost_estimate=cost,

time: 94 us -> 91.9 us (0.978)
  starting transfers between devices: 37.1 us -> 42.3 us
  Pallas kernels: 17.2 us -> 13.4 us
  waiting for transfers between devices: 38 us -> 34.4 us
    pallas_call x2, Pallas kernels: 15 us -> 11.2 us  [attend(): pl.pallas_call(functools.partial(attend_kernel, scaling, order), in_specs...]
    ppermute x6, starting transfers between devices: 7.68 us -> 10.9 us  [step(): to_near = lambda x, k: lax.ppermute(x, 'ctx', near_pairs[k])]
    ppermute x2, waiting for transfers between devices: 18.6 us -> 16 us  [step(): to_far = lambda x, t: lax.ppermute(x, 'ctx', far_pairs[t])]
    ppermute x6, starting transfers between devices: 28.9 us -> 30.6 us  [step(): swap = lambda x: lax.ppermute(x, 'ctx', core_pairs)]
  transfers between devices with their start and end apart: 16 -> 16, of which waited for: 12 -> 11; matrix products, arithmetic and copies ran while one was open for 0% -> 0% of each run, Pallas kernels for 0% -> 0%
where the time goes in v3:
time: 91.9 us; the launch traced here: 91.7 us
  starting transfers between devices  42.3 us (46%)
  waiting for transfers between devices  34.4 us (37%)
  Pallas kernels  13.4 us (15%)
  other arithmetic  1.42 us (2%)
    ppermute x6, starting transfers between devices, step(): swap = lambda x: lax.ppermute(x, 'ctx', core_pairs)  30.6 us
    ppermute x2, waiting for transfers between devices, step(): to_far = lambda x, t: lax.ppermute(x, 'ctx', far_pairs[t])  16 us
    pallas_call x2, Pallas kernels, attend(): pl.pallas_call(functools.partial(attend_kernel, scaling, order), in_specs...  11.2 us
    ppermute x6, starting transfers between devices, step(): to_near = lambda x, k: lax.ppermute(x, 'ctx', near_pairs[k])  10.9 us
    ppermute x2, waiting for transfers between devices, step(): to_head = lambda x, t: lax.ppermute(x, ('ctx', 'head'), head_pairs[t])  8.61 us
    ppermute x6, waiting for transfers between devices, step(): to_near = lambda x, k: lax.ppermute(x, 'ctx', near_pairs[k])  6.45 us
    ppermute x6, waiting for transfers between devices, step(): swap = lambda x: lax.ppermute(x, 'ctx', core_pairs)  3.38 us
  transfers between devices with their start and end apart: 16, of which 11 were waited for; matrix products, arithmetic and copies ran while one was open for 0% of the time, Pallas kernels for 0%

profile of v3, /device:TPU:33, one launch (start us, length us, event | category | flops | bytes accessed | tf_op | source)
XLA Modules:
  0.0 91.7 jit_solution(15428473946846576039)
XLA Ops:
  0.0 0.7 pad_add_fusion.info
  0.7 5.6 %attend.2 = (f32[2,136,256]{2,1,0:T(8,128)S(1)}, f32[2,136,256]{2,1,0:T(8,128)S(1)}) custom-call(s32[7]{0:T(128)S(1)} %pad_add_fusion.info, bf16[4,2,256,128]{3,2,1,0:T(8,128)(2,1)} %bitcast.7, bf16[4,4096,128]{2,1,0:T(8,128)(2,1)} %bitcast.10, bf16[4,4096,128]{2,1,0:T(8,128)(2,1)} %bitcast.12), custom_call_target="tpu_custom_call" | custom-call | flops 2147483648 | bytes 4194304 | tf_op jit(solution)/shard_map/attend/pallas_call | solution.py:187
  6.3 20.5 %collective-permute-start = (f32[2,136,256]{2,1,0:T(8,128)S(1)}, f32[2,136,256]{2,1,0:T(8,128)S(1)}, u32[]{:S(2)}, u32[]{:S(2)}) collective-permute-start(f32[2,136,256]{2,1,0:T(8,128)S(1)} %get-tuple-element.19), channel_id=1, source_target_pairs={{0,4},{4,0},{8,12},{12,8},{16,20},{20,16},{24,28},{28,24},{32,36},... | collective-permute-start | bytes 835592 | tf_op jit(solution)/shard_map/ppermute | solution.py:323
  26.9 1.2 %collective-permute-done.got_ref = f32[2,136,256]{2,1,0:T(8,128)S(1)} collective-permute-done((f32[2,136,256]{2,1,0:T(8,128)S(1)}, f32[2,136,256]{2,1,0:T(8,128)S(1)}, u32[]{:S(2)}, u32[]{:S(2)}) %collective-permute-start) | collective-permute-done | bytes 278560 | tf_op jit(solution)/shard_map/ppermute | solution.py:323
  28.1 0.1 merge_core.2
  28.1 0.0 copy-start
  28.1 0.0 copy-start.2
  28.2 0.0 copy-start.3
  28.2 0.0 copy-start.1
  28.2 5.6 %attend.3 = (f32[2,136,256]{2,1,0:T(8,128)S(1)}, f32[2,136,256]{2,1,0:T(8,128)S(1)}) custom-call(s32[7]{0:T(128)S(1)} %pad_add_fusion.info, bf16[4,2,256,128]{3,2,1,0:T(8,128)(2,1)} %bitcast.8, bf16[4,4096,128]{2,1,0:T(8,128)(2,1)} %bitcast.11, bf16[4,4096,128]{2,1,0:T(8,128)(2,1)} %bitcast.13), custom_call_target="tpu_custom_call" | custom-call | flops 2147483648 | bytes 4194304 | tf_op jit(solution)/shard_map/attend/pallas_call | solution.py:187
  33.8 0.5 collective-permute-start.1
  34.3 0.0 collective-permute-start.3
  34.3 0.0 collective-permute-start.4
  34.3 1.2 %collective-permute-done.1.got_ref = f32[2,136,256]{2,1,0:T(8,128)S(1)} collective-permute-done((f32[2,136,256]{2,1,0:T(8,128)S(1)}, f32[2,136,256]{2,1,0:T(8,128)S(1)}, u32[]{:S(2)}, u32[]{:S(2)}) %collective-permute-start.1) | collective-permute-done | bytes 278560 | tf_op jit(solution)/shard_map/ppermute | solution.py:323
  35.5 0.1 merge_core.3
  35.5 3.7 %collective-permute-start.2 = (f32[136,256]{1,0:T(8,128)S(1)}, f32[136,256]{1,0:T(8,128)S(1)}, u32[]{:S(2)}, u32[]{:S(2)}) collective-permute-start(f32[136,256]{1,0:T(8,128)S(1)} %get-tuple-element.28), channel_id=1, source_target_pairs={{0,8},{4,12},{8,0},{12,4},{16,24},{20,28},{24,16},{28,20},{32,40},... | collective-permute-start | bytes 417800 | tf_op jit(solution)/shard_map/ppermute | solution.py:324
  39.2 2.1 %collective-permute-done.3.refs_2_ = f32[136,256]{1,0:T(8,128)S(1)} collective-permute-done((f32[136,256]{1,0:T(8,128)S(1)}, f32[136,256]{1,0:T(8,128)S(1)}, u32[]{:S(2)}, u32[]{:S(2)}) %collective-permute-start.3) | collective-permute-done | bytes 139296 | tf_op jit(solution)/shard_map/ppermute | solution.py:324
  41.3 0.0 collective-permute-done.4.refs_3_
  41.3 4.4 %collective-permute-done.2.refs_1_ = f32[136,256]{1,0:T(8,128)S(1)} collective-permute-done((f32[136,256]{1,0:T(8,128)S(1)}, f32[136,256]{1,0:T(8,128)S(1)}, u32[]{:S(2)}, u32[]{:S(2)}) %collective-permute-start.2) | collective-permute-done | bytes 139296 | tf_op jit(solution)/shard_map/ppermute | solution.py:324
  45.7 0.1 merge.2.refs_0_
  45.7 0.1 collective-permute-start.5
  45.9 8.1 %collective-permute-done.5.refs_1_ = f32[136,256]{1,0:T(8,128)S(1)} collective-permute-done((f32[136,256]{1,0:T(8,128)S(1)}, f32[136,256]{1,0:T(8,128)S(1)}, u32[]{:S(2)}, u32[]{:S(2)}) %collective-permute-start.5) | collective-permute-done | bytes 139296 | tf_op jit(solution)/shard_map/ppermute | solution.py:325
  54.0 0.1 collective-permute-start.6
  54.2 7.9 %collective-permute-done.6.refs_1_ = f32[136,256]{1,0:T(8,128)S(1)} collective-permute-done((f32[136,256]{1,0:T(8,128)S(1)}, f32[136,256]{1,0:T(8,128)S(1)}, u32[]{:S(2)}, u32[]{:S(2)}) %collective-permute-start.6) | collective-permute-done | bytes 139296 | tf_op jit(solution)/shard_map/ppermute | solution.py:325
  62.1 0.0 copy-done
  62.1 0.0 copy-done.2
  62.1 0.0 copy-done.3
  62.1 1.0 %finish.1.refs_0_ = f32[128,256]{1,0:T(8,128)S(1)} custom-call(s32[7]{0:T(128)S(1)} %pad_add_fusion.info, f32[136,256]{1,0:T(8,128)S(1)} %merge.3.refs_0_, f32[136,256]{1,0:T(8,128)S(1)} %collective-permute-done.6.refs_1_, bf16[4,2,256,128]{3,2,1,0:T(8,128)(2,1)S(1)} %bitcast.9, bf16[4,2,32,128]{3,2,1,0:T(8,128)(2,1)S(1)} %copy-done.2, ...), custom_call_target="tpu_custom_call" | custom-call | tf_op jit(solution)/shard_map/finish/pallas_call | solution.py:370
  63.1 4.8 %collective-permute-start.12 = (f32[128,256]{1,0:T(8,128)S(1)}, f32[128,256]{1,0:T(8,128)S(1)}, u32[]{:S(2)}, u32[]{:S(2)}) collective-permute-start(f32[128,256]{1,0:T(8,128)S(1)} %finish.1.refs_0_), channel_id=1, source_target_pairs={{0,24},{4,124},{8,16},{12,116},{16,8},{20,44},{24,0},{28,36},{32,5... | collective-permute-start | bytes 393224 | tf_op jit(solution)/shard_map/ppermute | solution.py:324
  67.9 2.4 %collective-permute-start.10 = (f32[128,256]{1,0:T(8,128)S(1)}, f32[128,256]{1,0:T(8,128)S(1)}, u32[]{:S(2)}, u32[]{:S(2)}) collective-permute-start(f32[128,256]{1,0:T(8,128)S(1)} %finish.1.refs_0_), channel_id=1, source_target_pairs={{0,16},{4,116},{8,24},{12,124},{16,0},{20,36},{24,8},{28,44},{32,4... | collective-permute-start | bytes 393224 | tf_op jit(solution)/shard_map/ppermute | solution.py:324
  70.3 0.0 collective-permute-start.8
  70.3 3.6 %collective-permute-start.7 = (f32[128,256]{1,0:T(8,128)S(1)}, f32[128,256]{1,0:T(8,128)S(1)}, u32[]{:S(2)}, u32[]{:S(2)}) collective-permute-start(f32[128,256]{1,0:T(8,128)S(1)} %finish.1.refs_0_), channel_id=1, source_target_pairs={{0,4},{4,0},{8,12},{12,8},{16,20},{20,16},{24,28},{28,24},{32,36},... | collective-permute-start | bytes 393224 | tf_op jit(solution)/shard_map/ppermute | solution.py:323
  73.9 0.0 collective-permute-done.12.refs_6_
  73.9 5.5 %collective-permute-start.13 = (f32[128,256]{1,0:T(8,128)S(1)}, f32[128,256]{1,0:T(8,128)S(1)}, u32[]{:S(2)}, u32[]{:S(2)}) collective-permute-start(f32[128,256]{1,0:T(8,128)S(1)} %collective-permute-done.12.refs_6_), channel_id=1, source_target_pairs={{0,4},{4,0},{8,12},{12,8},{16,20},{20,16},{24,28},{28,24},{32,36},... | collective-permute-start | bytes 393224 | tf_op jit(solution)/shard_map/ppermute | solution.py:323
  79.3 0.0 collective-permute-done.10.refs_4_
  79.3 0.0 collective-permute-start.11
  79.4 0.0 collective-permute-done.8.refs_2_
  79.4 0.5 collective-permute-start.9
  79.9 0.0 collective-permute-done.7.refs_1_
  79.9 0.5 collective-permute-done.13.refs_7_
  80.3 0.4 collective-permute-done.11.refs_5_
  80.7 0.2 collective-permute-done.9.refs_3_
  80.9 0.0 copy-done.1
  80.9 1.1 %project.1 = f32[128,256]{1,0:T(8,128)S(1)} custom-call(s32[7]{0:T(128)S(1)} %pad_add_fusion.info, f32[128,256]{1,0:T(8,128)S(1)} %finish.1.refs_0_, f32[128,256]{1,0:T(8,128)S(1)} %collective-permute-done.7.refs_1_, f32[128,256]{1,0:T(8,128)S(1)} %collective-permute-done.8.refs_2_, f32[128,256]{1,0:T(8,128)S(1)} %collective-permute-done.9.refs_3_, ...), custom_call_target="tpu_custom_call" | custom-call | tf_op jit(solution)/shard_map/project/pallas_call | solution.py:383
  81.9 0.3 collective-permute-start.14
  82.3 4.8 %collective-permute-done.14 = f32[128,256]{1,0:T(8,128)S(1)} collective-permute-done((f32[128,256]{1,0:T(8,128)S(1)}, f32[128,256]{1,0:T(8,128)S(1)}, u32[]{:S(2)}, u32[]{:S(2)}) %collective-permute-start.14) | collective-permute-done | bytes 131104 | tf_op jit(solution)/shard_map/ppermute | solution.py:326
  87.1 0.1 collective-permute-start.15
  87.3 3.8 %collective-permute-done.15 = f32[128,256]{1,0:T(8,128)S(1)} collective-permute-done((f32[128,256]{1,0:T(8,128)S(1)}, f32[128,256]{1,0:T(8,128)S(1)}, u32[]{:S(2)}, u32[]{:S(2)}) %collective-permute-start.15) | collective-permute-done | bytes 131104 | tf_op jit(solution)/shard_map/ppermute | solution.py:326
  91.1 0.7 add.17
  (2 shorter events, 0.0 us)
Async XLA Ops:
  6.3 21.7 %collective-permute-start = (f32[2,136,256]{2,1,0:T(8,128)S(1)}, f32[2,136,256]{2,1,0:T(8,128)S(1)}, u32[]{:S(2)}, u32[]{:S(2)}) collective-permute-start(f32[2,136,256]{2,1,0:T(8,128)S(1)} %get-tuple-element.19), channel_id=1, source_target_pairs={{0,4},{4,0},{8,12},{12,8},{16,20},{20,16},{24,28},{28,24},{32,36},... | collective-permute-start | bytes 835592 | tf_op jit(solution)/shard_map/ppermute | solution.py:323
  28.1 33.9 %copy-start = (bf16[4,16,32,128]{3,2,1,0:T(8,128)(2,1)S(1)}, bf16[4,16,32,128]{3,2,1,0:T(8,128)(2,1)}, u32[]{:S(2)}) copy-start(bf16[4,16,32,128]{3,2,1,0:T(8,128)(2,1)} %param.7) | copy-start | bytes 1572868
  28.1 33.9 %copy-start.2 = (bf16[4,2,32,128]{3,2,1,0:T(8,128)(2,1)S(1)}, bf16[4,2,32,128]{3,2,1,0:T(8,128)(2,1)}, u32[]{:S(2)}) copy-start(bf16[4,2,32,128]{3,2,1,0:T(8,128)(2,1)} %refs_3_.1) | copy-start | bytes 196612
  28.2 33.9 %copy-start.3 = (bf16[4,2,32,128]{3,2,1,0:T(8,128)(2,1)S(1)}, bf16[4,2,32,128]{3,2,1,0:T(8,128)(2,1)}, u32[]{:S(2)}) copy-start(bf16[4,2,32,128]{3,2,1,0:T(8,128)(2,1)} %refs_4_.1) | copy-start | bytes 196612
  28.2 52.7 %copy-start.1 = (bf16[2048,256]{1,0:T(8,128)(2,1)S(1)}, bf16[2048,256]{1,0:T(8,128)(2,1)}, u32[]{:S(2)}) copy-start(bf16[2048,256]{1,0:T(8,128)(2,1)} %refs_8_.1) | copy-start | bytes 3145732
  33.8 1.7 %collective-permute-start.1 = (f32[2,136,256]{2,1,0:T(8,128)S(1)}, f32[2,136,256]{2,1,0:T(8,128)S(1)}, u32[]{:S(2)}, u32[]{:S(2)}) collective-permute-start(f32[2,136,256]{2,1,0:T(8,128)S(1)} %get-tuple-element.24), channel_id=1, source_target_pairs={{0,4},{4,0},{8,12},{12,8},{16,20},{20,16},{24,28},{28,24},{32,36},... | collective-permute-start | bytes 835592 | tf_op jit(solution)/shard_map/ppermute | solution.py:323
  34.3 7.0 %collective-permute-start.3 = (f32[136,256]{1,0:T(8,128)S(1)}, f32[136,256]{1,0:T(8,128)S(1)}, u32[]{:S(2)}, u32[]{:S(2)}) collective-permute-start(f32[136,256]{1,0:T(8,128)S(1)} %get-tuple-element.29), channel_id=1, source_target_pairs={{0,16},{4,116},{8,24},{12,124},{16,0},{20,36},{24,8},{28,44},{32,4... | collective-permute-start | bytes 417800 | tf_op jit(solution)/shard_map/ppermute | solution.py:324
  34.3 7.0 %collective-permute-start.4 = (f32[136,256]{1,0:T(8,128)S(1)}, f32[136,256]{1,0:T(8,128)S(1)}, u32[]{:S(2)}, u32[]{:S(2)}) collective-permute-start(f32[136,256]{1,0:T(8,128)S(1)} %get-tuple-element.30), channel_id=1, source_target_pairs={{0,24},{4,124},{8,16},{12,116},{16,8},{20,44},{24,0},{28,36},{32,5... | collective-permute-start | bytes 417800 | tf_op jit(solution)/shard_map/ppermute | solution.py:324
  35.5 10.1 %collective-permute-start.2 = (f32[136,256]{1,0:T(8,128)S(1)}, f32[136,256]{1,0:T(8,128)S(1)}, u32[]{:S(2)}, u32[]{:S(2)}) collective-permute-start(f32[136,256]{1,0:T(8,128)S(1)} %get-tuple-element.28), channel_id=1, source_target_pairs={{0,8},{4,12},{8,0},{12,4},{16,24},{20,28},{24,16},{28,20},{32,40},... | collective-permute-start | bytes 417800 | tf_op jit(solution)/shard_map/ppermute | solution.py:324
  45.7 8.2 %collective-permute-start.5 = (f32[136,256]{1,0:T(8,128)S(1)}, f32[136,256]{1,0:T(8,128)S(1)}, u32[]{:S(2)}, u32[]{:S(2)}) collective-permute-start(f32[136,256]{1,0:T(8,128)S(1)} %merge.2.refs_0_), channel_id=1, source_target_pairs={{0,32},{4,100},{8,40},{12,108},{16,48},{20,116},{24,56},{28,124},{... | collective-permute-start | bytes 417800 | tf_op jit(solution)/shard_map/ppermute | solution.py:325
  54.0 8.0 %collective-permute-start.6 = (f32[136,256]{1,0:T(8,128)S(1)}, f32[136,256]{1,0:T(8,128)S(1)}, u32[]{:S(2)}, u32[]{:S(2)}) collective-permute-start(f32[136,256]{1,0:T(8,128)S(1)} %merge.3.refs_0_), channel_id=1, source_target_pairs={{0,96},{4,36},{8,104},{12,44},{16,112},{20,52},{24,120},{28,60},{3... | collective-permute-start | bytes 417800 | tf_op jit(solution)/shard_map/ppermute | solution.py:325
  63.1 10.8 %collective-permute-start.12 = (f32[128,256]{1,0:T(8,128)S(1)}, f32[128,256]{1,0:T(8,128)S(1)}, u32[]{:S(2)}, u32[]{:S(2)}) collective-permute-start(f32[128,256]{1,0:T(8,128)S(1)} %finish.1.refs_0_), channel_id=1, source_target_pairs={{0,24},{4,124},{8,16},{12,116},{16,8},{20,44},{24,0},{28,36},{32,5... | collective-permute-start | bytes 393224 | tf_op jit(solution)/shard_map/ppermute | solution.py:324
  67.9 11.5 %collective-permute-start.10 = (f32[128,256]{1,0:T(8,128)S(1)}, f32[128,256]{1,0:T(8,128)S(1)}, u32[]{:S(2)}, u32[]{:S(2)}) collective-permute-start(f32[128,256]{1,0:T(8,128)S(1)} %finish.1.refs_0_), channel_id=1, source_target_pairs={{0,16},{4,116},{8,24},{12,124},{16,0},{20,36},{24,8},{28,44},{32,4... | collective-permute-start | bytes 393224 | tf_op jit(solution)/shard_map/ppermute | solution.py:324
  70.3 9.1 %collective-permute-start.8 = (f32[128,256]{1,0:T(8,128)S(1)}, f32[128,256]{1,0:T(8,128)S(1)}, u32[]{:S(2)}, u32[]{:S(2)}) collective-permute-start(f32[128,256]{1,0:T(8,128)S(1)} %finish.1.refs_0_), channel_id=1, source_target_pairs={{0,8},{4,12},{8,0},{12,4},{16,24},{20,28},{24,16},{28,20},{32,40},... | collective-permute-start | bytes 393224 | tf_op jit(solution)/shard_map/ppermute | solution.py:324
  70.3 9.6 %collective-permute-start.7 = (f32[128,256]{1,0:T(8,128)S(1)}, f32[128,256]{1,0:T(8,128)S(1)}, u32[]{:S(2)}, u32[]{:S(2)}) collective-permute-start(f32[128,256]{1,0:T(8,128)S(1)} %finish.1.refs_0_), channel_id=1, source_target_pairs={{0,4},{4,0},{8,12},{12,8},{16,20},{20,16},{24,28},{28,24},{32,36},... | collective-permute-start | bytes 393224 | tf_op jit(solution)/shard_map/ppermute | solution.py:323
  73.9 6.5 %collective-permute-start.13 = (f32[128,256]{1,0:T(8,128)S(1)}, f32[128,256]{1,0:T(8,128)S(1)}, u32[]{:S(2)}, u32[]{:S(2)}) collective-permute-start(f32[128,256]{1,0:T(8,128)S(1)} %collective-permute-done.12.refs_6_), channel_id=1, source_target_pairs={{0,4},{4,0},{8,12},{12,8},{16,20},{20,16},{24,28},{28,24},{32,36},... | collective-permute-start | bytes 393224 | tf_op jit(solution)/shard_map/ppermute | solution.py:323
  79.3 1.3 %collective-permute-start.11 = (f32[128,256]{1,0:T(8,128)S(1)}, f32[128,256]{1,0:T(8,128)S(1)}, u32[]{:S(2)}, u32[]{:S(2)}) collective-permute-start(f32[128,256]{1,0:T(8,128)S(1)} %collective-permute-done.10.refs_4_), channel_id=1, source_target_pairs={{0,4},{4,0},{8,12},{12,8},{16,20},{20,16},{24,28},{28,24},{32,36},... | collective-permute-start | bytes 393224 | tf_op jit(solution)/shard_map/ppermute | solution.py:323
  79.4 1.5 %collective-permute-start.9 = (f32[128,256]{1,0:T(8,128)S(1)}, f32[128,256]{1,0:T(8,128)S(1)}, u32[]{:S(2)}, u32[]{:S(2)}) collective-permute-start(f32[128,256]{1,0:T(8,128)S(1)} %collective-permute-done.8.refs_2_), channel_id=1, source_target_pairs={{0,4},{4,0},{8,12},{12,8},{16,20},{20,16},{24,28},{28,24},{32,36},... | collective-permute-start | bytes 393224 | tf_op jit(solution)/shard_map/ppermute | solution.py:323
  81.9 5.2 %collective-permute-start.14 = (f32[128,256]{1,0:T(8,128)S(1)}, f32[128,256]{1,0:T(8,128)S(1)}, u32[]{:S(2)}, u32[]{:S(2)}) collective-permute-start(f32[128,256]{1,0:T(8,128)S(1)} %project.1), channel_id=1, source_target_pairs={{0,1},{1,0},{2,3},{3,2},{4,7},{5,6},{6,5},{7,4},{8,9},{9,8},{10,11... | collective-permute-start | bytes 393224 | tf_op jit(solution)/shard_map/ppermute | solution.py:326
  87.1 3.9 %collective-permute-start.15 = (f32[128,256]{1,0:T(8,128)S(1)}, f32[128,256]{1,0:T(8,128)S(1)}, u32[]{:S(2)}, u32[]{:S(2)}) collective-permute-start(f32[128,256]{1,0:T(8,128)S(1)} %add.16), channel_id=1, source_target_pairs={{0,3},{1,2},{2,1},{3,0},{4,5},{5,4},{6,7},{7,6},{8,11},{9,10},{10,... | collective-permute-start | bytes 393224 | tf_op jit(solution)/shard_map/ppermute | solution.py:326

commit v4 on v3

--- a/solution.py
+++ b/solution.py
@@ -35,14 +35,14 @@
     steps = q_buf.shape[0]
 
     def copies(i):
-        seq = jnp.bitwise_xor(info[1], order(i))
+        seq = lax.rem(info[1] + order(i), radix)
         return [
             pltpu.make_async_copy(hbm.at[seq], buf.at[i], sems.at[i, n])
             for n, (hbm, buf) in enumerate(((q_hbm, q_buf), (k_hbm, k_buf), (v_hbm, v_buf)))
         ]
 
     def usable(i):
-        seq = jnp.bitwise_xor(info[1], order(i))
+        seq = lax.rem(info[1] + order(i), radix)
         return jnp.clip(info[3 + seq] - info[0], 0, k_buf.shape[1] // 2)
 
     for i in range(steps):
@@ -228,21 +228,24 @@
     out[depth:, :] = stats(top, total)
 
 
-def finish_kernel(scaling, draft, info, *refs):
-    parts, (q_ref, key_ref, value_ref), out = refs[:-4], refs[-4:-1], refs[-1]
-    depth = parts[0].shape[0] - stat_rows
-    numer, top, total = merged([p[...] for p in parts], depth)
+def own_kernel(scaling, draft, info, q_ref, key_ref, value_ref, out):
+    depth = out.shape[0] - stat_rows
     own = contract(key_ref[info[1], info[2]], q_ref[info[1], info[2]], 1, 1) * scaling
     at = lax.broadcasted_iota(jnp.int32, own.shape, 0)
     row = lax.broadcasted_iota(jnp.int32, own.shape, 1) % draft
     causal = at <= row
     own = jnp.where(causal, own, very_low)
-    overall = jnp.maximum(top, jnp.max(own, axis=0, keepdims=True))
-    carried = jnp.exp(top - overall)
-    fresh = jnp.where(causal, jnp.exp(own - overall), 0.0)
-    denominator = total * carried + jnp.sum(fresh, axis=0, keepdims=True)
-    added = contract(value_ref[info[1], info[2]].astype(f32), fresh, 0, 0, lax.Precision.HIGHEST)
-    out[...] = ((numer * carried + added) / denominator).astype(bf16).astype(f32)
+    top = jnp.max(own, axis=0, keepdims=True)
+    fresh = jnp.where(causal, jnp.exp(own - top), 0.0)
+    values = value_ref[info[1], info[2]].astype(f32)
+    out[:depth, :] = contract(values, fresh, 0, 0, lax.Precision.HIGHEST)
+    out[depth:, :] = stats(top, jnp.sum(fresh, axis=0, keepdims=True))
+
+
+def finish_kernel(*refs):
+    parts, out = refs[:-1], refs[-1]
+    numer, _, total = merged([p[...] for p in parts], out.shape[0])
+    out[...] = (numer / total).astype(bf16).astype(f32)
 
 
 def project_kernel(draft, info, *refs):
@@ -251,7 +254,7 @@
     for i, piece in enumerate(pieces):
         k, other = i // 2, i % 2
         g = jnp.bitwise_xor(info[2], other)
-        seq = jnp.bitwise_xor(info[1], k)
+        seq = lax.rem(info[1] + k, radix)
         at = pl.ds(pl.multiple_of(seq * draft, draft), draft)
         depth, queries = piece.shape
         for a in range(queries // depth):
@@ -282,25 +285,18 @@
     chips = n_ctx // 2
     far = chips // radix
 
-    def place(z, c):
-        return (z - c * (radix // 2)) % chips // radix, z % radix
-
-    def chip(b, j, c):
-        shift = c * (radix // 2)
-        return (b * radix + shift + (j - shift) % radix) % chips
-
-    def pairs(k):
+    def near_to(k):
         out = []
         for i in range(n_ctx):
             z, c = divmod(i, 2)
-            b, j = place(z, c)
-            out.append((i, 2 * chip(b, j ^ k, c) + c))
+            step = {0: 0, 1: 1, 2: 2 - 4 * c, 3: -1}[k]
+            out.append((i, 2 * ((z + step) % chips) + c))
         return out
 
     def partner(i, n, turn):
         return i ^ 1 if turn == 0 else (((i + 1) % n) ^ 1) - 1 if ((i + 1) % n) ^ 1 else n - 1
 
-    near_pairs = [pairs(k) for k in range(radix)]
+    near_pairs = [near_to(k) for k in range(radix)]
     far_pairs = [
         [
             (i, 2 * (partner(z // radix, far, t ^ c) * radix + z % radix) + c)
@@ -327,31 +323,32 @@
 
     index = lax.axis_index("ctx")
     core = index % 2
-    spot = place(index // 2, core)[1]
+    spot = index // 2 % radix
     info = jnp.concatenate([jnp.stack([index * ctx_len, spot, core]).astype(jnp.int32), lengths])
 
     grouped = query.reshape(seqs, heads, queries, head_dim)
     keys = key_cache.reshape(seqs, ctx_len * heads, head_dim)
     values = value_cache.reshape(seqs, ctx_len * heads, head_dim)
     chunk = jax.ShapeDtypeStruct((head_dim + stat_rows, queries), f32)
-    half_seqs = seqs // 2
     gate = info
     chunks = {}
-    for half in range(2):
-        order = lambda k, half=half: seqs - 1 - half * half_seqs - k
-        mine, theirs = attend(grouped, keys, values, gate, scaling, order, half_seqs)
+    for steps in ((2, 1, 3), (0,)):
+        order = lambda i, steps=steps: functools.reduce(
+            lambda at, n: jnp.where(i == n, steps[n], at), range(1, len(steps)), jnp.int32(steps[0])
+        )
+        mine, theirs = attend(grouped, keys, values, gate, scaling, order, len(steps))
         got = swap(theirs)
         found = pl.pallas_call(
             merge_core_kernel,
             in_specs=whole_vmem(2),
-            out_specs=whole_vmem(half_seqs),
-            out_shape=[chunk] * half_seqs,
+            out_specs=whole_vmem(len(steps)),
+            out_shape=[chunk] * len(steps),
             name="merge_core",
             compiler_params=limit(8),
         )(mine, got)
         gate, *found = lax.optimization_barrier((info, *found))
-        for k, x in enumerate(found):
-            chunks[order(k)] = to_near(x, order(k)) if order(k) else x
+        for k, x in zip(steps, found):
+            chunks[k] = to_near(x, k) if k else x
     chunks = [chunks[k] for k in range(radix)]
 
     def merge(parts):
@@ -366,16 +363,24 @@
 
     found = merge(chunks)
     found = merge([found, to_far(found, 0)])
-    parts = [found, to_far(found, 1)]
+    own = pl.pallas_call(
+        functools.partial(own_kernel, scaling, draft),
+        in_specs=[smem] + whole_vmem(3),
+        out_specs=pl.BlockSpec(memory_space=VMEM),
+        out_shape=chunk,
+        name="own",
+        compiler_params=limit(4),
+    )(info, grouped, new_key, new_value)
+    parts = [found, to_far(found, 1), own]
     att = pl.pallas_call(
-        functools.partial(finish_kernel, scaling, draft),
-        in_specs=[smem] + whole_vmem(5),
+        finish_kernel,
+        in_specs=whole_vmem(len(parts)),
         out_specs=pl.BlockSpec(memory_space=VMEM),
         out_shape=jax.ShapeDtypeStruct((head_dim, queries), f32),
         name="finish",
         compiler_params=limit(4),
-    )(info, *parts, grouped, new_key, new_value)
-    near = [att] + [to_near(att, k) for k in range(1, radix)]
+    )(*parts)
+    near = [att] + [to_near(att, radix - k) for k in range(1, radix)]
     pieces = []
     for part in near:
         pieces += [part, swap(part)]

time: 91.9 us -> 89.8 us (0.977)
  starting transfers between devices: 42.3 us -> 40.9 us
    ppermute x6, starting transfers between devices: 10.9 us -> 9.16 us  [step(): to_near = lambda x, k: lax.ppermute(x, 'ctx', near_pairs[k])]
    ppermute x6, waiting for transfers between devices: 3.38 us -> 2.37 us  [step(): swap = lambda x: lax.ppermute(x, 'ctx', core_pairs)]
  transfers between devices with their start and end apart: 16 -> 16, of which waited for: 11 -> 8; matrix products, arithmetic and copies ran while one was open for 0% -> 0% of each run, Pallas kernels for 0% -> 1%
where the time goes in v4:
time: 89.8 us; the launch traced here: 89.7 us
  starting transfers between devices  40.9 us (46%)
  waiting for transfers between devices  33.7 us (38%)
  Pallas kernels  13.5 us (15%)
  other arithmetic  1.42 us (2%)
    ppermute x6, starting transfers between devices, step(): swap = lambda x: lax.ppermute(x, 'ctx', core_pairs)  31.2 us
    ppermute x2, waiting for transfers between devices, step(): to_far = lambda x, t: lax.ppermute(x, 'ctx', far_pairs[t])  15.9 us
    pallas_call x2, Pallas kernels, attend(): pl.pallas_call(functools.partial(attend_kernel, scaling, order), in_specs...  11.2 us
    ppermute x6, starting transfers between devices, step(): to_near = lambda x, k: lax.ppermute(x, 'ctx', near_pairs[k])  9.16 us
    ppermute x2, waiting for transfers between devices, step(): to_head = lambda x, t: lax.ppermute(x, ('ctx', 'head'), head_pairs[t])  8.79 us
    ppermute x6, waiting for transfers between devices, step(): to_near = lambda x, k: lax.ppermute(x, 'ctx', near_pairs[k])  6.55 us
    ppermute x6, waiting for transfers between devices, step(): swap = lambda x: lax.ppermute(x, 'ctx', core_pairs)  2.37 us
  transfers between devices with their start and end apart: 16, of which 8 were waited for; matrix products, arithmetic and copies ran while one was open for 0% of the time, Pallas kernels for 1%

profile of v4, /device:TPU:33, one launch (start us, length us, event | category | flops | bytes accessed | tf_op | source)
XLA Modules:
  0.0 89.7 jit_solution(1124945290053465383)
XLA Ops:
  0.0 0.7 pad_add_fusion.info
  0.7 7.5 %attend.2 = (f32[3,136,256]{2,1,0:T(8,128)S(1)}, f32[3,136,256]{2,1,0:T(8,128)S(1)}) custom-call(s32[7]{0:T(128)S(1)} %pad_add_fusion.info, bf16[4,2,256,128]{3,2,1,0:T(8,128)(2,1)} %bitcast.7, bf16[4,4096,128]{2,1,0:T(8,128)(2,1)} %bitcast.10, bf16[4,4096,128]{2,1,0:T(8,128)(2,1)} %bitcast.12), custom_call_target="tpu_custom_call" | custom-call | flops 3221225472 | bytes 6291456 | tf_op jit(solution)/shard_map/attend/pallas_call | solution.py:187
  8.2 20.5 %collective-permute-start = (f32[3,136,256]{2,1,0:T(8,128)S(1)}, f32[3,136,256]{2,1,0:T(8,128)S(1)}, u32[]{:S(2)}, u32[]{:S(2)}) collective-permute-start(f32[3,136,256]{2,1,0:T(8,128)S(1)} %get-tuple-element.18), channel_id=1, source_target_pairs={{0,4},{4,0},{8,12},{12,8},{16,20},{20,16},{24,28},{28,24},{32,36},... | collective-permute-start | bytes 1253384 | tf_op jit(solution)/shard_map/ppermute | solution.py:319
  28.8 1.4 %collective-permute-done.got_ref = f32[3,136,256]{2,1,0:T(8,128)S(1)} collective-permute-done((f32[3,136,256]{2,1,0:T(8,128)S(1)}, f32[3,136,256]{2,1,0:T(8,128)S(1)}, u32[]{:S(2)}, u32[]{:S(2)}) %collective-permute-start) | collective-permute-done | bytes 417824 | tf_op jit(solution)/shard_map/ppermute | solution.py:319
  30.2 0.1 merge_core.2
  30.2 0.0 copy-start
  30.3 0.0 copy-start.2
  30.3 0.0 copy-start.3
  30.3 0.0 copy-start.1
  30.3 3.7 %attend.3 = (f32[1,136,256]{2,1,0:T(8,128)S(1)}, f32[1,136,256]{2,1,0:T(8,128)S(1)}) custom-call(s32[7]{0:T(128)S(1)} %pad_add_fusion.info, bf16[4,2,256,128]{3,2,1,0:T(8,128)(2,1)} %bitcast.8, bf16[4,4096,128]{2,1,0:T(8,128)(2,1)} %bitcast.11, bf16[4,4096,128]{2,1,0:T(8,128)(2,1)} %bitcast.13), custom_call_target="tpu_custom_call" | custom-call | flops 1073741824 | bytes 2097152 | tf_op jit(solution)/shard_map/attend/pallas_call | solution.py:187
  34.0 0.5 collective-permute-start.1
  34.5 0.0 collective-permute-start.2
  34.5 0.0 collective-permute-start.3
  34.5 2.7 %collective-permute-start.4 = (f32[136,256]{1,0:T(8,128)S(1)}, f32[136,256]{1,0:T(8,128)S(1)}, u32[]{:S(2)}, u32[]{:S(2)}) collective-permute-start(f32[136,256]{1,0:T(8,128)S(1)} %get-tuple-element.28), channel_id=1, source_target_pairs={{0,120},{4,124},{8,0},{12,4},{16,8},{20,12},{24,16},{28,20},{32,24... | collective-permute-start | bytes 417800 | tf_op jit(solution)/shard_map/ppermute | solution.py:320
  37.2 0.0 collective-permute-done.1.got_ref
  37.2 5.0 %collective-permute-done.2.refs_1_ = f32[136,256]{1,0:T(8,128)S(1)} collective-permute-done((f32[136,256]{1,0:T(8,128)S(1)}, f32[136,256]{1,0:T(8,128)S(1)}, u32[]{:S(2)}, u32[]{:S(2)}) %collective-permute-start.2) | collective-permute-done | bytes 139296 | tf_op jit(solution)/shard_map/ppermute | solution.py:320
  42.2 0.0 collective-permute-done.3.refs_2_
  42.2 1.6 %collective-permute-done.4.refs_3_ = f32[136,256]{1,0:T(8,128)S(1)} collective-permute-done((f32[136,256]{1,0:T(8,128)S(1)}, f32[136,256]{1,0:T(8,128)S(1)}, u32[]{:S(2)}, u32[]{:S(2)}) %collective-permute-start.4) | collective-permute-done | bytes 139296 | tf_op jit(solution)/shard_map/ppermute | solution.py:320
  43.8 0.1 merge.2.refs_0_
  43.9 0.1 collective-permute-start.5
  44.0 8.1 %collective-permute-done.5.refs_1_ = f32[136,256]{1,0:T(8,128)S(1)} collective-permute-done((f32[136,256]{1,0:T(8,128)S(1)}, f32[136,256]{1,0:T(8,128)S(1)}, u32[]{:S(2)}, u32[]{:S(2)}) %collective-permute-start.5) | collective-permute-done | bytes 139296 | tf_op jit(solution)/shard_map/ppermute | solution.py:321
  52.1 0.1 collective-permute-start.6
  52.3 0.0 copy-done
  52.3 0.0 copy-done.2
  52.3 0.0 copy-done.3
  52.3 1.0 %own.1.refs_2_ = f32[136,256]{1,0:T(8,128)S(1)} custom-call(s32[7]{0:T(128)S(1)} %pad_add_fusion.info, bf16[4,2,256,128]{3,2,1,0:T(8,128)(2,1)S(1)} %bitcast.9, bf16[4,2,32,128]{3,2,1,0:T(8,128)(2,1)S(1)} %copy-done.2, bf16[4,2,32,128]{3,2,1,0:T(8,128)(2,1)S(1)} %copy-done.3), custom_call_target="tpu_custom_call" | custom-call | tf_op jit(solution)/shard_map/own/pallas_call | solution.py:366
  53.3 7.9 %collective-permute-done.6.refs_1_ = f32[136,256]{1,0:T(8,128)S(1)} collective-permute-done((f32[136,256]{1,0:T(8,128)S(1)}, f32[136,256]{1,0:T(8,128)S(1)}, u32[]{:S(2)}, u32[]{:S(2)}) %collective-permute-start.6) | collective-permute-done | bytes 139296 | tf_op jit(solution)/shard_map/ppermute | solution.py:321
  61.1 0.1 finish.1.refs_0_
  61.2 5.2 %collective-permute-start.8 = (f32[128,256]{1,0:T(8,128)S(1)}, f32[128,256]{1,0:T(8,128)S(1)}, u32[]{:S(2)}, u32[]{:S(2)}) collective-permute-start(f32[128,256]{1,0:T(8,128)S(1)} %finish.1.refs_0_), channel_id=1, source_target_pairs={{0,120},{4,124},{8,0},{12,4},{16,8},{20,12},{24,16},{28,20},{32,24... | collective-permute-start | bytes 393224 | tf_op jit(solution)/shard_map/ppermute | solution.py:320
  66.4 0.0 collective-permute-start.10
  66.4 1.3 %collective-permute-start.12 = (f32[128,256]{1,0:T(8,128)S(1)}, f32[128,256]{1,0:T(8,128)S(1)}, u32[]{:S(2)}, u32[]{:S(2)}) collective-permute-start(f32[128,256]{1,0:T(8,128)S(1)} %finish.1.refs_0_), channel_id=1, source_target_pairs={{0,8},{4,12},{8,16},{12,20},{16,24},{20,28},{24,32},{28,36},{32,40... | collective-permute-start | bytes 393224 | tf_op jit(solution)/shard_map/ppermute | solution.py:320
  67.7 2.7 %collective-permute-start.7 = (f32[128,256]{1,0:T(8,128)S(1)}, f32[128,256]{1,0:T(8,128)S(1)}, u32[]{:S(2)}, u32[]{:S(2)}) collective-permute-start(f32[128,256]{1,0:T(8,128)S(1)} %finish.1.refs_0_), channel_id=1, source_target_pairs={{0,4},{4,0},{8,12},{12,8},{16,20},{20,16},{24,28},{28,24},{32,36},... | collective-permute-start | bytes 393224 | tf_op jit(solution)/shard_map/ppermute | solution.py:319
  70.3 0.0 collective-permute-done.8.refs_2_
  70.3 3.2 %collective-permute-start.9 = (f32[128,256]{1,0:T(8,128)S(1)}, f32[128,256]{1,0:T(8,128)S(1)}, u32[]{:S(2)}, u32[]{:S(2)}) collective-permute-start(f32[128,256]{1,0:T(8,128)S(1)} %collective-permute-done.8.refs_2_), channel_id=1, source_target_pairs={{0,4},{4,0},{8,12},{12,8},{16,20},{20,16},{24,28},{28,24},{32,36},... | collective-permute-start | bytes 393224 | tf_op jit(solution)/shard_map/ppermute | solution.py:319
  73.6 0.0 collective-permute-done.10.refs_4_
  73.6 3.0 %collective-permute-start.11 = (f32[128,256]{1,0:T(8,128)S(1)}, f32[128,256]{1,0:T(8,128)S(1)}, u32[]{:S(2)}, u32[]{:S(2)}) collective-permute-start(f32[128,256]{1,0:T(8,128)S(1)} %collective-permute-done.10.refs_4_), channel_id=1, source_target_pairs={{0,4},{4,0},{8,12},{12,8},{16,20},{20,16},{24,28},{28,24},{32,36},... | collective-permute-start | bytes 393224 | tf_op jit(solution)/shard_map/ppermute | solution.py:319
  76.6 0.0 collective-permute-done.12.refs_6_
  76.6 1.3 %collective-permute-start.13 = (f32[128,256]{1,0:T(8,128)S(1)}, f32[128,256]{1,0:T(8,128)S(1)}, u32[]{:S(2)}, u32[]{:S(2)}) collective-permute-start(f32[128,256]{1,0:T(8,128)S(1)} %collective-permute-done.12.refs_6_), channel_id=1, source_target_pairs={{0,4},{4,0},{8,12},{12,8},{16,20},{20,16},{24,28},{28,24},{32,36},... | collective-permute-start | bytes 393224 | tf_op jit(solution)/shard_map/ppermute | solution.py:319
  77.8 0.0 collective-permute-done.7.refs_1_
  77.8 0.0 collective-permute-done.9.refs_3_
  77.8 0.0 collective-permute-done.11.refs_5_
  77.9 1.0 %collective-permute-done.13.refs_7_ = f32[128,256]{1,0:T(8,128)S(1)} collective-permute-done((f32[128,256]{1,0:T(8,128)S(1)}, f32[128,256]{1,0:T(8,128)S(1)}, u32[]{:S(2)}, u32[]{:S(2)}) %collective-permute-start.13) | collective-permute-done | bytes 131104 | tf_op jit(solution)/shard_map/ppermute | solution.py:319
  78.8 0.0 copy-done.1
  78.8 1.1 %project.1 = f32[128,256]{1,0:T(8,128)S(1)} custom-call(s32[7]{0:T(128)S(1)} %pad_add_fusion.info, f32[128,256]{1,0:T(8,128)S(1)} %finish.1.refs_0_, f32[128,256]{1,0:T(8,128)S(1)} %collective-permute-done.7.refs_1_, f32[128,256]{1,0:T(8,128)S(1)} %collective-permute-done.8.refs_2_, f32[128,256]{1,0:T(8,128)S(1)} %collective-permute-done.9.refs_3_, ...), custom_call_target="tpu_custom_call" | custom-call | tf_op jit(solution)/shard_map/project/pallas_call | solution.py:388
  79.9 0.1 collective-permute-start.14
  80.0 5.0 %collective-permute-done.14 = f32[128,256]{1,0:T(8,128)S(1)} collective-permute-done((f32[128,256]{1,0:T(8,128)S(1)}, f32[128,256]{1,0:T(8,128)S(1)}, u32[]{:S(2)}, u32[]{:S(2)}) %collective-permute-start.14) | collective-permute-done | bytes 131104 | tf_op jit(solution)/shard_map/ppermute | solution.py:322
  85.1 0.1 collective-permute-start.15
  85.2 3.8 %collective-permute-done.15 = f32[128,256]{1,0:T(8,128)S(1)} collective-permute-done((f32[128,256]{1,0:T(8,128)S(1)}, f32[128,256]{1,0:T(8,128)S(1)}, u32[]{:S(2)}, u32[]{:S(2)}) %collective-permute-start.15) | collective-permute-done | bytes 131104 | tf_op jit(solution)/shard_map/ppermute | solution.py:322
  89.0 0.7 add.17
  (3 shorter events, 0.1 us)
Async XLA Ops:
  8.2 21.9 %collective-permute-start = (f32[3,136,256]{2,1,0:T(8,128)S(1)}, f32[3,136,256]{2,1,0:T(8,128)S(1)}, u32[]{:S(2)}, u32[]{:S(2)}) collective-permute-start(f32[3,136,256]{2,1,0:T(8,128)S(1)} %get-tuple-element.18), channel_id=1, source_target_pairs={{0,4},{4,0},{8,12},{12,8},{16,20},{20,16},{24,28},{28,24},{32,36},... | collective-permute-start | bytes 1253384 | tf_op jit(solution)/shard_map/ppermute | solution.py:319
  30.2 22.0 %copy-start = (bf16[4,16,32,128]{3,2,1,0:T(8,128)(2,1)S(1)}, bf16[4,16,32,128]{3,2,1,0:T(8,128)(2,1)}, u32[]{:S(2)}) copy-start(bf16[4,16,32,128]{3,2,1,0:T(8,128)(2,1)} %param.7) | copy-start | bytes 1572868
  30.3 22.0 %copy-start.2 = (bf16[4,2,32,128]{3,2,1,0:T(8,128)(2,1)S(1)}, bf16[4,2,32,128]{3,2,1,0:T(8,128)(2,1)}, u32[]{:S(2)}) copy-start(bf16[4,2,32,128]{3,2,1,0:T(8,128)(2,1)} %key_ref.1) | copy-start | bytes 196612
  30.3 22.0 %copy-start.3 = (bf16[4,2,32,128]{3,2,1,0:T(8,128)(2,1)S(1)}, bf16[4,2,32,128]{3,2,1,0:T(8,128)(2,1)}, u32[]{:S(2)}) copy-start(bf16[4,2,32,128]{3,2,1,0:T(8,128)(2,1)} %value_ref.1) | copy-start | bytes 196612
  30.3 48.5 %copy-start.1 = (bf16[2048,256]{1,0:T(8,128)(2,1)S(1)}, bf16[2048,256]{1,0:T(8,128)(2,1)}, u32[]{:S(2)}) copy-start(bf16[2048,256]{1,0:T(8,128)(2,1)} %refs_8_.1) | copy-start | bytes 3145732
  34.0 3.2 %collective-permute-start.1 = (f32[1,136,256]{2,1,0:T(8,128)S(1)}, f32[1,136,256]{2,1,0:T(8,128)S(1)}, u32[]{:S(2)}, u32[]{:S(2)}) collective-permute-start(f32[1,136,256]{2,1,0:T(8,128)S(1)} %get-tuple-element.24), channel_id=1, source_target_pairs={{0,4},{4,0},{8,12},{12,8},{16,20},{20,16},{24,28},{28,24},{32,36},... | collective-permute-start | bytes 417800 | tf_op jit(solution)/shard_map/ppermute | solution.py:319
  34.5 7.7 %collective-permute-start.2 = (f32[136,256]{1,0:T(8,128)S(1)}, f32[136,256]{1,0:T(8,128)S(1)}, u32[]{:S(2)}, u32[]{:S(2)}) collective-permute-start(f32[136,256]{1,0:T(8,128)S(1)} %get-tuple-element.26), channel_id=1, source_target_pairs={{0,8},{4,12},{8,16},{12,20},{16,24},{20,28},{24,32},{28,36},{32,40... | collective-permute-start | bytes 417800 | tf_op jit(solution)/shard_map/ppermute | solution.py:320
  34.5 7.7 %collective-permute-start.3 = (f32[136,256]{1,0:T(8,128)S(1)}, f32[136,256]{1,0:T(8,128)S(1)}, u32[]{:S(2)}, u32[]{:S(2)}) collective-permute-start(f32[136,256]{1,0:T(8,128)S(1)} %get-tuple-element.27), channel_id=1, source_target_pairs={{0,16},{4,116},{8,24},{12,124},{16,32},{20,4},{24,40},{28,12},{32,... | collective-permute-start | bytes 417800 | tf_op jit(solution)/shard_map/ppermute | solution.py:320
  34.5 9.3 %collective-permute-start.4 = (f32[136,256]{1,0:T(8,128)S(1)}, f32[136,256]{1,0:T(8,128)S(1)}, u32[]{:S(2)}, u32[]{:S(2)}) collective-permute-start(f32[136,256]{1,0:T(8,128)S(1)} %get-tuple-element.28), channel_id=1, source_target_pairs={{0,120},{4,124},{8,0},{12,4},{16,8},{20,12},{24,16},{28,20},{32,24... | collective-permute-start | bytes 417800 | tf_op jit(solution)/shard_map/ppermute | solution.py:320
  43.9 8.2 %collective-permute-start.5 = (f32[136,256]{1,0:T(8,128)S(1)}, f32[136,256]{1,0:T(8,128)S(1)}, u32[]{:S(2)}, u32[]{:S(2)}) collective-permute-start(f32[136,256]{1,0:T(8,128)S(1)} %merge.2.refs_0_), channel_id=1, source_target_pairs={{0,32},{4,100},{8,40},{12,108},{16,48},{20,116},{24,56},{28,124},{... | collective-permute-start | bytes 417800 | tf_op jit(solution)/shard_map/ppermute | solution.py:321
  52.1 9.0 %collective-permute-start.6 = (f32[136,256]{1,0:T(8,128)S(1)}, f32[136,256]{1,0:T(8,128)S(1)}, u32[]{:S(2)}, u32[]{:S(2)}) collective-permute-start(f32[136,256]{1,0:T(8,128)S(1)} %merge.3.refs_0_), channel_id=1, source_target_pairs={{0,96},{4,36},{8,104},{12,44},{16,112},{20,52},{24,120},{28,60},{3... | collective-permute-start | bytes 417800 | tf_op jit(solution)/shard_map/ppermute | solution.py:321
  61.2 9.1 %collective-permute-start.8 = (f32[128,256]{1,0:T(8,128)S(1)}, f32[128,256]{1,0:T(8,128)S(1)}, u32[]{:S(2)}, u32[]{:S(2)}) collective-permute-start(f32[128,256]{1,0:T(8,128)S(1)} %finish.1.refs_0_), channel_id=1, source_target_pairs={{0,120},{4,124},{8,0},{12,4},{16,8},{20,12},{24,16},{28,20},{32,24... | collective-permute-start | bytes 393224 | tf_op jit(solution)/shard_map/ppermute | solution.py:320
  66.4 7.2 %collective-permute-start.10 = (f32[128,256]{1,0:T(8,128)S(1)}, f32[128,256]{1,0:T(8,128)S(1)}, u32[]{:S(2)}, u32[]{:S(2)}) collective-permute-start(f32[128,256]{1,0:T(8,128)S(1)} %finish.1.refs_0_), channel_id=1, source_target_pairs={{0,16},{4,116},{8,24},{12,124},{16,32},{20,4},{24,40},{28,12},{32,... | collective-permute-start | bytes 393224 | tf_op jit(solution)/shard_map/ppermute | solution.py:320
  66.4 10.2 %collective-permute-start.12 = (f32[128,256]{1,0:T(8,128)S(1)}, f32[128,256]{1,0:T(8,128)S(1)}, u32[]{:S(2)}, u32[]{:S(2)}) collective-permute-start(f32[128,256]{1,0:T(8,128)S(1)} %finish.1.refs_0_), channel_id=1, source_target_pairs={{0,8},{4,12},{8,16},{12,20},{16,24},{20,28},{24,32},{28,36},{32,40... | collective-permute-start | bytes 393224 | tf_op jit(solution)/shard_map/ppermute | solution.py:320
  67.7 10.2 %collective-permute-start.7 = (f32[128,256]{1,0:T(8,128)S(1)}, f32[128,256]{1,0:T(8,128)S(1)}, u32[]{:S(2)}, u32[]{:S(2)}) collective-permute-start(f32[128,256]{1,0:T(8,128)S(1)} %finish.1.refs_0_), channel_id=1, source_target_pairs={{0,4},{4,0},{8,12},{12,8},{16,20},{20,16},{24,28},{28,24},{32,36},... | collective-permute-start | bytes 393224 | tf_op jit(solution)/shard_map/ppermute | solution.py:319
  70.3 7.5 %collective-permute-start.9 = (f32[128,256]{1,0:T(8,128)S(1)}, f32[128,256]{1,0:T(8,128)S(1)}, u32[]{:S(2)}, u32[]{:S(2)}) collective-permute-start(f32[128,256]{1,0:T(8,128)S(1)} %collective-permute-done.8.refs_2_), channel_id=1, source_target_pairs={{0,4},{4,0},{8,12},{12,8},{16,20},{20,16},{24,28},{28,24},{32,36},... | collective-permute-start | bytes 393224 | tf_op jit(solution)/shard_map/ppermute | solution.py:319
  73.6 4.3 %collective-permute-start.11 = (f32[128,256]{1,0:T(8,128)S(1)}, f32[128,256]{1,0:T(8,128)S(1)}, u32[]{:S(2)}, u32[]{:S(2)}) collective-permute-start(f32[128,256]{1,0:T(8,128)S(1)} %collective-permute-done.10.refs_4_), channel_id=1, source_target_pairs={{0,4},{4,0},{8,12},{12,8},{16,20},{20,16},{24,28},{28,24},{32,36},... | collective-permute-start | bytes 393224 | tf_op jit(solution)/shard_map/ppermute | solution.py:319
  76.6 2.3 %collective-permute-start.13 = (f32[128,256]{1,0:T(8,128)S(1)}, f32[128,256]{1,0:T(8,128)S(1)}, u32[]{:S(2)}, u32[]{:S(2)}) collective-permute-start(f32[128,256]{1,0:T(8,128)S(1)} %collective-permute-done.12.refs_6_), channel_id=1, source_target_pairs={{0,4},{4,0},{8,12},{12,8},{16,20},{20,16},{24,28},{28,24},{32,36},... | collective-permute-start | bytes 393224 | tf_op jit(solution)/shard_map/ppermute | solution.py:319
  79.9 5.2 %collective-permute-start.14 = (f32[128,256]{1,0:T(8,128)S(1)}, f32[128,256]{1,0:T(8,128)S(1)}, u32[]{:S(2)}, u32[]{:S(2)}) collective-permute-start(f32[128,256]{1,0:T(8,128)S(1)} %project.1), channel_id=1, source_target_pairs={{0,1},{1,0},{2,3},{3,2},{4,7},{5,6},{6,5},{7,4},{8,9},{9,8},{10,11... | collective-permute-start | bytes 393224 | tf_op jit(solution)/shard_map/ppermute | solution.py:322
  85.1 3.9 %collective-permute-start.15 = (f32[128,256]{1,0:T(8,128)S(1)}, f32[128,256]{1,0:T(8,128)S(1)}, u32[]{:S(2)}, u32[]{:S(2)}) collective-permute-start(f32[128,256]{1,0:T(8,128)S(1)} %add.16), channel_id=1, source_target_pairs={{0,3},{1,2},{2,1},{3,0},{4,5},{5,4},{6,7},{7,6},{8,11},{9,10},{10,... | collective-permute-start | bytes 393224 | tf_op jit(solution)/shard_map/ppermute | solution.py:322

commit v5 on v4

--- a/solution.py
+++ b/solution.py
@@ -30,45 +30,61 @@
     )
 
 
-def attend_kernel(scaling, order, info, q_hbm, k_hbm, v_hbm, mine_ref, theirs_ref, *scratch):
-    q_buf, k_buf, v_buf, s_ref, acc_ref, sems = scratch
+def attend_kernel(scaling, order, ahead, info, q_hbm, k_hbm, v_hbm, *refs):
+    n_out = 2 + 3 * ahead
+    mine_ref, theirs_ref, *next_refs = refs[:n_out]
+    q_buf, k_buf, v_buf, s_ref, acc_ref, sems = refs[n_out:]
     steps = q_buf.shape[0]
 
-    def copies(i):
-        seq = lax.rem(info[1] + order(i), radix)
+    def usable(seq):
+        return jnp.clip(info[3 + seq] - info[0], 0, k_buf.shape[1] // 2)
+
+    def seq_of(i):
+        return lax.rem(info[1] + order(i), radix)
+
+    def copies(i, seq, bufs):
         return [
-            pltpu.make_async_copy(hbm.at[seq], buf.at[i], sems.at[i, n])
-            for n, (hbm, buf) in enumerate(((q_hbm, q_buf), (k_hbm, k_buf), (v_hbm, v_buf)))
+            pltpu.make_async_copy(hbm.at[seq], buf, sems.at[i, n])
+            for n, (hbm, buf) in enumerate(zip((q_hbm, k_hbm, v_hbm), bufs))
         ]
 
-    def usable(i):
-        seq = lax.rem(info[1] + order(i), radix)
-        return jnp.clip(info[3 + seq] - info[0], 0, k_buf.shape[1] // 2)
+    def slot(i):
+        return copies(i, seq_of(i), (q_buf.at[i], k_buf.at[i], v_buf.at[i]))
 
     for i in range(steps):
 
-        @pl.when(usable(i) > 0)
+        @pl.when(usable(seq_of(i)) > 0)
         def _():
-            for copy in copies(i):
+            for copy in slot(i):
                 copy.start()
 
+    if ahead:
+        later = copies(steps, info[1], next_refs)
+
+        @pl.when(usable(info[1]) > 0)
+        def _():
+            for copy in later:
+                copy.start()
+
     def one(i, _):
-        attend_one(
-            scaling,
-            info[2],
-            usable(i),
-            copies(i),
-            q_buf.at[i],
-            k_buf.at[i],
-            v_buf.at[i],
-            mine_ref.at[i],
-            theirs_ref.at[i],
-            s_ref,
-            acc_ref,
-        )
+        count = usable(seq_of(i))
+        refs = (q_buf.at[i], k_buf.at[i], v_buf.at[i], mine_ref.at[i], theirs_ref.at[i])
+        attend_one(scaling, info[2], count, slot(i), *refs, s_ref, acc_ref)
         return _
 
     lax.fori_loop(0, steps, one, 0)
+    if ahead:
+
+        @pl.when(usable(info[1]) > 0)
+        def _():
+            for copy in later:
+                copy.wait()
+
+
+def attend_last_kernel(scaling, info, q_ref, k_ref, v_ref, mine_ref, theirs_ref, s_ref, acc_ref):
+    count = jnp.clip(info[3 + info[1]] - info[0], 0, k_ref.shape[0] // 2)
+    refs = (q_ref, k_ref, v_ref, mine_ref.at[0], theirs_ref.at[0])
+    attend_one(scaling, info[2], count, None, *refs, s_ref, acc_ref)
 
 
 def attend_one(scaling, core, usable, copies, q_ref, k_ref, v_ref, mine_ref, theirs_ref, s_ref, acc_ref):
@@ -84,10 +100,12 @@
     pick_even = jnp.where(even_row, 1.0, 0.0).astype(bf16)
     pick_odd = jnp.where(even_row, 0.0, 1.0).astype(bf16)
 
-    @pl.when(some)
-    def _():
-        copies[0].wait()
-        copies[1].wait()
+    if copies:
+
+        @pl.when(some)
+        def _():
+            copies[0].wait()
+            copies[1].wait()
 
     qc = jnp.concatenate([q_ref[0].T, q_ref[1].T], axis=0)
 
@@ -153,9 +171,11 @@
     top0, top1, both = tops(most)
     acc_ref[...] = jnp.zeros_like(acc_ref)
 
-    @pl.when(some)
-    def _():
-        copies[2].wait()
+    if copies:
+
+        @pl.when(some)
+        def _():
+            copies[2].wait()
 
     def add(p, count):
         acc_ref[...] += sum(weighted(p + i, per_page, both) for i in range(count))
@@ -174,33 +194,61 @@
     theirs_ref[head_dim:, :] = jnp.where(first, s1, s0)
 
 
-def attend(query, key_cache, value_cache, info, scaling, order, steps):
+def attend(query, key_cache, value_cache, info, scaling, steps):
     _, heads, queries, head_dim = query.shape
     rows = key_cache.shape[1]
-    out = jax.ShapeDtypeStruct((steps, head_dim + stat_rows, queries), f32)
-    cost = pl.CostEstimate(
-        flops=8 * steps * rows * queries * head_dim,
-        transcendentals=steps * rows * queries,
-        bytes_accessed=4 * steps * rows * head_dim,
-    )
+    block = (head_dim + stat_rows, queries)
+    work = [VMEM((rows, queries), f32), VMEM((2 * head_dim + 16, queries), f32)]
+
+    def cost(n):
+        return pl.CostEstimate(
+            flops=8 * n * rows * queries * head_dim,
+            transcendentals=n * rows * queries,
+            bytes_accessed=4 * n * rows * head_dim,
+        )
+
+    def outs(n):
+        return [jax.ShapeDtypeStruct((n, *block), f32)] * 2
+
+    def order(i):
+        at = jnp.int32(steps[0])
+        for n, k in enumerate(steps):
+            at = jnp.where(i == n, k, at)
+        return at
+
+    n = len(steps)
     in_hbm = [pltpu.with_memory_space_constraint(x, pltpu.HBM) for x in (query, key_cache, value_cache)]
-    return pl.pallas_call(
-        functools.partial(attend_kernel, scaling, order),
+    *most, q, k, v = pl.pallas_call(
+        functools.partial(attend_kernel, scaling, order, True),
         in_specs=[smem] + [pl.BlockSpec(memory_space=pltpu.HBM)] * 3,
-        out_specs=[pl.BlockSpec(memory_space=VMEM)] * 2,
-        out_shape=[out, out],
+        out_specs=whole_vmem(5),
+        out_shape=outs(n)
+        + [jax.ShapeDtypeStruct(x.shape[1:], x.dtype) for x in (query, key_cache, value_cache)],
         scratch_shapes=[
-            VMEM((steps, heads, queries, head_dim), bf16),
-            VMEM((steps, rows, head_dim), bf16),
-            VMEM((steps, rows, head_dim), bf16),
-            VMEM((rows, queries), f32),
-            VMEM((2 * head_dim + 16, queries), f32),
-            pltpu.SemaphoreType.DMA((steps, 3)),
+            VMEM((n, heads, queries, head_dim), bf16),
+            VMEM((n, rows, head_dim), bf16),
+            VMEM((n, rows, head_dim), bf16),
+            *work,
+            pltpu.SemaphoreType.DMA((n + 1, 3)),
         ],
         name="attend",
-        compiler_params=limit(24),
-        cost_estimate=cost,
+        compiler_params=limit(26),
+        cost_estimate=cost(n),
     )(info, *in_hbm)
+
+    def last(info):
+        return pl.pallas_call(
+            functools.partial(attend_last_kernel, scaling),
+            in_specs=[smem] + whole_vmem(3),
+            out_specs=whole_vmem(2),
+            out_shape=outs(1),
+            scratch_shapes=work,
+            name="attend_last",
+            compiler_params=limit(16),
+            cost_estimate=cost(1),
+        )(info, q, k, v)
+
+    return most, last
 
 
 def merged(parts, depth):
@@ -220,16 +268,20 @@
         out[depth:, :] = stats(top, total)
 
 
-def merge_kernel(*refs):
-    parts, out = refs[:-1], refs[-1]
-    depth = out.shape[0] - stat_rows
-    numer, top, total = merged([p[...] for p in parts], depth)
-    out[:depth, :] = numer
-    out[depth:, :] = stats(top, total)
-
-
-def own_kernel(scaling, draft, info, q_ref, key_ref, value_ref, out):
-    depth = out.shape[0] - stat_rows
+def put_halves(outs, numer, top, total):
+    depth, lanes = numer.shape[0], outs[0].shape[1]
+    for n, out in enumerate(outs):
+        at = slice(n * lanes, (n + 1) * lanes)
+        out[:depth, :] = numer[:, at]
+        out[depth:, :] = stats(top[:, at], total[:, at])
+
+
+def merge_kernel(n_out, *refs):
+    parts, outs = refs[:-n_out], refs[-n_out:]
+    put_halves(outs, *merged([p[...] for p in parts], outs[0].shape[0] - stat_rows))
+
+
+def own_kernel(scaling, draft, info, q_ref, key_ref, value_ref, *outs):
     own = contract(key_ref[info[1], info[2]], q_ref[info[1], info[2]], 1, 1) * scaling
     at = lax.broadcasted_iota(jnp.int32, own.shape, 0)
     row = lax.broadcasted_iota(jnp.int32, own.shape, 1) % draft
@@ -238,8 +290,8 @@
     top = jnp.max(own, axis=0, keepdims=True)
     fresh = jnp.where(causal, jnp.exp(own - top), 0.0)
     values = value_ref[info[1], info[2]].astype(f32)
-    out[:depth, :] = contract(values, fresh, 0, 0, lax.Precision.HIGHEST)
-    out[depth:, :] = stats(top, jnp.sum(fresh, axis=0, keepdims=True))
+    numer = contract(values, fresh, 0, 0, lax.Precision.HIGHEST)
+    put_halves(outs, numer, top, jnp.sum(fresh, axis=0, keepdims=True))
 
 
 def finish_kernel(*refs):
@@ -248,21 +300,25 @@
     out[...] = (numer / total).astype(bf16).astype(f32)
 
 
-def project_kernel(draft, info, *refs):
-    pieces, (w_ref, out_ref, x_ref) = refs[:-3], refs[-3:]
+def project_kernel(draft, half, info, *refs):
+    n = 2 * radix
+    pieces, extra, (w_ref, out_ref, x_ref) = refs[:n], refs[n:-3], refs[-3:]
     width = x_ref.shape[2]
     for i, piece in enumerate(pieces):
         k, other = i // 2, i % 2
         g = jnp.bitwise_xor(info[2], other)
         seq = lax.rem(info[1] + k, radix)
         at = pl.ds(pl.multiple_of(seq * draft, draft), draft)
-        depth, queries = piece.shape
-        for a in range(queries // depth):
-            att = piece[:, a * depth : (a + 1) * depth].T.astype(bf16)
-            for h in range(depth // draft):
-                col = (a * (depth // draft) + h) * depth
-                x_ref[g, at, col : col + depth] = att[h * draft : (h + 1) * draft]
-    out_ref[...] = sum(contract(x_ref[g], w_ref[g * width : (g + 1) * width, :], 1, 0) for g in range(2))
+        depth, lanes = piece.shape
+        att = piece[...].T.astype(bf16)
+        for h in range(lanes // draft):
+            x_ref[g, at, h * depth : (h + 1) * depth] = att[h * draft : (h + 1) * draft]
+    whole = w_ref.shape[0] // 2
+    products = [
+        contract(x_ref[g], w_ref[g * whole + half * width : g * whole + (half + 1) * width, :], 1, 0)
+        for g in range(2)
+    ]
+    out_ref[...] = sum(products + [e[...] for e in extra])
 
 
 def whole_vmem(n):
@@ -330,70 +386,77 @@
     keys = key_cache.reshape(seqs, ctx_len * heads, head_dim)
     values = value_cache.reshape(seqs, ctx_len * heads, head_dim)
     chunk = jax.ShapeDtypeStruct((head_dim + stat_rows, queries), f32)
+    steps = (2, 1, 3)
+    pair, last = attend(grouped, keys, values, info, scaling, steps)
+    chunks = {}
     gate = info
-    chunks = {}
-    for steps in ((2, 1, 3), (0,)):
-        order = lambda i, steps=steps: functools.reduce(
-            lambda at, n: jnp.where(i == n, steps[n], at), range(1, len(steps)), jnp.int32(steps[0])
-        )
-        mine, theirs = attend(grouped, keys, values, gate, scaling, order, len(steps))
+    for call, seqs_of in enumerate((steps, (0,))):
+        mine, theirs = pair if call == 0 else last(gate)
         got = swap(theirs)
         found = pl.pallas_call(
             merge_core_kernel,
             in_specs=whole_vmem(2),
-            out_specs=whole_vmem(len(steps)),
-            out_shape=[chunk] * len(steps),
+            out_specs=whole_vmem(len(seqs_of)),
+            out_shape=[chunk] * len(seqs_of),
             name="merge_core",
             compiler_params=limit(8),
         )(mine, got)
         gate, *found = lax.optimization_barrier((info, *found))
-        for k, x in zip(steps, found):
+        for k, x in zip(seqs_of, found):
             chunks[k] = to_near(x, k) if k else x
     chunks = [chunks[k] for k in range(radix)]
-
-    def merge(parts):
+    half_chunk = jax.ShapeDtypeStruct((head_dim + stat_rows, queries // 2), f32)
+
+    def merge(parts, n_out):
         return pl.pallas_call(
-            merge_kernel,
+            functools.partial(merge_kernel, n_out),
             in_specs=whole_vmem(len(parts)),
-            out_specs=pl.BlockSpec(memory_space=VMEM),
-            out_shape=chunk,
+            out_specs=whole_vmem(n_out),
+            out_shape=[half_chunk] * n_out,
             name="merge",
             compiler_params=limit(4),
         )(*parts)
 
-    found = merge(chunks)
-    found = merge([found, to_far(found, 0)])
+    found = merge(chunks, 2)
     own = pl.pallas_call(
         functools.partial(own_kernel, scaling, draft),
         in_specs=[smem] + whole_vmem(3),
-        out_specs=pl.BlockSpec(memory_space=VMEM),
-        out_shape=chunk,
+        out_specs=whole_vmem(2),
+        out_shape=[half_chunk] * 2,
         name="own",
         compiler_params=limit(4),
     )(info, grouped, new_key, new_value)
-    parts = [found, to_far(found, 1), own]
-    att = pl.pallas_call(
-        finish_kernel,
-        in_specs=whole_vmem(len(parts)),
-        out_specs=pl.BlockSpec(memory_space=VMEM),
-        out_shape=jax.ShapeDtypeStruct((head_dim, queries), f32),
-        name="finish",
-        compiler_params=limit(4),
-    )(*parts)
-    near = [att] + [to_near(att, radix - k) for k in range(1, radix)]
-    pieces = []
-    for part in near:
-        pieces += [part, swap(part)]
     width = out_weight.shape[1]
-    out = pl.pallas_call(
-        functools.partial(project_kernel, draft),
-        in_specs=[smem] + whole_vmem(len(pieces) + 1),
-        out_specs=pl.BlockSpec(memory_space=VMEM),
-        out_shape=jax.ShapeDtypeStruct((seqs * draft, width), f32),
-        scratch_shapes=[VMEM((heads, seqs * draft, out_weight.shape[0] // heads), bf16)],
-        name="project",
-        compiler_params=limit(8),
-    )(info, *pieces, out_weight)
+    found = [merge([x, to_far(x, 0)], 1)[0] for x in found]
+    out = []
+    for n, x in enumerate(found):
+        parts = [x, to_far(x, 1), own[n]]
+        att = pl.pallas_call(
+            finish_kernel,
+            in_specs=whole_vmem(len(parts)),
+            out_specs=pl.BlockSpec(memory_space=VMEM),
+            out_shape=jax.ShapeDtypeStruct((head_dim, queries // 2), f32),
+            name="finish",
+            compiler_params=limit(4),
+        )(*parts)
+        near = [att] + [to_near(att, radix - k) for k in range(1, radix)]
+        pieces = []
+        for part in near:
+            pieces += [part, swap(part)]
+        out = [
+            pl.pallas_call(
+                functools.partial(project_kernel, draft, n),
+                in_specs=[smem] + whole_vmem(len(pieces) + len(out) + 1),
+                out_specs=pl.BlockSpec(memory_space=VMEM),
+                out_shape=jax.ShapeDtypeStruct((seqs * draft, width), f32),
+                scratch_shapes=[
+                    VMEM((heads, seqs * draft, out_weight.shape[0] // heads // 2), bf16)
+                ],
+                name="project",
+                compiler_params=limit(8),
+            )(info, *pieces, *out, out_weight)
+        ]
+    out = out[0]
     for t in range(2):
         out = out + to_head(out, t)
     return out.reshape(seqs, draft, width)

time: 89.8 us -> 88.8 us (0.989)
  waiting for transfers between devices: 33.7 us -> 21.9 us
  starting transfers between devices: 40.9 us -> 52.1 us
    ppermute x2 -> x4, waiting for transfers between devices: 15.9 us -> 3.57 us  [step(): to_far = lambda x, t: lax.ppermute(x, 'ctx', far_pairs[t])]
    ppermute x2 -> x4, starting transfers between devices: 0.28 us -> 10.7 us  [step(): to_far = lambda x, t: lax.ppermute(x, 'ctx', far_pairs[t])]
    ppermute x6 -> x9, starting transfers between devices: 9.16 us -> 12.3 us  [step(): to_near = lambda x, k: lax.ppermute(x, 'ctx', near_pairs[k])]
    ppermute x6 -> x10, starting transfers between devices: 31.2 us -> 28.9 us  [step(): swap = lambda x: lax.ppermute(x, 'ctx', core_pairs)]
    ppermute x6 -> x9, waiting for transfers between devices: 6.55 us -> 8.11 us  [step(): to_near = lambda x, k: lax.ppermute(x, 'ctx', near_pairs[k])]
    ppermute x6 -> x10, waiting for transfers between devices: 2.37 us -> 1.41 us  [step(): swap = lambda x: lax.ppermute(x, 'ctx', core_pairs)]
    pallas_call x5 -> x7, Pallas kernels: 12.4 us -> 11.9 us  [the longest x1 7.54 us: attend(): pl.pallas_call(functools.partial(attend_kernel, scaling, order, True), in...]
  transfers between devices with their start and end apart: 16 -> 25, of which waited for: 8 -> 9; matrix products, arithmetic and copies ran while one was open for 0% -> 0% of each run, Pallas kernels for 1% -> 2%
where the time goes in v5:
time: 88.8 us; the launch traced here: 88.7 us
  starting transfers between devices  52.1 us (59%)
  waiting for transfers between devices  21.9 us (25%)
  Pallas kernels  13 us (15%)
  other arithmetic  1.42 us (2%)
    ppermute x10, starting transfers between devices, step(): swap = lambda x: lax.ppermute(x, 'ctx', core_pairs)  28.9 us
    ppermute x9, starting transfers between devices, step(): to_near = lambda x, k: lax.ppermute(x, 'ctx', near_pairs[k])  12.3 us
    ppermute x4, starting transfers between devices, step(): to_far = lambda x, t: lax.ppermute(x, 'ctx', far_pairs[t])  10.7 us
    ppermute x2, waiting for transfers between devices, step(): to_head = lambda x, t: lax.ppermute(x, ('ctx', 'head'), head_pairs[t])  8.79 us
    ppermute x9, waiting for transfers between devices, step(): to_near = lambda x, k: lax.ppermute(x, 'ctx', near_pairs[k])  8.11 us
    pallas_call x1, Pallas kernels, attend(): pl.pallas_call(functools.partial(attend_kernel, scaling, order, True), in...  7.54 us
    ppermute x4, waiting for transfers between devices, step(): to_far = lambda x, t: lax.ppermute(x, 'ctx', far_pairs[t])  3.57 us
    pallas_call x1, Pallas kernels, last(): pl.pallas_call(functools.partial(attend_last_kernel, scaling), in_specs=[...  2.44 us
  transfers between devices with their start and end apart: 25, of which 9 were waited for; matrix products, arithmetic and copies ran while one was open for 0% of the time, Pallas kernels for 2%

profile of v5, /device:TPU:33, one launch (start us, length us, event | category | flops | bytes accessed | tf_op | source)
XLA Modules:
  0.0 88.7 jit_solution(11789775159854158563)
XLA Ops:
  0.0 0.7 pad_add_fusion.info
  0.7 7.5 %attend.1 = (f32[3,136,256]{2,1,0:T(8,128)S(1)}, f32[3,136,256]{2,1,0:T(8,128)S(1)}, bf16[2,256,128]{2,1,0:T(8,128)(2,1)S(1)}, bf16[4096,128]{1,0:T(8,128)(2,1)S(1)}, bf16[4096,128]{1,0:T(8,128)(2,1)S(1)}) custom-call(s32[7]{0:T(128)S(1)} %pad_add_fusion.info, bf16[4,2,256,128]{3,2,1,0:T(8,128)(2,1)} %bitcast.7, bf16[4,4096,128]{2,1,0:T(8,128)(2,1)} %bitcast.9, ...), custom_call_target="tpu_custom_call" | custom-call | flops 3221225472 | bytes 6291456 | tf_op jit(solution)/shard_map/attend/pallas_call | solution.py:221
  8.3 0.0 copy-start.1
  8.3 0.0 copy-start.2
  8.3 0.0 copy-start.3
  8.3 0.0 copy-start
  8.3 20.5 %collective-permute-start = (f32[3,136,256]{2,1,0:T(8,128)S(1)}, f32[3,136,256]{2,1,0:T(8,128)S(1)}, u32[]{:S(2)}, u32[]{:S(2)}) collective-permute-start(f32[3,136,256]{2,1,0:T(8,128)S(1)} %get-tuple-element.25), channel_id=1, source_target_pairs={{0,4},{4,0},{8,12},{12,8},{16,20},{20,16},{24,28},{28,24},{32,36},... | collective-permute-start | bytes 1253384 | tf_op jit(solution)/shard_map/ppermute | solution.py:375
  28.9 1.4 %collective-permute-done.got_ref = f32[3,136,256]{2,1,0:T(8,128)S(1)} collective-permute-done((f32[3,136,256]{2,1,0:T(8,128)S(1)}, f32[3,136,256]{2,1,0:T(8,128)S(1)}, u32[]{:S(2)}, u32[]{:S(2)}) %collective-permute-start) | collective-permute-done | bytes 417824 | tf_op jit(solution)/shard_map/ppermute | solution.py:375
  30.2 0.1 merge_core.2
  30.3 2.4 %attend_last.1 = (f32[1,136,256]{2,1,0:T(8,128)S(1)}, f32[1,136,256]{2,1,0:T(8,128)S(1)}) custom-call(s32[7]{0:T(128)S(1)} %pad_add_fusion.info, bf16[2,256,128]{2,1,0:T(8,128)(2,1)S(1)} %get-tuple-element.30.q_ref, bf16[4096,128]{1,0:T(8,128)(2,1)S(1)} %get-tuple-element.31.k_ref, bf16[4096,128]{1,0:T(8,128)(2,1)S(1)} %get-tuple-element.32.v_ref), custom_call_target="tpu_custom_call" | custom-call | flops 1073741824 | bytes 2097152 | tf_op jit(solution)/shard_map/attend_last/pallas_call | solution.py:240
  32.8 0.5 collective-permute-start.1
  33.3 0.0 collective-permute-start.2
  33.3 0.0 collective-permute-start.3
  33.3 2.7 %collective-permute-start.4 = (f32[136,256]{1,0:T(8,128)S(1)}, f32[136,256]{1,0:T(8,128)S(1)}, u32[]{:S(2)}, u32[]{:S(2)}) collective-permute-start(f32[136,256]{1,0:T(8,128)S(1)} %get-tuple-element.38), channel_id=1, source_target_pairs={{0,120},{4,124},{8,0},{12,4},{16,8},{20,12},{24,16},{28,20},{32,24... | collective-permute-start | bytes 417800 | tf_op jit(solution)/shard_map/ppermute | solution.py:376
  36.0 0.0 collective-permute-done.1.got_ref
  36.0 5.0 %collective-permute-done.2.refs_1_ = f32[136,256]{1,0:T(8,128)S(1)} collective-permute-done((f32[136,256]{1,0:T(8,128)S(1)}, f32[136,256]{1,0:T(8,128)S(1)}, u32[]{:S(2)}, u32[]{:S(2)}) %collective-permute-start.2) | collective-permute-done | bytes 139296 | tf_op jit(solution)/shard_map/ppermute | solution.py:376
  41.0 0.0 collective-permute-done.3.refs_2_
  41.0 1.6 %collective-permute-done.4.refs_3_ = f32[136,256]{1,0:T(8,128)S(1)} collective-permute-done((f32[136,256]{1,0:T(8,128)S(1)}, f32[136,256]{1,0:T(8,128)S(1)}, u32[]{:S(2)}, u32[]{:S(2)}) %collective-permute-start.4) | collective-permute-done | bytes 139296 | tf_op jit(solution)/shard_map/ppermute | solution.py:376
  42.5 0.1 merge.3
  42.6 0.1 collective-permute-start.14
  42.8 5.3 %collective-permute-start.5 = (f32[136,128]{1,0:T(8,128)S(1)}, f32[136,128]{1,0:T(8,128)S(1)}, u32[]{:S(2)}, u32[]{:S(2)}) collective-permute-start(f32[136,128]{1,0:T(8,128)S(1)} %get-tuple-element.39.refs_0_), channel_id=1, source_target_pairs={{0,32},{4,100},{8,40},{12,108},{16,48},{20,116},{24,56},{28,124},{... | collective-permute-start | bytes 208904 | tf_op jit(solution)/shard_map/ppermute | solution.py:377
  48.1 2.0 %collective-permute-done.14.refs_1_ = f32[136,128]{1,0:T(8,128)S(1)} collective-permute-done((f32[136,128]{1,0:T(8,128)S(1)}, f32[136,128]{1,0:T(8,128)S(1)}, u32[]{:S(2)}, u32[]{:S(2)}) %collective-permute-start.14) | collective-permute-done | bytes 69664 | tf_op jit(solution)/shard_map/ppermute | solution.py:377
  50.1 0.1 collective-permute-start.15
  50.3 0.6 collective-permute-done.5.refs_1_
  50.9 5.0 %collective-permute-start.6 = (f32[136,128]{1,0:T(8,128)S(1)}, f32[136,128]{1,0:T(8,128)S(1)}, u32[]{:S(2)}, u32[]{:S(2)}) collective-permute-start(f32[136,128]{1,0:T(8,128)S(1)} %merge.4.refs_0_), channel_id=1, source_target_pairs={{0,96},{4,36},{8,104},{12,44},{16,112},{20,52},{24,120},{28,60},{3... | collective-permute-start | bytes 208904 | tf_op jit(solution)/shard_map/ppermute | solution.py:377
  56.0 0.0 copy-done.1
  56.0 1.0 %own.1 = (f32[136,128]{1,0:T(8,128)S(1)}, f32[136,128]{1,0:T(8,128)S(1)}) custom-call(s32[7]{0:T(128)S(1)} %pad_add_fusion.info, bf16[4,2,256,128]{3,2,1,0:T(8,128)(2,1)S(1)} %bitcast.8, bf16[4,2,32,128]{3,2,1,0:T(8,128)(2,1)S(1)} %copy-done.2, bf16[4,2,32,128]{3,2,1,0:T(8,128)(2,1)S(1)} %copy-done.3), custom_call_target="tpu_custom_call" | custom-call | tf_op jit(solution)/shard_map/own/pallas_call | solution.py:421
  57.0 1.0 %collective-permute-done.15.refs_1_ = f32[136,128]{1,0:T(8,128)S(1)} collective-permute-done((f32[136,128]{1,0:T(8,128)S(1)}, f32[136,128]{1,0:T(8,128)S(1)}, u32[]{:S(2)}, u32[]{:S(2)}) %collective-permute-start.15) | collective-permute-done | bytes 69664 | tf_op jit(solution)/shard_map/ppermute | solution.py:377
  58.0 2.1 %collective-permute-start.17 = (f32[128,128]{1,0:T(8,128)S(1)}, f32[128,128]{1,0:T(8,128)S(1)}, u32[]{:S(2)}, u32[]{:S(2)}) collective-permute-start(f32[128,128]{1,0:T(8,128)S(1)} %finish.3.refs_0_), channel_id=1, source_target_pairs={{0,120},{4,124},{8,0},{12,4},{16,8},{20,12},{24,16},{28,20},{32,24... | collective-permute-start | bytes 196616 | tf_op jit(solution)/shard_map/ppermute | solution.py:376
  60.1 0.0 collective-permute-start.19
  60.1 1.3 %collective-permute-start.21 = (f32[128,128]{1,0:T(8,128)S(1)}, f32[128,128]{1,0:T(8,128)S(1)}, u32[]{:S(2)}, u32[]{:S(2)}) collective-permute-start(f32[128,128]{1,0:T(8,128)S(1)} %finish.3.refs_0_), channel_id=1, source_target_pairs={{0,8},{4,12},{8,16},{12,20},{16,24},{20,28},{24,32},{28,36},{32,40... | collective-permute-start | bytes 196616 | tf_op jit(solution)/shard_map/ppermute | solution.py:376
  61.4 4.9 %collective-permute-start.16 = (f32[128,128]{1,0:T(8,128)S(1)}, f32[128,128]{1,0:T(8,128)S(1)}, u32[]{:S(2)}, u32[]{:S(2)}) collective-permute-start(f32[128,128]{1,0:T(8,128)S(1)} %finish.3.refs_0_), channel_id=1, source_target_pairs={{0,4},{4,0},{8,12},{12,8},{16,20},{20,16},{24,28},{28,24},{32,36},... | collective-permute-start | bytes 196616 | tf_op jit(solution)/shard_map/ppermute | solution.py:375
  66.3 0.0 collective-permute-done.6.refs_1_
  66.3 3.5 %collective-permute-start.10 = (f32[128,128]{1,0:T(8,128)S(1)}, f32[128,128]{1,0:T(8,128)S(1)}, u32[]{:S(2)}, u32[]{:S(2)}) collective-permute-start(f32[128,128]{1,0:T(8,128)S(1)} %finish.2.refs_0_), channel_id=1, source_target_pairs={{0,16},{4,116},{8,24},{12,124},{16,32},{20,4},{24,40},{28,12},{32,... | collective-permute-start | bytes 196616 | tf_op jit(solution)/shard_map/ppermute | solution.py:376
  69.8 0.0 collective-permute-done.17.refs_2_
  69.8 0.8 collective-permute-start.12
  70.6 0.0 collective-permute-done.19.refs_4_
  70.6 1.9 %collective-permute-start.8 = (f32[128,128]{1,0:T(8,128)S(1)}, f32[128,128]{1,0:T(8,128)S(1)}, u32[]{:S(2)}, u32[]{:S(2)}) collective-permute-start(f32[128,128]{1,0:T(8,128)S(1)} %finish.2.refs_0_), channel_id=1, source_target_pairs={{0,120},{4,124},{8,0},{12,4},{16,8},{20,12},{24,16},{28,20},{32,24... | collective-permute-start | bytes 196616 | tf_op jit(solution)/shard_map/ppermute | solution.py:376
  72.5 0.0 collective-permute-done.21.refs_6_
  72.5 0.0 collective-permute-start.18
  72.5 0.0 collective-permute-done.16.refs_1_
  72.5 0.5 collective-permute-start.20
  73.0 0.0 collective-permute-done.10.refs_4_
  73.0 0.6 collective-permute-start.7
  73.5 1.6 %collective-permute-done.12.refs_6_ = f32[128,128]{1,0:T(8,128)S(1)} collective-permute-done((f32[128,128]{1,0:T(8,128)S(1)}, f32[128,128]{1,0:T(8,128)S(1)}, u32[]{:S(2)}, u32[]{:S(2)}) %collective-permute-start.12) | collective-permute-done | bytes 65568 | tf_op jit(solution)/shard_map/ppermute | solution.py:376
  75.1 0.5 collective-permute-start.22
  75.7 0.0 collective-permute-done.8.refs_2_
  75.7 0.9 collective-permute-start.11
  76.5 0.0 collective-permute-done.18.refs_3_
  76.5 0.0 collective-permute-start.13
  76.5 0.0 collective-permute-done.20.refs_5_
  76.5 0.5 collective-permute-start.9
  77.0 0.0 collective-permute-done.22.refs_7_
  77.0 0.9 %project.2.refs_8_ = f32[128,256]{1,0:T(8,128)S(1)} custom-call(s32[7]{0:T(128)S(1)} %pad_add_fusion.info, f32[128,128]{1,0:T(8,128)S(1)} %finish.3.refs_0_, f32[128,128]{1,0:T(8,128)S(1)} %collective-permute-done.16.refs_1_, f32[128,128]{1,0:T(8,128)S(1)} %collective-permute-done.17.refs_2_, f32[128,128]{1,0:T(8,128)S(1)} %collective-permute-done.18.refs_3_, ...), custom_call_target="tpu_custom_call" | custom-call | tf_op jit(solution)/shard_map/project/pallas_call | solution.py:447
  77.9 0.0 collective-permute-done.7.refs_1_
  77.9 0.0 collective-permute-done.11.refs_5_
  78.0 0.0 collective-permute-done.13.refs_7_
  78.0 0.0 collective-permute-done.9.refs_3_
  78.0 0.9 %project.3 = f32[128,256]{1,0:T(8,128)S(1)} custom-call(s32[7]{0:T(128)S(1)} %pad_add_fusion.info, f32[128,128]{1,0:T(8,128)S(1)} %finish.2.refs_0_, f32[128,128]{1,0:T(8,128)S(1)} %collective-permute-done.7.refs_1_, f32[128,128]{1,0:T(8,128)S(1)} %collective-permute-done.8.refs_2_, f32[128,128]{1,0:T(8,128)S(1)} %collective-permute-done.9.refs_3_, ...), custom_call_target="tpu_custom_call" | custom-call | tf_op jit(solution)/shard_map/project/pallas_call | solution.py:447
  78.9 0.1 collective-permute-start.23
  79.0 5.0 %collective-permute-done.23 = f32[128,256]{1,0:T(8,128)S(1)} collective-permute-done((f32[128,256]{1,0:T(8,128)S(1)}, f32[128,256]{1,0:T(8,128)S(1)}, u32[]{:S(2)}, u32[]{:S(2)}) %collective-permute-start.23) | collective-permute-done | bytes 131104 | tf_op jit(solution)/shard_map/ppermute | solution.py:378
  84.1 0.1 collective-permute-start.24
  84.2 3.8 %collective-permute-done.24 = f32[128,256]{1,0:T(8,128)S(1)} collective-permute-done((f32[128,256]{1,0:T(8,128)S(1)}, f32[128,256]{1,0:T(8,128)S(1)}, u32[]{:S(2)}, u32[]{:S(2)}) %collective-permute-start.24) | collective-permute-done | bytes 131104 | tf_op jit(solution)/shard_map/ppermute | solution.py:378
  88.0 0.7 add.17
  (9 shorter events, 0.2 us)
Async XLA Ops:
  8.3 47.7 %copy-start.1 = (bf16[4,16,32,128]{3,2,1,0:T(8,128)(2,1)S(1)}, bf16[4,16,32,128]{3,2,1,0:T(8,128)(2,1)}, u32[]{:S(2)}) copy-start(bf16[4,16,32,128]{3,2,1,0:T(8,128)(2,1)} %param.7) | copy-start | bytes 1572868
  8.3 47.7 %copy-start.2 = (bf16[4,2,32,128]{3,2,1,0:T(8,128)(2,1)S(1)}, bf16[4,2,32,128]{3,2,1,0:T(8,128)(2,1)}, u32[]{:S(2)}) copy-start(bf16[4,2,32,128]{3,2,1,0:T(8,128)(2,1)} %key_ref.1) | copy-start | bytes 196612
  8.3 47.7 %copy-start.3 = (bf16[4,2,32,128]{3,2,1,0:T(8,128)(2,1)S(1)}, bf16[4,2,32,128]{3,2,1,0:T(8,128)(2,1)}, u32[]{:S(2)}) copy-start(bf16[4,2,32,128]{3,2,1,0:T(8,128)(2,1)} %value_ref.1) | copy-start | bytes 196612
  8.3 68.7 %copy-start = (bf16[2048,256]{1,0:T(8,128)(2,1)S(1)}, bf16[2048,256]{1,0:T(8,128)(2,1)}, u32[]{:S(2)}) copy-start(bf16[2048,256]{1,0:T(8,128)(2,1)} %refs_9_.1) | copy-start | bytes 3145732
  8.3 21.9 %collective-permute-start = (f32[3,136,256]{2,1,0:T(8,128)S(1)}, f32[3,136,256]{2,1,0:T(8,128)S(1)}, u32[]{:S(2)}, u32[]{:S(2)}) collective-permute-start(f32[3,136,256]{2,1,0:T(8,128)S(1)} %get-tuple-element.25), channel_id=1, source_target_pairs={{0,4},{4,0},{8,12},{12,8},{16,20},{20,16},{24,28},{28,24},{32,36},... | collective-permute-start | bytes 1253384 | tf_op jit(solution)/shard_map/ppermute | solution.py:375
  32.8 3.2 %collective-permute-start.1 = (f32[1,136,256]{2,1,0:T(8,128)S(1)}, f32[1,136,256]{2,1,0:T(8,128)S(1)}, u32[]{:S(2)}, u32[]{:S(2)}) collective-permute-start(f32[1,136,256]{2,1,0:T(8,128)S(1)} %get-tuple-element.34), channel_id=1, source_target_pairs={{0,4},{4,0},{8,12},{12,8},{16,20},{20,16},{24,28},{28,24},{32,36},... | collective-permute-start | bytes 417800 | tf_op jit(solution)/shard_map/ppermute | solution.py:375
  33.3 7.7 %collective-permute-start.2 = (f32[136,256]{1,0:T(8,128)S(1)}, f32[136,256]{1,0:T(8,128)S(1)}, u32[]{:S(2)}, u32[]{:S(2)}) collective-permute-start(f32[136,256]{1,0:T(8,128)S(1)} %get-tuple-element.36), channel_id=1, source_target_pairs={{0,8},{4,12},{8,16},{12,20},{16,24},{20,28},{24,32},{28,36},{32,40... | collective-permute-start | bytes 417800 | tf_op jit(solution)/shard_map/ppermute | solution.py:376
  33.3 7.7 %collective-permute-start.3 = (f32[136,256]{1,0:T(8,128)S(1)}, f32[136,256]{1,0:T(8,128)S(1)}, u32[]{:S(2)}, u32[]{:S(2)}) collective-permute-start(f32[136,256]{1,0:T(8,128)S(1)} %get-tuple-element.37), channel_id=1, source_target_pairs={{0,16},{4,116},{8,24},{12,124},{16,32},{20,4},{24,40},{28,12},{32,... | collective-permute-start | bytes 417800 | tf_op jit(solution)/shard_map/ppermute | solution.py:376
  33.3 9.3 %collective-permute-start.4 = (f32[136,256]{1,0:T(8,128)S(1)}, f32[136,256]{1,0:T(8,128)S(1)}, u32[]{:S(2)}, u32[]{:S(2)}) collective-permute-start(f32[136,256]{1,0:T(8,128)S(1)} %get-tuple-element.38), channel_id=1, source_target_pairs={{0,120},{4,124},{8,0},{12,4},{16,8},{20,12},{24,16},{28,20},{32,24... | collective-permute-start | bytes 417800 | tf_op jit(solution)/shard_map/ppermute | solution.py:376
  42.6 7.5 %collective-permute-start.14 = (f32[136,128]{1,0:T(8,128)S(1)}, f32[136,128]{1,0:T(8,128)S(1)}, u32[]{:S(2)}, u32[]{:S(2)}) collective-permute-start(f32[136,128]{1,0:T(8,128)S(1)} %get-tuple-element.41.refs_0_), channel_id=1, source_target_pairs={{0,32},{4,100},{8,40},{12,108},{16,48},{20,116},{24,56},{28,124},{... | collective-permute-start | bytes 208904 | tf_op jit(solution)/shard_map/ppermute | solution.py:377
  42.8 8.1 %collective-permute-start.5 = (f32[136,128]{1,0:T(8,128)S(1)}, f32[136,128]{1,0:T(8,128)S(1)}, u32[]{:S(2)}, u32[]{:S(2)}) collective-permute-start(f32[136,128]{1,0:T(8,128)S(1)} %get-tuple-element.39.refs_0_), channel_id=1, source_target_pairs={{0,32},{4,100},{8,40},{12,108},{16,48},{20,116},{24,56},{28,124},{... | collective-permute-start | bytes 208904 | tf_op jit(solution)/shard_map/ppermute | solution.py:377
  50.1 7.8 %collective-permute-start.15 = (f32[136,128]{1,0:T(8,128)S(1)}, f32[136,128]{1,0:T(8,128)S(1)}, u32[]{:S(2)}, u32[]{:S(2)}) collective-permute-start(f32[136,128]{1,0:T(8,128)S(1)} %merge.5.refs_0_), channel_id=1, source_target_pairs={{0,96},{4,36},{8,104},{12,44},{16,112},{20,52},{24,120},{28,60},{3... | collective-permute-start | bytes 208904 | tf_op jit(solution)/shard_map/ppermute | solution.py:377
  50.9 15.4 %collective-permute-start.6 = (f32[136,128]{1,0:T(8,128)S(1)}, f32[136,128]{1,0:T(8,128)S(1)}, u32[]{:S(2)}, u32[]{:S(2)}) collective-permute-start(f32[136,128]{1,0:T(8,128)S(1)} %merge.4.refs_0_), channel_id=1, source_target_pairs={{0,96},{4,36},{8,104},{12,44},{16,112},{20,52},{24,120},{28,60},{3... | collective-permute-start | bytes 208904 | tf_op jit(solution)/shard_map/ppermute | solution.py:377
  58.0 11.8 %collective-permute-start.17 = (f32[128,128]{1,0:T(8,128)S(1)}, f32[128,128]{1,0:T(8,128)S(1)}, u32[]{:S(2)}, u32[]{:S(2)}) collective-permute-start(f32[128,128]{1,0:T(8,128)S(1)} %finish.3.refs_0_), channel_id=1, source_target_pairs={{0,120},{4,124},{8,0},{12,4},{16,8},{20,12},{24,16},{28,20},{32,24... | collective-permute-start | bytes 196616 | tf_op jit(solution)/shard_map/ppermute | solution.py:376
  60.1 10.5 %collective-permute-start.19 = (f32[128,128]{1,0:T(8,128)S(1)}, f32[128,128]{1,0:T(8,128)S(1)}, u32[]{:S(2)}, u32[]{:S(2)}) collective-permute-start(f32[128,128]{1,0:T(8,128)S(1)} %finish.3.refs_0_), channel_id=1, source_target_pairs={{0,16},{4,116},{8,24},{12,124},{16,32},{20,4},{24,40},{28,12},{32,... | collective-permute-start | bytes 196616 | tf_op jit(solution)/shard_map/ppermute | solution.py:376
  60.1 12.4 %collective-permute-start.21 = (f32[128,128]{1,0:T(8,128)S(1)}, f32[128,128]{1,0:T(8,128)S(1)}, u32[]{:S(2)}, u32[]{:S(2)}) collective-permute-start(f32[128,128]{1,0:T(8,128)S(1)} %finish.3.refs_0_), channel_id=1, source_target_pairs={{0,8},{4,12},{8,16},{12,20},{16,24},{20,28},{24,32},{28,36},{32,40... | collective-permute-start | bytes 196616 | tf_op jit(solution)/shard_map/ppermute | solution.py:376
  61.4 11.1 %collective-permute-start.16 = (f32[128,128]{1,0:T(8,128)S(1)}, f32[128,128]{1,0:T(8,128)S(1)}, u32[]{:S(2)}, u32[]{:S(2)}) collective-permute-start(f32[128,128]{1,0:T(8,128)S(1)} %finish.3.refs_0_), channel_id=1, source_target_pairs={{0,4},{4,0},{8,12},{12,8},{16,20},{20,16},{24,28},{28,24},{32,36},... | collective-permute-start | bytes 196616 | tf_op jit(solution)/shard_map/ppermute | solution.py:375
  66.3 6.7 %collective-permute-start.10 = (f32[128,128]{1,0:T(8,128)S(1)}, f32[128,128]{1,0:T(8,128)S(1)}, u32[]{:S(2)}, u32[]{:S(2)}) collective-permute-start(f32[128,128]{1,0:T(8,128)S(1)} %finish.2.refs_0_), channel_id=1, source_target_pairs={{0,16},{4,116},{8,24},{12,124},{16,32},{20,4},{24,40},{28,12},{32,... | collective-permute-start | bytes 196616 | tf_op jit(solution)/shard_map/ppermute | solution.py:376
  69.8 5.3 %collective-permute-start.12 = (f32[128,128]{1,0:T(8,128)S(1)}, f32[128,128]{1,0:T(8,128)S(1)}, u32[]{:S(2)}, u32[]{:S(2)}) collective-permute-start(f32[128,128]{1,0:T(8,128)S(1)} %finish.2.refs_0_), channel_id=1, source_target_pairs={{0,8},{4,12},{8,16},{12,20},{16,24},{20,28},{24,32},{28,36},{32,40... | collective-permute-start | bytes 196616 | tf_op jit(solution)/shard_map/ppermute | solution.py:376
  70.6 5.1 %collective-permute-start.8 = (f32[128,128]{1,0:T(8,128)S(1)}, f32[128,128]{1,0:T(8,128)S(1)}, u32[]{:S(2)}, u32[]{:S(2)}) collective-permute-start(f32[128,128]{1,0:T(8,128)S(1)} %finish.2.refs_0_), channel_id=1, source_target_pairs={{0,120},{4,124},{8,0},{12,4},{16,8},{20,12},{24,16},{28,20},{32,24... | collective-permute-start | bytes 196616 | tf_op jit(solution)/shard_map/ppermute | solution.py:376
  72.5 4.0 %collective-permute-start.18 = (f32[128,128]{1,0:T(8,128)S(1)}, f32[128,128]{1,0:T(8,128)S(1)}, u32[]{:S(2)}, u32[]{:S(2)}) collective-permute-start(f32[128,128]{1,0:T(8,128)S(1)} %collective-permute-done.17.refs_2_), channel_id=1, source_target_pairs={{0,4},{4,0},{8,12},{12,8},{16,20},{20,16},{24,28},{28,24},{32,36},... | collective-permute-start | bytes 196616 | tf_op jit(solution)/shard_map/ppermute | solution.py:375
  72.5 4.0 %collective-permute-start.20 = (f32[128,128]{1,0:T(8,128)S(1)}, f32[128,128]{1,0:T(8,128)S(1)}, u32[]{:S(2)}, u32[]{:S(2)}) collective-permute-start(f32[128,128]{1,0:T(8,128)S(1)} %collective-permute-done.19.refs_4_), channel_id=1, source_target_pairs={{0,4},{4,0},{8,12},{12,8},{16,20},{20,16},{24,28},{28,24},{32,36},... | collective-permute-start | bytes 196616 | tf_op jit(solution)/shard_map/ppermute | solution.py:375
  73.0 5.0 %collective-permute-start.7 = (f32[128,128]{1,0:T(8,128)S(1)}, f32[128,128]{1,0:T(8,128)S(1)}, u32[]{:S(2)}, u32[]{:S(2)}) collective-permute-start(f32[128,128]{1,0:T(8,128)S(1)} %finish.2.refs_0_), channel_id=1, source_target_pairs={{0,4},{4,0},{8,12},{12,8},{16,20},{20,16},{24,28},{28,24},{32,36},... | collective-permute-start | bytes 196616 | tf_op jit(solution)/shard_map/ppermute | solution.py:375
  75.1 1.9 %collective-permute-start.22 = (f32[128,128]{1,0:T(8,128)S(1)}, f32[128,128]{1,0:T(8,128)S(1)}, u32[]{:S(2)}, u32[]{:S(2)}) collective-permute-start(f32[128,128]{1,0:T(8,128)S(1)} %collective-permute-done.21.refs_6_), channel_id=1, source_target_pairs={{0,4},{4,0},{8,12},{12,8},{16,20},{20,16},{24,28},{28,24},{32,36},... | collective-permute-start | bytes 196616 | tf_op jit(solution)/shard_map/ppermute | solution.py:375
  75.7 2.3 %collective-permute-start.11 = (f32[128,128]{1,0:T(8,128)S(1)}, f32[128,128]{1,0:T(8,128)S(1)}, u32[]{:S(2)}, u32[]{:S(2)}) collective-permute-start(f32[128,128]{1,0:T(8,128)S(1)} %collective-permute-done.10.refs_4_), channel_id=1, source_target_pairs={{0,4},{4,0},{8,12},{12,8},{16,20},{20,16},{24,28},{28,24},{32,36},... | collective-permute-start | bytes 196616 | tf_op jit(solution)/shard_map/ppermute | solution.py:375
  76.5 1.4 %collective-permute-start.13 = (f32[128,128]{1,0:T(8,128)S(1)}, f32[128,128]{1,0:T(8,128)S(1)}, u32[]{:S(2)}, u32[]{:S(2)}) collective-permute-start(f32[128,128]{1,0:T(8,128)S(1)} %collective-permute-done.12.refs_6_), channel_id=1, source_target_pairs={{0,4},{4,0},{8,12},{12,8},{16,20},{20,16},{24,28},{28,24},{32,36},... | collective-permute-start | bytes 196616 | tf_op jit(solution)/shard_map/ppermute | solution.py:375
  76.5 1.4 %collective-permute-start.9 = (f32[128,128]{1,0:T(8,128)S(1)}, f32[128,128]{1,0:T(8,128)S(1)}, u32[]{:S(2)}, u32[]{:S(2)}) collective-permute-start(f32[128,128]{1,0:T(8,128)S(1)} %collective-permute-done.8.refs_2_), channel_id=1, source_target_pairs={{0,4},{4,0},{8,12},{12,8},{16,20},{20,16},{24,28},{28,24},{32,36},... | collective-permute-start | bytes 196616 | tf_op jit(solution)/shard_map/ppermute | solution.py:375
  78.9 5.2 %collective-permute-start.23 = (f32[128,256]{1,0:T(8,128)S(1)}, f32[128,256]{1,0:T(8,128)S(1)}, u32[]{:S(2)}, u32[]{:S(2)}) collective-permute-start(f32[128,256]{1,0:T(8,128)S(1)} %project.3), channel_id=1, source_target_pairs={{0,1},{1,0},{2,3},{3,2},{4,7},{5,6},{6,5},{7,4},{8,9},{9,8},{10,11... | collective-permute-start | bytes 393224 | tf_op jit(solution)/shard_map/ppermute | solution.py:378
  84.1 3.9 %collective-permute-start.24 = (f32[128,256]{1,0:T(8,128)S(1)}, f32[128,256]{1,0:T(8,128)S(1)}, u32[]{:S(2)}, u32[]{:S(2)}) collective-permute-start(f32[128,256]{1,0:T(8,128)S(1)} %add.16), channel_id=1, source_target_pairs={{0,3},{1,2},{2,1},{3,0},{4,5},{5,4},{6,7},{7,6},{8,11},{9,10},{10,... | collective-permute-start | bytes 393224 | tf_op jit(solution)/shard_map/ppermute | solution.py:378

commit v6 on v5

--- a/solution.py
+++ b/solution.py
@@ -51,25 +51,32 @@
     def slot(i):
         return copies(i, seq_of(i), (q_buf.at[i], k_buf.at[i], v_buf.at[i]))
 
-    for i in range(steps):
-
+    def begin(i):
         @pl.when(usable(seq_of(i)) > 0)
         def _():
             for copy in slot(i):
                 copy.start()
 
+    begin(0)
     if ahead:
         later = copies(steps, info[1], next_refs)
 
-        @pl.when(usable(info[1]) > 0)
-        def _():
-            for copy in later:
-                copy.start()
-
     def one(i, _):
+        def then():
+            @pl.when(i + 1 < steps)
+            def _():
+                begin(jnp.minimum(i + 1, steps - 1))
+
+            if ahead:
+
+                @pl.when(jnp.logical_and(i + 1 == steps, usable(info[1]) > 0))
+                def _():
+                    for copy in later:
+                        copy.start()
+
         count = usable(seq_of(i))
         refs = (q_buf.at[i], k_buf.at[i], v_buf.at[i], mine_ref.at[i], theirs_ref.at[i])
-        attend_one(scaling, info[2], count, slot(i), *refs, s_ref, acc_ref)
+        attend_one(scaling, info[2], count, slot(i), *refs, s_ref, acc_ref, then)
         return _
 
     lax.fori_loop(0, steps, one, 0)
@@ -87,7 +94,7 @@
     attend_one(scaling, info[2], count, None, *refs, s_ref, acc_ref)
 
 
-def attend_one(scaling, core, usable, copies, q_ref, k_ref, v_ref, mine_ref, theirs_ref, s_ref, acc_ref):
+def attend_one(scaling, core, usable, copies, q_ref, k_ref, v_ref, mine_ref, theirs_ref, s_ref, acc_ref, then=None):
     rows, head_dim = k_ref.shape
     queries = q_ref.shape[1]
     per_page = 2 * page
@@ -106,6 +113,8 @@
         def _():
             copies[0].wait()
             copies[1].wait()
+
+        then()
 
     qc = jnp.concatenate([q_ref[0].T, q_ref[1].T], axis=0)
 
@@ -268,20 +277,16 @@
         out[depth:, :] = stats(top, total)
 
 
-def put_halves(outs, numer, top, total):
-    depth, lanes = numer.shape[0], outs[0].shape[1]
-    for n, out in enumerate(outs):
-        at = slice(n * lanes, (n + 1) * lanes)
-        out[:depth, :] = numer[:, at]
-        out[depth:, :] = stats(top[:, at], total[:, at])
-
-
-def merge_kernel(n_out, *refs):
-    parts, outs = refs[:-n_out], refs[-n_out:]
-    put_halves(outs, *merged([p[...] for p in parts], outs[0].shape[0] - stat_rows))
-
-
-def own_kernel(scaling, draft, info, q_ref, key_ref, value_ref, *outs):
+def merge_kernel(*refs):
+    parts, out = refs[:-1], refs[-1]
+    depth = out.shape[0] - stat_rows
+    numer, top, total = merged([p[...] for p in parts], depth)
+    out[:depth, :] = numer
+    out[depth:, :] = stats(top, total)
+
+
+def own_kernel(scaling, draft, info, q_ref, key_ref, value_ref, out):
+    depth = out.shape[0] - stat_rows
     own = contract(key_ref[info[1], info[2]], q_ref[info[1], info[2]], 1, 1) * scaling
     at = lax.broadcasted_iota(jnp.int32, own.shape, 0)
     row = lax.broadcasted_iota(jnp.int32, own.shape, 1) % draft
@@ -290,8 +295,8 @@
     top = jnp.max(own, axis=0, keepdims=True)
     fresh = jnp.where(causal, jnp.exp(own - top), 0.0)
     values = value_ref[info[1], info[2]].astype(f32)
-    numer = contract(values, fresh, 0, 0, lax.Precision.HIGHEST)
-    put_halves(outs, numer, top, jnp.sum(fresh, axis=0, keepdims=True))
+    out[:depth, :] = contract(values, fresh, 0, 0, lax.Precision.HIGHEST)
+    out[depth:, :] = stats(top, jnp.sum(fresh, axis=0, keepdims=True))
 
 
 def finish_kernel(*refs):
@@ -300,25 +305,21 @@
     out[...] = (numer / total).astype(bf16).astype(f32)
 
 
-def project_kernel(draft, half, info, *refs):
-    n = 2 * radix
-    pieces, extra, (w_ref, out_ref, x_ref) = refs[:n], refs[n:-3], refs[-3:]
+def project_kernel(draft, info, *refs):
+    pieces, (w_ref, out_ref, x_ref) = refs[:-3], refs[-3:]
     width = x_ref.shape[2]
     for i, piece in enumerate(pieces):
         k, other = i // 2, i % 2
         g = jnp.bitwise_xor(info[2], other)
         seq = lax.rem(info[1] + k, radix)
         at = pl.ds(pl.multiple_of(seq * draft, draft), draft)
-        depth, lanes = piece.shape
-        att = piece[...].T.astype(bf16)
-        for h in range(lanes // draft):
-            x_ref[g, at, h * depth : (h + 1) * depth] = att[h * draft : (h + 1) * draft]
-    whole = w_ref.shape[0] // 2
-    products = [
-        contract(x_ref[g], w_ref[g * whole + half * width : g * whole + (half + 1) * width, :], 1, 0)
-        for g in range(2)
-    ]
-    out_ref[...] = sum(products + [e[...] for e in extra])
+        depth, queries = piece.shape
+        for a in range(queries // depth):
+            att = piece[:, a * depth : (a + 1) * depth].T.astype(bf16)
+            for h in range(depth // draft):
+                col = (a * (depth // draft) + h) * depth
+                x_ref[g, at, col : col + depth] = att[h * draft : (h + 1) * draft]
+    out_ref[...] = sum(contract(x_ref[g], w_ref[g * width : (g + 1) * width, :], 1, 0) for g in range(2))
 
 
 def whole_vmem(n):
@@ -405,58 +406,50 @@
         for k, x in zip(seqs_of, found):
             chunks[k] = to_near(x, k) if k else x
     chunks = [chunks[k] for k in range(radix)]
-    half_chunk = jax.ShapeDtypeStruct((head_dim + stat_rows, queries // 2), f32)
-
-    def merge(parts, n_out):
+
+    def merge(parts):
         return pl.pallas_call(
-            functools.partial(merge_kernel, n_out),
+            merge_kernel,
             in_specs=whole_vmem(len(parts)),
-            out_specs=whole_vmem(n_out),
-            out_shape=[half_chunk] * n_out,
+            out_specs=pl.BlockSpec(memory_space=VMEM),
+            out_shape=chunk,
             name="merge",
             compiler_params=limit(4),
         )(*parts)
 
-    found = merge(chunks, 2)
+    found = merge(chunks)
+    found = merge([found, to_far(found, 0)])
     own = pl.pallas_call(
         functools.partial(own_kernel, scaling, draft),
         in_specs=[smem] + whole_vmem(3),
-        out_specs=whole_vmem(2),
-        out_shape=[half_chunk] * 2,
+        out_specs=pl.BlockSpec(memory_space=VMEM),
+        out_shape=chunk,
         name="own",
         compiler_params=limit(4),
     )(info, grouped, new_key, new_value)
+    parts = [found, to_far(found, 1), own]
+    att = pl.pallas_call(
+        finish_kernel,
+        in_specs=whole_vmem(len(parts)),
+        out_specs=pl.BlockSpec(memory_space=VMEM),
+        out_shape=jax.ShapeDtypeStruct((head_dim, queries), f32),
+        name="finish",
+        compiler_params=limit(4),
+    )(*parts)
+    near = [att] + [to_near(att, radix - k) for k in range(1, radix)]
+    pieces = []
+    for part in near:
+        pieces += [part, swap(part)]
     width = out_weight.shape[1]
-    found = [merge([x, to_far(x, 0)], 1)[0] for x in found]
-    out = []
-    for n, x in enumerate(found):
-        parts = [x, to_far(x, 1), own[n]]
-        att = pl.pallas_call(
-            finish_kernel,
-            in_specs=whole_vmem(len(parts)),
-            out_specs=pl.BlockSpec(memory_space=VMEM),
-            out_shape=jax.ShapeDtypeStruct((head_dim, queries // 2), f32),
-            name="finish",
-            compiler_params=limit(4),
-        )(*parts)
-        near = [att] + [to_near(att, radix - k) for k in range(1, radix)]
-        pieces = []
-        for part in near:
-            pieces += [part, swap(part)]
-        out = [
-            pl.pallas_call(
-                functools.partial(project_kernel, draft, n),
-                in_specs=[smem] + whole_vmem(len(pieces) + len(out) + 1),
-                out_specs=pl.BlockSpec(memory_space=VMEM),
-                out_shape=jax.ShapeDtypeStruct((seqs * draft, width), f32),
-                scratch_shapes=[
-                    VMEM((heads, seqs * draft, out_weight.shape[0] // heads // 2), bf16)
-                ],
-                name="project",
-                compiler_params=limit(8),
-            )(info, *pieces, *out, out_weight)
-        ]
-    out = out[0]
+    out = pl.pallas_call(
+        functools.partial(project_kernel, draft),
+        in_specs=[smem] + whole_vmem(len(pieces) + 1),
+        out_specs=pl.BlockSpec(memory_space=VMEM),
+        out_shape=jax.ShapeDtypeStruct((seqs * draft, width), f32),
+        scratch_shapes=[VMEM((heads, seqs * draft, out_weight.shape[0] // heads), bf16)],
+        name="project",
+        compiler_params=limit(8),
+    )(info, *pieces, out_weight)
     for t in range(2):
         out = out + to_head(out, t)
     return out.reshape(seqs, draft, width)

time: 88.8 us -> 87 us (0.980)
  starting transfers between devices: 52.1 us -> 39.4 us
  waiting for transfers between devices: 21.9 us -> 33.6 us
    ppermute x4 -> x2, waiting for transfers between devices: 3.57 us -> 16 us  [step(): to_far = lambda x, t: lax.ppermute(x, 'ctx', far_pairs[t])]
    ppermute x4 -> x2, starting transfers between devices: 10.7 us -> 0.28 us  [step(): to_far = lambda x, t: lax.ppermute(x, 'ctx', far_pairs[t])]
    ppermute x9 -> x6, starting transfers between devices: 12.3 us -> 8.65 us  [step(): to_near = lambda x, k: lax.ppermute(x, 'ctx', near_pairs[k])]
    ppermute x9 -> x6, waiting for transfers between devices: 8.11 us -> 6.55 us  [step(): to_near = lambda x, k: lax.ppermute(x, 'ctx', near_pairs[k])]
    ppermute x10 -> x6, waiting for transfers between devices: 1.41 us -> 2.72 us  [step(): swap = lambda x: lax.ppermute(x, 'ctx', core_pairs)]
    ppermute x10 -> x6, starting transfers between devices: 28.9 us -> 29.8 us  [step(): swap = lambda x: lax.ppermute(x, 'ctx', core_pairs)]
    pallas_call x5 -> x3, Pallas kernels: 1.9 us -> 1.13 us  [the longest x1 1.05 us: step(): pl.pallas_call(functools.partial(project_kernel, draft), in_specs=[smem]...]
  transfers between devices with their start and end apart: 25 -> 16, of which waited for: 9 -> 9; matrix products, arithmetic and copies ran while one was open for 0% -> 0% of each run, Pallas kernels for 2% -> 1%
where the time goes in v6:
time: 87 us; the launch traced here: 86.9 us
  starting transfers between devices  39.4 us (45%)
  waiting for transfers between devices  33.6 us (39%)
  Pallas kernels  12.3 us (14%)
  other arithmetic  1.42 us (2%)
    ppermute x6, starting transfers between devices, step(): swap = lambda x: lax.ppermute(x, 'ctx', core_pairs)  29.8 us
    ppermute x2, waiting for transfers between devices, step(): to_far = lambda x, t: lax.ppermute(x, 'ctx', far_pairs[t])  16 us
    ppermute x6, starting transfers between devices, step(): to_near = lambda x, k: lax.ppermute(x, 'ctx', near_pairs[k])  8.65 us
    ppermute x2, waiting for transfers between devices, step(): to_head = lambda x, t: lax.ppermute(x, ('ctx', 'head'), head_pairs[t])  8.33 us
    pallas_call x1, Pallas kernels, attend(): pl.pallas_call(functools.partial(attend_kernel, scaling, order, True), in...  7.57 us
    ppermute x6, waiting for transfers between devices, step(): to_near = lambda x, k: lax.ppermute(x, 'ctx', near_pairs[k])  6.55 us
    ppermute x6, waiting for transfers between devices, step(): swap = lambda x: lax.ppermute(x, 'ctx', core_pairs)  2.72 us
    pallas_call x1, Pallas kernels, last(): pl.pallas_call(functools.partial(attend_last_kernel, scaling), in_specs=[...  2.44 us
  transfers between devices with their start and end apart: 16, of which 9 were waited for; matrix products, arithmetic and copies ran while one was open for 0% of the time, Pallas kernels for 1%

profile of v6, /device:TPU:33, one launch (start us, length us, event | category | flops | bytes accessed | tf_op | source)
XLA Modules:
  0.0 86.9 jit_solution(1316836733452746480)
XLA Ops:
  0.0 0.7 pad_add_fusion.info
  0.7 7.6 %attend.1 = (f32[3,136,256]{2,1,0:T(8,128)S(1)}, f32[3,136,256]{2,1,0:T(8,128)S(1)}, bf16[2,256,128]{2,1,0:T(8,128)(2,1)S(1)}, bf16[4096,128]{1,0:T(8,128)(2,1)S(1)}, bf16[4096,128]{1,0:T(8,128)(2,1)S(1)}) custom-call(s32[7]{0:T(128)S(1)} %pad_add_fusion.info, bf16[4,2,256,128]{3,2,1,0:T(8,128)(2,1)} %bitcast.7, bf16[4,4096,128]{2,1,0:T(8,128)(2,1)} %bitcast.9, ...), custom_call_target="tpu_custom_call" | custom-call | flops 3221225472 | bytes 6291456 | tf_op jit(solution)/shard_map/attend/pallas_call | solution.py:230
  8.3 0.0 copy-start.1
  8.3 0.0 copy-start.2
  8.3 0.0 copy-start.3
  8.3 0.0 copy-start
  8.4 20.5 %collective-permute-start = (f32[3,136,256]{2,1,0:T(8,128)S(1)}, f32[3,136,256]{2,1,0:T(8,128)S(1)}, u32[]{:S(2)}, u32[]{:S(2)}) collective-permute-start(f32[3,136,256]{2,1,0:T(8,128)S(1)} %get-tuple-element.21), channel_id=1, source_target_pairs={{0,4},{4,0},{8,12},{12,8},{16,20},{20,16},{24,28},{28,24},{32,36},... | collective-permute-start | bytes 1253384 | tf_op jit(solution)/shard_map/ppermute | solution.py:376
  28.9 1.4 %collective-permute-done.got_ref = f32[3,136,256]{2,1,0:T(8,128)S(1)} collective-permute-done((f32[3,136,256]{2,1,0:T(8,128)S(1)}, f32[3,136,256]{2,1,0:T(8,128)S(1)}, u32[]{:S(2)}, u32[]{:S(2)}) %collective-permute-start) | collective-permute-done | bytes 417824 | tf_op jit(solution)/shard_map/ppermute | solution.py:376
  30.3 0.1 merge_core.2
  30.4 2.4 %attend_last.1 = (f32[1,136,256]{2,1,0:T(8,128)S(1)}, f32[1,136,256]{2,1,0:T(8,128)S(1)}) custom-call(s32[7]{0:T(128)S(1)} %pad_add_fusion.info, bf16[2,256,128]{2,1,0:T(8,128)(2,1)S(1)} %get-tuple-element.26.q_ref, bf16[4096,128]{1,0:T(8,128)(2,1)S(1)} %get-tuple-element.27.k_ref, bf16[4096,128]{1,0:T(8,128)(2,1)S(1)} %get-tuple-element.28.v_ref), custom_call_target="tpu_custom_call" | custom-call | flops 1073741824 | bytes 2097152 | tf_op jit(solution)/shard_map/attend_last/pallas_call | solution.py:249
  32.8 0.5 collective-permute-start.1
  33.3 0.0 collective-permute-start.2
  33.3 0.0 collective-permute-start.3
  33.3 2.7 %collective-permute-start.4 = (f32[136,256]{1,0:T(8,128)S(1)}, f32[136,256]{1,0:T(8,128)S(1)}, u32[]{:S(2)}, u32[]{:S(2)}) collective-permute-start(f32[136,256]{1,0:T(8,128)S(1)} %get-tuple-element.34), channel_id=1, source_target_pairs={{0,120},{4,124},{8,0},{12,4},{16,8},{20,12},{24,16},{28,20},{32,24... | collective-permute-start | bytes 417800 | tf_op jit(solution)/shard_map/ppermute | solution.py:377
  36.0 0.0 collective-permute-done.1.got_ref
  36.0 5.0 %collective-permute-done.2.refs_1_ = f32[136,256]{1,0:T(8,128)S(1)} collective-permute-done((f32[136,256]{1,0:T(8,128)S(1)}, f32[136,256]{1,0:T(8,128)S(1)}, u32[]{:S(2)}, u32[]{:S(2)}) %collective-permute-start.2) | collective-permute-done | bytes 139296 | tf_op jit(solution)/shard_map/ppermute | solution.py:377
  41.0 0.0 collective-permute-done.3.refs_2_
  41.0 1.6 %collective-permute-done.4.refs_3_ = f32[136,256]{1,0:T(8,128)S(1)} collective-permute-done((f32[136,256]{1,0:T(8,128)S(1)}, f32[136,256]{1,0:T(8,128)S(1)}, u32[]{:S(2)}, u32[]{:S(2)}) %collective-permute-start.4) | collective-permute-done | bytes 139296 | tf_op jit(solution)/shard_map/ppermute | solution.py:377
  42.6 0.1 merge.2.refs_0_
  42.6 0.1 collective-permute-start.5
  42.8 8.1 %collective-permute-done.5.refs_1_ = f32[136,256]{1,0:T(8,128)S(1)} collective-permute-done((f32[136,256]{1,0:T(8,128)S(1)}, f32[136,256]{1,0:T(8,128)S(1)}, u32[]{:S(2)}, u32[]{:S(2)}) %collective-permute-start.5) | collective-permute-done | bytes 139296 | tf_op jit(solution)/shard_map/ppermute | solution.py:378
  50.9 0.1 collective-permute-start.6
  51.0 0.0 copy-done.1
  51.1 0.0 copy-done.2
  51.1 0.0 copy-done.3
  51.1 1.0 %own.1.refs_2_ = f32[136,256]{1,0:T(8,128)S(1)} custom-call(s32[7]{0:T(128)S(1)} %pad_add_fusion.info, bf16[4,2,256,128]{3,2,1,0:T(8,128)(2,1)S(1)} %bitcast.8, bf16[4,2,32,128]{3,2,1,0:T(8,128)(2,1)S(1)} %copy-done.2, bf16[4,2,32,128]{3,2,1,0:T(8,128)(2,1)S(1)} %copy-done.3), custom_call_target="tpu_custom_call" | custom-call | tf_op jit(solution)/shard_map/own/pallas_call | solution.py:422
  52.1 7.9 %collective-permute-done.6.refs_1_ = f32[136,256]{1,0:T(8,128)S(1)} collective-permute-done((f32[136,256]{1,0:T(8,128)S(1)}, f32[136,256]{1,0:T(8,128)S(1)}, u32[]{:S(2)}, u32[]{:S(2)}) %collective-permute-start.6) | collective-permute-done | bytes 139296 | tf_op jit(solution)/shard_map/ppermute | solution.py:378
  60.0 0.1 finish.1.refs_0_
  60.0 1.5 %collective-permute-start.10 = (f32[128,256]{1,0:T(8,128)S(1)}, f32[128,256]{1,0:T(8,128)S(1)}, u32[]{:S(2)}, u32[]{:S(2)}) collective-permute-start(f32[128,256]{1,0:T(8,128)S(1)} %finish.1.refs_0_), channel_id=1, source_target_pairs={{0,16},{4,116},{8,24},{12,124},{16,32},{20,4},{24,40},{28,12},{32,... | collective-permute-start | bytes 393224 | tf_op jit(solution)/shard_map/ppermute | solution.py:377
  61.5 4.4 %collective-permute-start.12 = (f32[128,256]{1,0:T(8,128)S(1)}, f32[128,256]{1,0:T(8,128)S(1)}, u32[]{:S(2)}, u32[]{:S(2)}) collective-permute-start(f32[128,256]{1,0:T(8,128)S(1)} %finish.1.refs_0_), channel_id=1, source_target_pairs={{0,8},{4,12},{8,16},{12,20},{16,24},{20,28},{24,32},{28,36},{32,40... | collective-permute-start | bytes 393224 | tf_op jit(solution)/shard_map/ppermute | solution.py:377
  66.0 0.0 collective-permute-start.8
  66.0 4.4 %collective-permute-start.7 = (f32[128,256]{1,0:T(8,128)S(1)}, f32[128,256]{1,0:T(8,128)S(1)}, u32[]{:S(2)}, u32[]{:S(2)}) collective-permute-start(f32[128,256]{1,0:T(8,128)S(1)} %finish.1.refs_0_), channel_id=1, source_target_pairs={{0,4},{4,0},{8,12},{12,8},{16,20},{20,16},{24,28},{28,24},{32,36},... | collective-permute-start | bytes 393224 | tf_op jit(solution)/shard_map/ppermute | solution.py:376
  70.4 0.0 collective-permute-done.10.refs_4_
  70.4 0.2 collective-permute-start.11
  70.6 0.0 collective-permute-done.12.refs_6_
  70.6 4.1 %collective-permute-start.13 = (f32[128,256]{1,0:T(8,128)S(1)}, f32[128,256]{1,0:T(8,128)S(1)}, u32[]{:S(2)}, u32[]{:S(2)}) collective-permute-start(f32[128,256]{1,0:T(8,128)S(1)} %collective-permute-done.12.refs_6_), channel_id=1, source_target_pairs={{0,4},{4,0},{8,12},{12,8},{16,20},{20,16},{24,28},{28,24},{32,36},... | collective-permute-start | bytes 393224 | tf_op jit(solution)/shard_map/ppermute | solution.py:376
  74.7 0.0 collective-permute-done.8.refs_2_
  74.7 0.0 collective-permute-start.9
  74.7 0.0 collective-permute-done.7.refs_1_
  74.7 0.0 collective-permute-done.11.refs_5_
  74.7 1.0 %collective-permute-done.13.refs_7_ = f32[128,256]{1,0:T(8,128)S(1)} collective-permute-done((f32[128,256]{1,0:T(8,128)S(1)}, f32[128,256]{1,0:T(8,128)S(1)}, u32[]{:S(2)}, u32[]{:S(2)}) %collective-permute-start.13) | collective-permute-done | bytes 131104 | tf_op jit(solution)/shard_map/ppermute | solution.py:376
  75.7 0.4 collective-permute-done.9.refs_3_
  76.1 0.0 copy-done
  76.1 1.0 %project.1 = f32[128,256]{1,0:T(8,128)S(1)} custom-call(s32[7]{0:T(128)S(1)} %pad_add_fusion.info, f32[128,256]{1,0:T(8,128)S(1)} %finish.1.refs_0_, f32[128,256]{1,0:T(8,128)S(1)} %collective-permute-done.7.refs_1_, f32[128,256]{1,0:T(8,128)S(1)} %collective-permute-done.8.refs_2_, f32[128,256]{1,0:T(8,128)S(1)} %collective-permute-done.9.refs_3_, ...), custom_call_target="tpu_custom_call" | custom-call | tf_op jit(solution)/shard_map/project/pallas_call | solution.py:444
  77.1 0.6 collective-permute-start.14
  77.7 4.5 %collective-permute-done.14 = f32[128,256]{1,0:T(8,128)S(1)} collective-permute-done((f32[128,256]{1,0:T(8,128)S(1)}, f32[128,256]{1,0:T(8,128)S(1)}, u32[]{:S(2)}, u32[]{:S(2)}) %collective-permute-start.14) | collective-permute-done | bytes 131104 | tf_op jit(solution)/shard_map/ppermute | solution.py:379
  82.3 0.1 collective-permute-start.15
  82.4 3.8 %collective-permute-done.15 = f32[128,256]{1,0:T(8,128)S(1)} collective-permute-done((f32[128,256]{1,0:T(8,128)S(1)}, f32[128,256]{1,0:T(8,128)S(1)}, u32[]{:S(2)}, u32[]{:S(2)}) %collective-permute-start.15) | collective-permute-done | bytes 131104 | tf_op jit(solution)/shard_map/ppermute | solution.py:379
  86.2 0.7 add.17
  (3 shorter events, 0.1 us)
Async XLA Ops:
  8.3 42.7 %copy-start.1 = (bf16[4,16,32,128]{3,2,1,0:T(8,128)(2,1)S(1)}, bf16[4,16,32,128]{3,2,1,0:T(8,128)(2,1)}, u32[]{:S(2)}) copy-start(bf16[4,16,32,128]{3,2,1,0:T(8,128)(2,1)} %param.7) | copy-start | bytes 1572868
  8.3 42.7 %copy-start.2 = (bf16[4,2,32,128]{3,2,1,0:T(8,128)(2,1)S(1)}, bf16[4,2,32,128]{3,2,1,0:T(8,128)(2,1)}, u32[]{:S(2)}) copy-start(bf16[4,2,32,128]{3,2,1,0:T(8,128)(2,1)} %key_ref.1) | copy-start | bytes 196612
  8.3 42.7 %copy-start.3 = (bf16[4,2,32,128]{3,2,1,0:T(8,128)(2,1)S(1)}, bf16[4,2,32,128]{3,2,1,0:T(8,128)(2,1)}, u32[]{:S(2)}) copy-start(bf16[4,2,32,128]{3,2,1,0:T(8,128)(2,1)} %value_ref.1) | copy-start | bytes 196612
  8.3 67.7 %copy-start = (bf16[2048,256]{1,0:T(8,128)(2,1)S(1)}, bf16[2048,256]{1,0:T(8,128)(2,1)}, u32[]{:S(2)}) copy-start(bf16[2048,256]{1,0:T(8,128)(2,1)} %refs_8_.1) | copy-start | bytes 3145732
  8.4 21.9 %collective-permute-start = (f32[3,136,256]{2,1,0:T(8,128)S(1)}, f32[3,136,256]{2,1,0:T(8,128)S(1)}, u32[]{:S(2)}, u32[]{:S(2)}) collective-permute-start(f32[3,136,256]{2,1,0:T(8,128)S(1)} %get-tuple-element.21), channel_id=1, source_target_pairs={{0,4},{4,0},{8,12},{12,8},{16,20},{20,16},{24,28},{28,24},{32,36},... | collective-permute-start | bytes 1253384 | tf_op jit(solution)/shard_map/ppermute | solution.py:376
  32.8 3.2 %collective-permute-start.1 = (f32[1,136,256]{2,1,0:T(8,128)S(1)}, f32[1,136,256]{2,1,0:T(8,128)S(1)}, u32[]{:S(2)}, u32[]{:S(2)}) collective-permute-start(f32[1,136,256]{2,1,0:T(8,128)S(1)} %get-tuple-element.30), channel_id=1, source_target_pairs={{0,4},{4,0},{8,12},{12,8},{16,20},{20,16},{24,28},{28,24},{32,36},... | collective-permute-start | bytes 417800 | tf_op jit(solution)/shard_map/ppermute | solution.py:376
  33.3 7.7 %collective-permute-start.2 = (f32[136,256]{1,0:T(8,128)S(1)}, f32[136,256]{1,0:T(8,128)S(1)}, u32[]{:S(2)}, u32[]{:S(2)}) collective-permute-start(f32[136,256]{1,0:T(8,128)S(1)} %get-tuple-element.32), channel_id=1, source_target_pairs={{0,8},{4,12},{8,16},{12,20},{16,24},{20,28},{24,32},{28,36},{32,40... | collective-permute-start | bytes 417800 | tf_op jit(solution)/shard_map/ppermute | solution.py:377
  33.3 7.7 %collective-permute-start.3 = (f32[136,256]{1,0:T(8,128)S(1)}, f32[136,256]{1,0:T(8,128)S(1)}, u32[]{:S(2)}, u32[]{:S(2)}) collective-permute-start(f32[136,256]{1,0:T(8,128)S(1)} %get-tuple-element.33), channel_id=1, source_target_pairs={{0,16},{4,116},{8,24},{12,124},{16,32},{20,4},{24,40},{28,12},{32,... | collective-permute-start | bytes 417800 | tf_op jit(solution)/shard_map/ppermute | solution.py:377
  33.3 9.3 %collective-permute-start.4 = (f32[136,256]{1,0:T(8,128)S(1)}, f32[136,256]{1,0:T(8,128)S(1)}, u32[]{:S(2)}, u32[]{:S(2)}) collective-permute-start(f32[136,256]{1,0:T(8,128)S(1)} %get-tuple-element.34), channel_id=1, source_target_pairs={{0,120},{4,124},{8,0},{12,4},{16,8},{20,12},{24,16},{28,20},{32,24... | collective-permute-start | bytes 417800 | tf_op jit(solution)/shard_map/ppermute | solution.py:377
  42.6 8.2 %collective-permute-start.5 = (f32[136,256]{1,0:T(8,128)S(1)}, f32[136,256]{1,0:T(8,128)S(1)}, u32[]{:S(2)}, u32[]{:S(2)}) collective-permute-start(f32[136,256]{1,0:T(8,128)S(1)} %merge.2.refs_0_), channel_id=1, source_target_pairs={{0,32},{4,100},{8,40},{12,108},{16,48},{20,116},{24,56},{28,124},{... | collective-permute-start | bytes 417800 | tf_op jit(solution)/shard_map/ppermute | solution.py:378
  50.9 9.1 %collective-permute-start.6 = (f32[136,256]{1,0:T(8,128)S(1)}, f32[136,256]{1,0:T(8,128)S(1)}, u32[]{:S(2)}, u32[]{:S(2)}) collective-permute-start(f32[136,256]{1,0:T(8,128)S(1)} %merge.3.refs_0_), channel_id=1, source_target_pairs={{0,96},{4,36},{8,104},{12,44},{16,112},{20,52},{24,120},{28,60},{3... | collective-permute-start | bytes 417800 | tf_op jit(solution)/shard_map/ppermute | solution.py:378
  60.0 10.4 %collective-permute-start.10 = (f32[128,256]{1,0:T(8,128)S(1)}, f32[128,256]{1,0:T(8,128)S(1)}, u32[]{:S(2)}, u32[]{:S(2)}) collective-permute-start(f32[128,256]{1,0:T(8,128)S(1)} %finish.1.refs_0_), channel_id=1, source_target_pairs={{0,16},{4,116},{8,24},{12,124},{16,32},{20,4},{24,40},{28,12},{32,... | collective-permute-start | bytes 393224 | tf_op jit(solution)/shard_map/ppermute | solution.py:377
  61.5 9.0 %collective-permute-start.12 = (f32[128,256]{1,0:T(8,128)S(1)}, f32[128,256]{1,0:T(8,128)S(1)}, u32[]{:S(2)}, u32[]{:S(2)}) collective-permute-start(f32[128,256]{1,0:T(8,128)S(1)} %finish.1.refs_0_), channel_id=1, source_target_pairs={{0,8},{4,12},{8,16},{12,20},{16,24},{20,28},{24,32},{28,36},{32,40... | collective-permute-start | bytes 393224 | tf_op jit(solution)/shard_map/ppermute | solution.py:377
  66.0 8.7 %collective-permute-start.8 = (f32[128,256]{1,0:T(8,128)S(1)}, f32[128,256]{1,0:T(8,128)S(1)}, u32[]{:S(2)}, u32[]{:S(2)}) collective-permute-start(f32[128,256]{1,0:T(8,128)S(1)} %finish.1.refs_0_), channel_id=1, source_target_pairs={{0,120},{4,124},{8,0},{12,4},{16,8},{20,12},{24,16},{28,20},{32,24... | collective-permute-start | bytes 393224 | tf_op jit(solution)/shard_map/ppermute | solution.py:377
  66.0 8.7 %collective-permute-start.7 = (f32[128,256]{1,0:T(8,128)S(1)}, f32[128,256]{1,0:T(8,128)S(1)}, u32[]{:S(2)}, u32[]{:S(2)}) collective-permute-start(f32[128,256]{1,0:T(8,128)S(1)} %finish.1.refs_0_), channel_id=1, source_target_pairs={{0,4},{4,0},{8,12},{12,8},{16,20},{20,16},{24,28},{28,24},{32,36},... | collective-permute-start | bytes 393224 | tf_op jit(solution)/shard_map/ppermute | solution.py:376
  70.4 4.4 %collective-permute-start.11 = (f32[128,256]{1,0:T(8,128)S(1)}, f32[128,256]{1,0:T(8,128)S(1)}, u32[]{:S(2)}, u32[]{:S(2)}) collective-permute-start(f32[128,256]{1,0:T(8,128)S(1)} %collective-permute-done.10.refs_4_), channel_id=1, source_target_pairs={{0,4},{4,0},{8,12},{12,8},{16,20},{20,16},{24,28},{28,24},{32,36},... | collective-permute-start | bytes 393224 | tf_op jit(solution)/shard_map/ppermute | solution.py:376
  70.6 5.1 %collective-permute-start.13 = (f32[128,256]{1,0:T(8,128)S(1)}, f32[128,256]{1,0:T(8,128)S(1)}, u32[]{:S(2)}, u32[]{:S(2)}) collective-permute-start(f32[128,256]{1,0:T(8,128)S(1)} %collective-permute-done.12.refs_6_), channel_id=1, source_target_pairs={{0,4},{4,0},{8,12},{12,8},{16,20},{20,16},{24,28},{28,24},{32,36},... | collective-permute-start | bytes 393224 | tf_op jit(solution)/shard_map/ppermute | solution.py:376
  74.7 1.3 %collective-permute-start.9 = (f32[128,256]{1,0:T(8,128)S(1)}, f32[128,256]{1,0:T(8,128)S(1)}, u32[]{:S(2)}, u32[]{:S(2)}) collective-permute-start(f32[128,256]{1,0:T(8,128)S(1)} %collective-permute-done.8.refs_2_), channel_id=1, source_target_pairs={{0,4},{4,0},{8,12},{12,8},{16,20},{20,16},{24,28},{28,24},{32,36},... | collective-permute-start | bytes 393224 | tf_op jit(solution)/shard_map/ppermute | solution.py:376
  77.1 5.2 %collective-permute-start.14 = (f32[128,256]{1,0:T(8,128)S(1)}, f32[128,256]{1,0:T(8,128)S(1)}, u32[]{:S(2)}, u32[]{:S(2)}) collective-permute-start(f32[128,256]{1,0:T(8,128)S(1)} %project.1), channel_id=1, source_target_pairs={{0,1},{1,0},{2,3},{3,2},{4,7},{5,6},{6,5},{7,4},{8,9},{9,8},{10,11... | collective-permute-start | bytes 393224 | tf_op jit(solution)/shard_map/ppermute | solution.py:379
  82.3 3.9 %collective-permute-start.15 = (f32[128,256]{1,0:T(8,128)S(1)}, f32[128,256]{1,0:T(8,128)S(1)}, u32[]{:S(2)}, u32[]{:S(2)}) collective-permute-start(f32[128,256]{1,0:T(8,128)S(1)} %add.16), channel_id=1, source_target_pairs={{0,3},{1,2},{2,1},{3,0},{4,5},{5,4},{6,7},{7,6},{8,11},{9,10},{10,... | collective-permute-start | bytes 393224 | tf_op jit(solution)/shard_map/ppermute | solution.py:379

commit v7 on v5

--- a/solution.py
+++ b/solution.py
@@ -51,25 +51,32 @@
     def slot(i):
         return copies(i, seq_of(i), (q_buf.at[i], k_buf.at[i], v_buf.at[i]))
 
-    for i in range(steps):
-
+    def begin(i):
         @pl.when(usable(seq_of(i)) > 0)
         def _():
             for copy in slot(i):
                 copy.start()
 
+    begin(0)
     if ahead:
         later = copies(steps, info[1], next_refs)
 
-        @pl.when(usable(info[1]) > 0)
-        def _():
-            for copy in later:
-                copy.start()
-
     def one(i, _):
+        def then():
+            @pl.when(i + 1 < steps)
+            def _():
+                begin(jnp.minimum(i + 1, steps - 1))
+
+            if ahead:
+
+                @pl.when(jnp.logical_and(i + 1 == steps, usable(info[1]) > 0))
+                def _():
+                    for copy in later:
+                        copy.start()
+
         count = usable(seq_of(i))
         refs = (q_buf.at[i], k_buf.at[i], v_buf.at[i], mine_ref.at[i], theirs_ref.at[i])
-        attend_one(scaling, info[2], count, slot(i), *refs, s_ref, acc_ref)
+        attend_one(scaling, info[2], count, slot(i), *refs, s_ref, acc_ref, then)
         return _
 
     lax.fori_loop(0, steps, one, 0)
@@ -87,7 +94,7 @@
     attend_one(scaling, info[2], count, None, *refs, s_ref, acc_ref)
 
 
-def attend_one(scaling, core, usable, copies, q_ref, k_ref, v_ref, mine_ref, theirs_ref, s_ref, acc_ref):
+def attend_one(scaling, core, usable, copies, q_ref, k_ref, v_ref, mine_ref, theirs_ref, s_ref, acc_ref, then=None):
     rows, head_dim = k_ref.shape
     queries = q_ref.shape[1]
     per_page = 2 * page
@@ -106,6 +113,8 @@
         def _():
             copies[0].wait()
             copies[1].wait()
+
+        then()
 
     qc = jnp.concatenate([q_ref[0].T, q_ref[1].T], axis=0)
 
@@ -389,9 +398,8 @@
     steps = (2, 1, 3)
     pair, last = attend(grouped, keys, values, info, scaling, steps)
     chunks = {}
-    gate = info
     for call, seqs_of in enumerate((steps, (0,))):
-        mine, theirs = pair if call == 0 else last(gate)
+        mine, theirs = pair if call == 0 else last(info)
         got = swap(theirs)
         found = pl.pallas_call(
             merge_core_kernel,
@@ -401,7 +409,6 @@
             name="merge_core",
             compiler_params=limit(8),
         )(mine, got)
-        gate, *found = lax.optimization_barrier((info, *found))
         for k, x in zip(seqs_of, found):
             chunks[k] = to_near(x, k) if k else x
     chunks = [chunks[k] for k in range(radix)]

time: 88.8 us -> 88.3 us (level)
  waiting for transfers between devices: 21.9 us -> 20.8 us
    ppermute x10, starting transfers between devices: 28.9 us -> 32.3 us  [step(): swap = lambda x: lax.ppermute(x, 'ctx', core_pairs)]
    ppermute x9, starting transfers between devices: 12.3 us -> 9.39 us  [step(): to_near = lambda x, k: lax.ppermute(x, 'ctx', near_pairs[k])]
    ppermute x10, waiting for transfers between devices: 1.41 us -> 0.28 us  [step(): swap = lambda x: lax.ppermute(x, 'ctx', core_pairs)]
  transfers between devices with their start and end apart: 25 -> 25, of which waited for: 9 -> 9; matrix products, arithmetic and copies ran while one was open for 0% -> 0% of each run, Pallas kernels for 2% -> 5%
where the time goes in v7:
time: 88.3 us; the launch traced here: 88.2 us
  starting transfers between devices  52.6 us (60%)
  waiting for transfers between devices  20.8 us (24%)
  Pallas kernels  13.1 us (15%)
  other arithmetic  1.42 us (2%)
    ppermute x10, starting transfers between devices, step(): swap = lambda x: lax.ppermute(x, 'ctx', core_pairs)  32.3 us
    ppermute x4, starting transfers between devices, step(): to_far = lambda x, t: lax.ppermute(x, 'ctx', far_pairs[t])  10.7 us
    ppermute x9, starting transfers between devices, step(): to_near = lambda x, k: lax.ppermute(x, 'ctx', near_pairs[k])  9.39 us
    ppermute x2, waiting for transfers between devices, step(): to_head = lambda x, t: lax.ppermute(x, ('ctx', 'head'), head_pairs[t])  8.79 us
    ppermute x9, waiting for transfers between devices, step(): to_near = lambda x, k: lax.ppermute(x, 'ctx', near_pairs[k])  8.24 us
    pallas_call x1, Pallas kernels, attend(): pl.pallas_call(functools.partial(attend_kernel, scaling, order, True), in...  7.57 us
    ppermute x4, waiting for transfers between devices, step(): to_far = lambda x, t: lax.ppermute(x, 'ctx', far_pairs[t])  3.48 us
    pallas_call x1, Pallas kernels, last(): pl.pallas_call(functools.partial(attend_last_kernel, scaling), in_specs=[...  2.44 us
  transfers between devices with their start and end apart: 25, of which 9 were waited for; matrix products, arithmetic and copies ran while one was open for 0% of the time, Pallas kernels for 5%

profile of v7, /device:TPU:33, one launch (start us, length us, event | category | flops | bytes accessed | tf_op | source)
XLA Modules:
  0.0 88.2 jit_solution(7804785517890406451)
XLA Ops:
  0.0 0.7 pad_add_fusion.info
  0.7 7.6 %attend.1 = (f32[3,136,256]{2,1,0:T(8,128)S(1)}, f32[3,136,256]{2,1,0:T(8,128)S(1)}, bf16[2,256,128]{2,1,0:T(8,128)(2,1)S(1)}, bf16[4096,128]{1,0:T(8,128)(2,1)S(1)}, bf16[4096,128]{1,0:T(8,128)(2,1)S(1)}) custom-call(s32[7]{0:T(128)S(1)} %pad_add_fusion.info, bf16[4,2,256,128]{3,2,1,0:T(8,128)(2,1)} %bitcast.7, bf16[4,4096,128]{2,1,0:T(8,128)(2,1)} %bitcast.9, ...), custom_call_target="tpu_custom_call" | custom-call | flops 3221225472 | bytes 6291456 | tf_op jit(solution)/shard_map/attend/pallas_call | solution.py:230
  8.3 0.0 copy-start.1
  8.3 0.0 copy-start.2
  8.3 0.0 copy-start.3
  8.3 0.0 copy-start
  8.4 20.5 %collective-permute-start.1 = (f32[3,136,256]{2,1,0:T(8,128)S(1)}, f32[3,136,256]{2,1,0:T(8,128)S(1)}, u32[]{:S(2)}, u32[]{:S(2)}) collective-permute-start(f32[3,136,256]{2,1,0:T(8,128)S(1)} %get-tuple-element.25), channel_id=1, source_target_pairs={{0,4},{4,0},{8,12},{12,8},{16,20},{20,16},{24,28},{28,24},{32,36},... | collective-permute-start | bytes 1253384 | tf_op jit(solution)/shard_map/ppermute | solution.py:384
  28.9 2.4 %attend_last.1 = (f32[1,136,256]{2,1,0:T(8,128)S(1)}, f32[1,136,256]{2,1,0:T(8,128)S(1)}) custom-call(s32[7]{0:T(128)S(1)} %pad_add_fusion.info, bf16[2,256,128]{2,1,0:T(8,128)(2,1)S(1)} %get-tuple-element.19.q_ref, bf16[4096,128]{1,0:T(8,128)(2,1)S(1)} %get-tuple-element.20.k_ref, bf16[4096,128]{1,0:T(8,128)(2,1)S(1)} %get-tuple-element.21.v_ref), custom_call_target="tpu_custom_call" | custom-call | flops 1073741824 | bytes 2097152 | tf_op jit(solution)/shard_map/attend_last/pallas_call | solution.py:249
  31.3 0.2 collective-permute-start
  31.5 0.0 collective-permute-done.1.got_ref
  31.5 0.1 merge_core.3
  31.6 0.1 collective-permute-start.2
  31.7 0.1 collective-permute-start.3
  31.9 2.5 %collective-permute-start.4 = (f32[136,256]{1,0:T(8,128)S(1)}, f32[136,256]{1,0:T(8,128)S(1)}, u32[]{:S(2)}, u32[]{:S(2)}) collective-permute-start(f32[136,256]{1,0:T(8,128)S(1)} %get-tuple-element.28), channel_id=1, source_target_pairs={{0,120},{4,124},{8,0},{12,4},{16,8},{20,12},{24,16},{28,20},{32,24... | collective-permute-start | bytes 417800 | tf_op jit(solution)/shard_map/ppermute | solution.py:385
  34.4 0.0 collective-permute-done.got_ref
  34.4 3.3 %collective-permute-done.2.refs_1_ = f32[136,256]{1,0:T(8,128)S(1)} collective-permute-done((f32[136,256]{1,0:T(8,128)S(1)}, f32[136,256]{1,0:T(8,128)S(1)}, u32[]{:S(2)}, u32[]{:S(2)}) %collective-permute-start.2) | collective-permute-done | bytes 139296 | tf_op jit(solution)/shard_map/ppermute | solution.py:385
  37.7 0.0 collective-permute-done.3.refs_2_
  37.7 3.4 %collective-permute-done.4.refs_3_ = f32[136,256]{1,0:T(8,128)S(1)} collective-permute-done((f32[136,256]{1,0:T(8,128)S(1)}, f32[136,256]{1,0:T(8,128)S(1)}, u32[]{:S(2)}, u32[]{:S(2)}) %collective-permute-start.4) | collective-permute-done | bytes 139296 | tf_op jit(solution)/shard_map/ppermute | solution.py:385
  41.1 0.1 merge.3
  41.2 0.1 collective-permute-start.5
  41.3 5.3 %collective-permute-start.14 = (f32[136,128]{1,0:T(8,128)S(1)}, f32[136,128]{1,0:T(8,128)S(1)}, u32[]{:S(2)}, u32[]{:S(2)}) collective-permute-start(f32[136,128]{1,0:T(8,128)S(1)} %get-tuple-element.31.refs_0_), channel_id=1, source_target_pairs={{0,32},{4,100},{8,40},{12,108},{16,48},{20,116},{24,56},{28,124},{... | collective-permute-start | bytes 208904 | tf_op jit(solution)/shard_map/ppermute | solution.py:386
  46.7 2.0 %collective-permute-done.5.refs_1_ = f32[136,128]{1,0:T(8,128)S(1)} collective-permute-done((f32[136,128]{1,0:T(8,128)S(1)}, f32[136,128]{1,0:T(8,128)S(1)}, u32[]{:S(2)}, u32[]{:S(2)}) %collective-permute-start.5) | collective-permute-done | bytes 69664 | tf_op jit(solution)/shard_map/ppermute | solution.py:386
  48.7 0.1 collective-permute-start.6
  48.9 0.6 collective-permute-done.14.refs_1_
  49.5 5.0 %collective-permute-start.15 = (f32[136,128]{1,0:T(8,128)S(1)}, f32[136,128]{1,0:T(8,128)S(1)}, u32[]{:S(2)}, u32[]{:S(2)}) collective-permute-start(f32[136,128]{1,0:T(8,128)S(1)} %merge.5.refs_0_), channel_id=1, source_target_pairs={{0,96},{4,36},{8,104},{12,44},{16,112},{20,52},{24,120},{28,60},{3... | collective-permute-start | bytes 208904 | tf_op jit(solution)/shard_map/ppermute | solution.py:386
  54.5 0.0 copy-done.1
  54.6 1.0 %own.1 = (f32[136,128]{1,0:T(8,128)S(1)}, f32[136,128]{1,0:T(8,128)S(1)}) custom-call(s32[7]{0:T(128)S(1)} %pad_add_fusion.info, bf16[4,2,256,128]{3,2,1,0:T(8,128)(2,1)S(1)} %bitcast.8, bf16[4,2,32,128]{3,2,1,0:T(8,128)(2,1)S(1)} %copy-done.2, bf16[4,2,32,128]{3,2,1,0:T(8,128)(2,1)S(1)} %copy-done.3), custom_call_target="tpu_custom_call" | custom-call | tf_op jit(solution)/shard_map/own/pallas_call | solution.py:428
  55.5 0.9 collective-permute-done.6.refs_1_
  56.5 2.5 %collective-permute-start.8 = (f32[128,128]{1,0:T(8,128)S(1)}, f32[128,128]{1,0:T(8,128)S(1)}, u32[]{:S(2)}, u32[]{:S(2)}) collective-permute-start(f32[128,128]{1,0:T(8,128)S(1)} %finish.2.refs_0_), channel_id=1, source_target_pairs={{0,120},{4,124},{8,0},{12,4},{16,8},{20,12},{24,16},{28,20},{32,24... | collective-permute-start | bytes 196616 | tf_op jit(solution)/shard_map/ppermute | solution.py:385
  59.0 0.0 collective-permute-start.10
  59.0 0.0 collective-permute-done.15.refs_1_
  59.0 1.5 %collective-permute-start.17 = (f32[128,128]{1,0:T(8,128)S(1)}, f32[128,128]{1,0:T(8,128)S(1)}, u32[]{:S(2)}, u32[]{:S(2)}) collective-permute-start(f32[128,128]{1,0:T(8,128)S(1)} %finish.3.refs_0_), channel_id=1, source_target_pairs={{0,120},{4,124},{8,0},{12,4},{16,8},{20,12},{24,16},{28,20},{32,24... | collective-permute-start | bytes 196616 | tf_op jit(solution)/shard_map/ppermute | solution.py:385
  60.5 2.1 %collective-permute-start.19 = (f32[128,128]{1,0:T(8,128)S(1)}, f32[128,128]{1,0:T(8,128)S(1)}, u32[]{:S(2)}, u32[]{:S(2)}) collective-permute-start(f32[128,128]{1,0:T(8,128)S(1)} %finish.3.refs_0_), channel_id=1, source_target_pairs={{0,16},{4,116},{8,24},{12,124},{16,32},{20,4},{24,40},{28,12},{32,... | collective-permute-start | bytes 196616 | tf_op jit(solution)/shard_map/ppermute | solution.py:385
  62.6 0.0 collective-permute-start.12
  62.6 0.0 collective-permute-done.8.refs_2_
  62.6 0.5 collective-permute-start.21
  63.1 1.5 %collective-permute-done.10.refs_4_ = f32[128,128]{1,0:T(8,128)S(1)} collective-permute-done((f32[128,128]{1,0:T(8,128)S(1)}, f32[128,128]{1,0:T(8,128)S(1)}, u32[]{:S(2)}, u32[]{:S(2)}) %collective-permute-start.10) | collective-permute-done | bytes 65568 | tf_op jit(solution)/shard_map/ppermute | solution.py:385
  64.7 8.1 %collective-permute-start.16 = (f32[128,128]{1,0:T(8,128)S(1)}, f32[128,128]{1,0:T(8,128)S(1)}, u32[]{:S(2)}, u32[]{:S(2)}) collective-permute-start(f32[128,128]{1,0:T(8,128)S(1)} %finish.3.refs_0_), channel_id=1, source_target_pairs={{0,4},{4,0},{8,12},{12,8},{16,20},{20,16},{24,28},{28,24},{32,36},... | collective-permute-start | bytes 196616 | tf_op jit(solution)/shard_map/ppermute | solution.py:384
  72.7 0.0 collective-permute-done.17.refs_2_
  72.7 0.1 collective-permute-start.18
  72.9 0.0 collective-permute-done.19.refs_4_
  72.9 2.1 %collective-permute-start.20 = (f32[128,128]{1,0:T(8,128)S(1)}, f32[128,128]{1,0:T(8,128)S(1)}, u32[]{:S(2)}, u32[]{:S(2)}) collective-permute-start(f32[128,128]{1,0:T(8,128)S(1)} %collective-permute-done.19.refs_4_), channel_id=1, source_target_pairs={{0,4},{4,0},{8,12},{12,8},{16,20},{20,16},{24,28},{28,24},{32,36},... | collective-permute-start | bytes 196616 | tf_op jit(solution)/shard_map/ppermute | solution.py:384
  75.0 0.0 collective-permute-done.12.refs_6_
  75.0 0.0 collective-permute-start.7
  75.0 0.0 collective-permute-done.21.refs_6_
  75.0 0.6 collective-permute-start.22
  75.6 0.0 collective-permute-done.16.refs_1_
  75.6 0.0 collective-permute-start.9
  75.7 0.0 collective-permute-done.18.refs_3_
  75.7 0.5 collective-permute-start.11
  76.2 0.0 collective-permute-done.20.refs_5_
  76.2 0.1 collective-permute-start.13
  76.3 0.3 collective-permute-done.22.refs_7_
  76.5 0.9 %project.2.refs_8_ = f32[128,256]{1,0:T(8,128)S(1)} custom-call(s32[7]{0:T(128)S(1)} %pad_add_fusion.info, f32[128,128]{1,0:T(8,128)S(1)} %finish.3.refs_0_, f32[128,128]{1,0:T(8,128)S(1)} %collective-permute-done.16.refs_1_, f32[128,128]{1,0:T(8,128)S(1)} %collective-permute-done.17.refs_2_, f32[128,128]{1,0:T(8,128)S(1)} %collective-permute-done.18.refs_3_, ...), custom_call_target="tpu_custom_call" | custom-call | tf_op jit(solution)/shard_map/project/pallas_call | solution.py:454
  77.5 0.0 collective-permute-done.7.refs_1_
  77.5 0.0 collective-permute-done.9.refs_3_
  77.5 0.0 collective-permute-done.11.refs_5_
  77.5 0.0 collective-permute-done.13.refs_7_
  77.5 0.9 %project.3 = f32[128,256]{1,0:T(8,128)S(1)} custom-call(s32[7]{0:T(128)S(1)} %pad_add_fusion.info, f32[128,128]{1,0:T(8,128)S(1)} %finish.2.refs_0_, f32[128,128]{1,0:T(8,128)S(1)} %collective-permute-done.7.refs_1_, f32[128,128]{1,0:T(8,128)S(1)} %collective-permute-done.8.refs_2_, f32[128,128]{1,0:T(8,128)S(1)} %collective-permute-done.9.refs_3_, ...), custom_call_target="tpu_custom_call" | custom-call | tf_op jit(solution)/shard_map/project/pallas_call | solution.py:454
  78.4 0.1 collective-permute-start.23
  78.5 5.0 %collective-permute-done.23 = f32[128,256]{1,0:T(8,128)S(1)} collective-permute-done((f32[128,256]{1,0:T(8,128)S(1)}, f32[128,256]{1,0:T(8,128)S(1)}, u32[]{:S(2)}, u32[]{:S(2)}) %collective-permute-start.23) | collective-permute-done | bytes 131104 | tf_op jit(solution)/shard_map/ppermute | solution.py:387
  83.6 0.1 collective-permute-start.24
  83.7 3.8 %collective-permute-done.24 = f32[128,256]{1,0:T(8,128)S(1)} collective-permute-done((f32[128,256]{1,0:T(8,128)S(1)}, f32[128,256]{1,0:T(8,128)S(1)}, u32[]{:S(2)}, u32[]{:S(2)}) %collective-permute-start.24) | collective-permute-done | bytes 131104 | tf_op jit(solution)/shard_map/ppermute | solution.py:387
  87.5 0.7 add.17
  (9 shorter events, 0.2 us)
Async XLA Ops:
  8.3 46.2 %copy-start.1 = (bf16[4,16,32,128]{3,2,1,0:T(8,128)(2,1)S(1)}, bf16[4,16,32,128]{3,2,1,0:T(8,128)(2,1)}, u32[]{:S(2)}) copy-start(bf16[4,16,32,128]{3,2,1,0:T(8,128)(2,1)} %param.7) | copy-start | bytes 1572868
  8.3 46.2 %copy-start.2 = (bf16[4,2,32,128]{3,2,1,0:T(8,128)(2,1)S(1)}, bf16[4,2,32,128]{3,2,1,0:T(8,128)(2,1)}, u32[]{:S(2)}) copy-start(bf16[4,2,32,128]{3,2,1,0:T(8,128)(2,1)} %key_ref.1) | copy-start | bytes 196612
  8.3 46.2 %copy-start.3 = (bf16[4,2,32,128]{3,2,1,0:T(8,128)(2,1)S(1)}, bf16[4,2,32,128]{3,2,1,0:T(8,128)(2,1)}, u32[]{:S(2)}) copy-start(bf16[4,2,32,128]{3,2,1,0:T(8,128)(2,1)} %value_ref.1) | copy-start | bytes 196612
  8.3 68.2 %copy-start = (bf16[2048,256]{1,0:T(8,128)(2,1)S(1)}, bf16[2048,256]{1,0:T(8,128)(2,1)}, u32[]{:S(2)}) copy-start(bf16[2048,256]{1,0:T(8,128)(2,1)} %refs_9_.1) | copy-start | bytes 3145732
  8.4 23.1 %collective-permute-start.1 = (f32[3,136,256]{2,1,0:T(8,128)S(1)}, f32[3,136,256]{2,1,0:T(8,128)S(1)}, u32[]{:S(2)}, u32[]{:S(2)}) collective-permute-start(f32[3,136,256]{2,1,0:T(8,128)S(1)} %get-tuple-element.25), channel_id=1, source_target_pairs={{0,4},{4,0},{8,12},{12,8},{16,20},{20,16},{24,28},{28,24},{32,36},... | collective-permute-start | bytes 1253384 | tf_op jit(solution)/shard_map/ppermute | solution.py:384
  31.3 3.0 %collective-permute-start = (f32[1,136,256]{2,1,0:T(8,128)S(1)}, f32[1,136,256]{2,1,0:T(8,128)S(1)}, u32[]{:S(2)}, u32[]{:S(2)}) collective-permute-start(f32[1,136,256]{2,1,0:T(8,128)S(1)} %get-tuple-element.23), channel_id=1, source_target_pairs={{0,4},{4,0},{8,12},{12,8},{16,20},{20,16},{24,28},{28,24},{32,36},... | collective-permute-start | bytes 417800 | tf_op jit(solution)/shard_map/ppermute | solution.py:384
  31.6 6.1 %collective-permute-start.2 = (f32[136,256]{1,0:T(8,128)S(1)}, f32[136,256]{1,0:T(8,128)S(1)}, u32[]{:S(2)}, u32[]{:S(2)}) collective-permute-start(f32[136,256]{1,0:T(8,128)S(1)} %get-tuple-element.26), channel_id=1, source_target_pairs={{0,8},{4,12},{8,16},{12,20},{16,24},{20,28},{24,32},{28,36},{32,40... | collective-permute-start | bytes 417800 | tf_op jit(solution)/shard_map/ppermute | solution.py:385
  31.7 6.0 %collective-permute-start.3 = (f32[136,256]{1,0:T(8,128)S(1)}, f32[136,256]{1,0:T(8,128)S(1)}, u32[]{:S(2)}, u32[]{:S(2)}) collective-permute-start(f32[136,256]{1,0:T(8,128)S(1)} %get-tuple-element.27), channel_id=1, source_target_pairs={{0,16},{4,116},{8,24},{12,124},{16,32},{20,4},{24,40},{28,12},{32,... | collective-permute-start | bytes 417800 | tf_op jit(solution)/shard_map/ppermute | solution.py:385
  31.9 9.3 %collective-permute-start.4 = (f32[136,256]{1,0:T(8,128)S(1)}, f32[136,256]{1,0:T(8,128)S(1)}, u32[]{:S(2)}, u32[]{:S(2)}) collective-permute-start(f32[136,256]{1,0:T(8,128)S(1)} %get-tuple-element.28), channel_id=1, source_target_pairs={{0,120},{4,124},{8,0},{12,4},{16,8},{20,12},{24,16},{28,20},{32,24... | collective-permute-start | bytes 417800 | tf_op jit(solution)/shard_map/ppermute | solution.py:385
  41.2 7.5 %collective-permute-start.5 = (f32[136,128]{1,0:T(8,128)S(1)}, f32[136,128]{1,0:T(8,128)S(1)}, u32[]{:S(2)}, u32[]{:S(2)}) collective-permute-start(f32[136,128]{1,0:T(8,128)S(1)} %get-tuple-element.29.refs_0_), channel_id=1, source_target_pairs={{0,32},{4,100},{8,40},{12,108},{16,48},{20,116},{24,56},{28,124},{... | collective-permute-start | bytes 208904 | tf_op jit(solution)/shard_map/ppermute | solution.py:386
  41.3 8.1 %collective-permute-start.14 = (f32[136,128]{1,0:T(8,128)S(1)}, f32[136,128]{1,0:T(8,128)S(1)}, u32[]{:S(2)}, u32[]{:S(2)}) collective-permute-start(f32[136,128]{1,0:T(8,128)S(1)} %get-tuple-element.31.refs_0_), channel_id=1, source_target_pairs={{0,32},{4,100},{8,40},{12,108},{16,48},{20,116},{24,56},{28,124},{... | collective-permute-start | bytes 208904 | tf_op jit(solution)/shard_map/ppermute | solution.py:386
  48.7 7.7 %collective-permute-start.6 = (f32[136,128]{1,0:T(8,128)S(1)}, f32[136,128]{1,0:T(8,128)S(1)}, u32[]{:S(2)}, u32[]{:S(2)}) collective-permute-start(f32[136,128]{1,0:T(8,128)S(1)} %merge.4.refs_0_), channel_id=1, source_target_pairs={{0,96},{4,36},{8,104},{12,44},{16,112},{20,52},{24,120},{28,60},{3... | collective-permute-start | bytes 208904 | tf_op jit(solution)/shard_map/ppermute | solution.py:386
  49.5 9.5 %collective-permute-start.15 = (f32[136,128]{1,0:T(8,128)S(1)}, f32[136,128]{1,0:T(8,128)S(1)}, u32[]{:S(2)}, u32[]{:S(2)}) collective-permute-start(f32[136,128]{1,0:T(8,128)S(1)} %merge.5.refs_0_), channel_id=1, source_target_pairs={{0,96},{4,36},{8,104},{12,44},{16,112},{20,52},{24,120},{28,60},{3... | collective-permute-start | bytes 208904 | tf_op jit(solution)/shard_map/ppermute | solution.py:386
  56.5 6.2 %collective-permute-start.8 = (f32[128,128]{1,0:T(8,128)S(1)}, f32[128,128]{1,0:T(8,128)S(1)}, u32[]{:S(2)}, u32[]{:S(2)}) collective-permute-start(f32[128,128]{1,0:T(8,128)S(1)} %finish.2.refs_0_), channel_id=1, source_target_pairs={{0,120},{4,124},{8,0},{12,4},{16,8},{20,12},{24,16},{28,20},{32,24... | collective-permute-start | bytes 196616 | tf_op jit(solution)/shard_map/ppermute | solution.py:385
  59.0 5.7 %collective-permute-start.10 = (f32[128,128]{1,0:T(8,128)S(1)}, f32[128,128]{1,0:T(8,128)S(1)}, u32[]{:S(2)}, u32[]{:S(2)}) collective-permute-start(f32[128,128]{1,0:T(8,128)S(1)} %finish.2.refs_0_), channel_id=1, source_target_pairs={{0,16},{4,116},{8,24},{12,124},{16,32},{20,4},{24,40},{28,12},{32,... | collective-permute-start | bytes 196616 | tf_op jit(solution)/shard_map/ppermute | solution.py:385
  59.0 13.7 %collective-permute-start.17 = (f32[128,128]{1,0:T(8,128)S(1)}, f32[128,128]{1,0:T(8,128)S(1)}, u32[]{:S(2)}, u32[]{:S(2)}) collective-permute-start(f32[128,128]{1,0:T(8,128)S(1)} %finish.3.refs_0_), channel_id=1, source_target_pairs={{0,120},{4,124},{8,0},{12,4},{16,8},{20,12},{24,16},{28,20},{32,24... | collective-permute-start | bytes 196616 | tf_op jit(solution)/shard_map/ppermute | solution.py:385
  60.5 12.4 %collective-permute-start.19 = (f32[128,128]{1,0:T(8,128)S(1)}, f32[128,128]{1,0:T(8,128)S(1)}, u32[]{:S(2)}, u32[]{:S(2)}) collective-permute-start(f32[128,128]{1,0:T(8,128)S(1)} %finish.3.refs_0_), channel_id=1, source_target_pairs={{0,16},{4,116},{8,24},{12,124},{16,32},{20,4},{24,40},{28,12},{32,... | collective-permute-start | bytes 196616 | tf_op jit(solution)/shard_map/ppermute | solution.py:385
  62.6 12.4 %collective-permute-start.12 = (f32[128,128]{1,0:T(8,128)S(1)}, f32[128,128]{1,0:T(8,128)S(1)}, u32[]{:S(2)}, u32[]{:S(2)}) collective-permute-start(f32[128,128]{1,0:T(8,128)S(1)} %finish.2.refs_0_), channel_id=1, source_target_pairs={{0,8},{4,12},{8,16},{12,20},{16,24},{20,28},{24,32},{28,36},{32,40... | collective-permute-start | bytes 196616 | tf_op jit(solution)/shard_map/ppermute | solution.py:385
  62.6 12.4 %collective-permute-start.21 = (f32[128,128]{1,0:T(8,128)S(1)}, f32[128,128]{1,0:T(8,128)S(1)}, u32[]{:S(2)}, u32[]{:S(2)}) collective-permute-start(f32[128,128]{1,0:T(8,128)S(1)} %finish.3.refs_0_), channel_id=1, source_target_pairs={{0,8},{4,12},{8,16},{12,20},{16,24},{20,28},{24,32},{28,36},{32,40... | collective-permute-start | bytes 196616 | tf_op jit(solution)/shard_map/ppermute | solution.py:385
  64.7 11.0 %collective-permute-start.16 = (f32[128,128]{1,0:T(8,128)S(1)}, f32[128,128]{1,0:T(8,128)S(1)}, u32[]{:S(2)}, u32[]{:S(2)}) collective-permute-start(f32[128,128]{1,0:T(8,128)S(1)} %finish.3.refs_0_), channel_id=1, source_target_pairs={{0,4},{4,0},{8,12},{12,8},{16,20},{20,16},{24,28},{28,24},{32,36},... | collective-permute-start | bytes 196616 | tf_op jit(solution)/shard_map/ppermute | solution.py:384
  72.7 3.0 %collective-permute-start.18 = (f32[128,128]{1,0:T(8,128)S(1)}, f32[128,128]{1,0:T(8,128)S(1)}, u32[]{:S(2)}, u32[]{:S(2)}) collective-permute-start(f32[128,128]{1,0:T(8,128)S(1)} %collective-permute-done.17.refs_2_), channel_id=1, source_target_pairs={{0,4},{4,0},{8,12},{12,8},{16,20},{20,16},{24,28},{28,24},{32,36},... | collective-permute-start | bytes 196616 | tf_op jit(solution)/shard_map/ppermute | solution.py:384
  72.9 3.3 %collective-permute-start.20 = (f32[128,128]{1,0:T(8,128)S(1)}, f32[128,128]{1,0:T(8,128)S(1)}, u32[]{:S(2)}, u32[]{:S(2)}) collective-permute-start(f32[128,128]{1,0:T(8,128)S(1)} %collective-permute-done.19.refs_4_), channel_id=1, source_target_pairs={{0,4},{4,0},{8,12},{12,8},{16,20},{20,16},{24,28},{28,24},{32,36},... | collective-permute-start | bytes 196616 | tf_op jit(solution)/shard_map/ppermute | solution.py:384
  75.0 2.5 %collective-permute-start.7 = (f32[128,128]{1,0:T(8,128)S(1)}, f32[128,128]{1,0:T(8,128)S(1)}, u32[]{:S(2)}, u32[]{:S(2)}) collective-permute-start(f32[128,128]{1,0:T(8,128)S(1)} %finish.2.refs_0_), channel_id=1, source_target_pairs={{0,4},{4,0},{8,12},{12,8},{16,20},{20,16},{24,28},{28,24},{32,36},... | collective-permute-start | bytes 196616 | tf_op jit(solution)/shard_map/ppermute | solution.py:384
  75.0 1.5 %collective-permute-start.22 = (f32[128,128]{1,0:T(8,128)S(1)}, f32[128,128]{1,0:T(8,128)S(1)}, u32[]{:S(2)}, u32[]{:S(2)}) collective-permute-start(f32[128,128]{1,0:T(8,128)S(1)} %collective-permute-done.21.refs_6_), channel_id=1, source_target_pairs={{0,4},{4,0},{8,12},{12,8},{16,20},{20,16},{24,28},{28,24},{32,36},... | collective-permute-start | bytes 196616 | tf_op jit(solution)/shard_map/ppermute | solution.py:384
  75.6 1.8 %collective-permute-start.9 = (f32[128,128]{1,0:T(8,128)S(1)}, f32[128,128]{1,0:T(8,128)S(1)}, u32[]{:S(2)}, u32[]{:S(2)}) collective-permute-start(f32[128,128]{1,0:T(8,128)S(1)} %collective-permute-done.8.refs_2_), channel_id=1, source_target_pairs={{0,4},{4,0},{8,12},{12,8},{16,20},{20,16},{24,28},{28,24},{32,36},... | collective-permute-start | bytes 196616 | tf_op jit(solution)/shard_map/ppermute | solution.py:384
  75.7 1.8 %collective-permute-start.11 = (f32[128,128]{1,0:T(8,128)S(1)}, f32[128,128]{1,0:T(8,128)S(1)}, u32[]{:S(2)}, u32[]{:S(2)}) collective-permute-start(f32[128,128]{1,0:T(8,128)S(1)} %collective-permute-done.10.refs_4_), channel_id=1, source_target_pairs={{0,4},{4,0},{8,12},{12,8},{16,20},{20,16},{24,28},{28,24},{32,36},... | collective-permute-start | bytes 196616 | tf_op jit(solution)/shard_map/ppermute | solution.py:384
  76.2 1.3 %collective-permute-start.13 = (f32[128,128]{1,0:T(8,128)S(1)}, f32[128,128]{1,0:T(8,128)S(1)}, u32[]{:S(2)}, u32[]{:S(2)}) collective-permute-start(f32[128,128]{1,0:T(8,128)S(1)} %collective-permute-done.12.refs_6_), channel_id=1, source_target_pairs={{0,4},{4,0},{8,12},{12,8},{16,20},{20,16},{24,28},{28,24},{32,36},... | collective-permute-start | bytes 196616 | tf_op jit(solution)/shard_map/ppermute | solution.py:384
  78.4 5.2 %collective-permute-start.23 = (f32[128,256]{1,0:T(8,128)S(1)}, f32[128,256]{1,0:T(8,128)S(1)}, u32[]{:S(2)}, u32[]{:S(2)}) collective-permute-start(f32[128,256]{1,0:T(8,128)S(1)} %project.3), channel_id=1, source_target_pairs={{0,1},{1,0},{2,3},{3,2},{4,7},{5,6},{6,5},{7,4},{8,9},{9,8},{10,11... | collective-permute-start | bytes 393224 | tf_op jit(solution)/shard_map/ppermute | solution.py:387
  83.6 3.9 %collective-permute-start.24 = (f32[128,256]{1,0:T(8,128)S(1)}, f32[128,256]{1,0:T(8,128)S(1)}, u32[]{:S(2)}, u32[]{:S(2)}) collective-permute-start(f32[128,256]{1,0:T(8,128)S(1)} %add.16), channel_id=1, source_target_pairs={{0,3},{1,2},{2,1},{3,0},{4,5},{5,4},{6,7},{7,6},{8,11},{9,10},{10,... | collective-permute-start | bytes 393224 | tf_op jit(solution)/shard_map/ppermute | solution.py:387
